TPU v7x, 32 devices: a 4x4x1 block of a 4x4x8 slice. The times are simulated.
32 devices in a mesh: data: 1 (over z), model: 4 (over y), stage: 8 (over x, core).
Axes of the slice: x: 4, y: 4, z: 1, core: 2. Of those that a mesh axis runs over, the one named last changes fastest.
The devices are a block of a 4x4x8 slice.
Arguments:
- tokens_in: bfloat16 [4, 1024, 512], P(None, 'data')
- targets: bfloat16 [4, 1024, 512], P(None, 'data')
- w_qkv: bfloat16 [8, 1, 512, 8, 3, 64], P('stage', None, None, 'model')
- w_out: bfloat16 [8, 1, 8, 64, 512], P('stage', None, 'model')
- w_up: bfloat16 [8, 1, 512, 2048], P('stage', None, None, 'model')
- w_down: bfloat16 [8, 1, 2048, 512], P('stage', None, 'model')
Outputs:
- output 1: float32 [8, 1, 512, 8, 3, 64], P(('data', 'stage'), None, None, 'model')
- output 2: float32 [8, 1, 8, 64, 512], P(('data', 'stage'), None, 'model')
- output 3: float32 [8, 1, 512, 2048], P(('data', 'stage'), None, None, 'model')
- output 4: float32 [8, 1, 2048, 512], P(('data', 'stage'), None, 'model')
- output 5: float32 [1], P('data')
All inputs are finite; a program needn't handle non-finite values.
Results may differ from a plain program's by a relative error of at most 0.0164868.
Values are sent between devices in bfloat16 or wider.
A program may use at most 768 MiB of HBM per device.

v0:
```python
import jax
import jax.numpy as jnp
from jax import lax
from jax.sharding import PartitionSpec as P


def rms_norm(hidden):
    hid32 = hidden.astype(jnp.float32)
    inv_rms = lax.rsqrt(jnp.mean(hid32 * hid32, axis=-1, keepdims=True) + 1e-6)
    return (hid32 * inv_rms).astype(jnp.bfloat16)


def gelu_fn(pre_act):
    return jax.nn.gelu(pre_act.astype(jnp.float32), approximate=True)


def attn_core(queries, keys_in, values):
    seq_len = queries.shape[0]
    sm_scale = queries.shape[-1] ** -0.5
    scores = jnp.einsum("qhe,khe->hqk", queries, keys_in, preferred_element_type=jnp.float32) * sm_scale
    causal = lax.broadcasted_iota(jnp.int32, (seq_len, seq_len), 0) >= lax.broadcasted_iota(jnp.int32, (seq_len, seq_len), 1)
    scores = jnp.where(causal[None], scores, -1e30)
    prob_bf = jax.nn.softmax(scores, axis=-1).astype(jnp.bfloat16)
    return jnp.einsum("hqk,khe->qhe", prob_bf, values, preferred_element_type=jnp.float32).astype(jnp.bfloat16)


def layer_fwd(hidden, w_qkv, w_out, w_up, w_down):
    normed = rms_norm(hidden)
    qkv_loc = jnp.einsum("bd,dhse->bhse", normed, w_qkv, preferred_element_type=jnp.float32).astype(jnp.bfloat16)
    attn_out = attn_core(qkv_loc[:, :, 0], qkv_loc[:, :, 1], qkv_loc[:, :, 2])
    part_a = jnp.einsum("bhe,hed->bd", attn_out, w_out, preferred_element_type=jnp.float32).astype(jnp.bfloat16)
    branch_a = lax.psum(part_a, "model")
    h_mid = (hidden.astype(jnp.float32) + branch_a.astype(jnp.float32)).astype(jnp.bfloat16)
    pre_act = jnp.dot(rms_norm(h_mid), w_up, preferred_element_type=jnp.float32).astype(jnp.bfloat16)
    act_bf = gelu_fn(pre_act).astype(jnp.bfloat16)
    part_m = jnp.dot(act_bf, w_down, preferred_element_type=jnp.float32).astype(jnp.bfloat16)
    branch_m = lax.psum(part_m, "model")
    h_out = (h_mid.astype(jnp.float32) + branch_m.astype(jnp.float32)).astype(jnp.bfloat16)
    return h_out, (hidden, qkv_loc, h_mid, pre_act)


def layer_bwd(grad_out, saved, w_qkv, w_out, w_up, w_down):
    hidden, qkv_loc, h_mid, pre_act = saved
    normed2, norm2_pull = jax.vjp(rms_norm, h_mid)
    act_f32, gelu_pull = jax.vjp(gelu_fn, pre_act)
    act_bf = act_f32.astype(jnp.bfloat16)
    grad_act = jnp.einsum("bd,fd->bf", grad_out, w_down, preferred_element_type=jnp.float32)
    grad_pre = gelu_pull(grad_act)[0]
    part_n2 = jnp.einsum("bf,df->bd", grad_pre, w_up, preferred_element_type=jnp.float32).astype(jnp.bfloat16)
    grad_n2 = lax.psum(part_n2, "model")
    grad_mid = (grad_out.astype(jnp.float32) + norm2_pull(grad_n2)[0].astype(jnp.float32)).astype(jnp.bfloat16)
    g_down = jnp.einsum("bf,bd->fd", act_bf, grad_out, preferred_element_type=jnp.float32)
    g_up = jnp.einsum("bd,bf->df", normed2, grad_pre, preferred_element_type=jnp.float32)
    normed1, norm1_pull = jax.vjp(rms_norm, hidden)
    attn_out, attn_pull = jax.vjp(attn_core, qkv_loc[:, :, 0], qkv_loc[:, :, 1], qkv_loc[:, :, 2])
    grad_attn = jnp.einsum("bd,hed->bhe", grad_mid, w_out, preferred_element_type=jnp.float32).astype(jnp.bfloat16)
    grad_q, grad_k, grad_v = attn_pull(grad_attn)
    grad_qkv = jnp.stack([grad_q, grad_k, grad_v], axis=2)
    part_n1 = jnp.einsum("bhse,dhse->bd", grad_qkv, w_qkv, preferred_element_type=jnp.float32).astype(jnp.bfloat16)
    grad_n1 = lax.psum(part_n1, "model")
    grad_in = (grad_mid.astype(jnp.float32) + norm1_pull(grad_n1)[0].astype(jnp.float32)).astype(jnp.bfloat16)
    g_out = jnp.einsum("bhe,bd->hed", attn_out, grad_mid, preferred_element_type=jnp.float32)
    g_qkv = jnp.einsum("bd,bhse->dhse", normed1, grad_qkv, preferred_element_type=jnp.float32)
    return grad_in, (g_qkv, g_out, g_up, g_down)


def read_slot(buf_arr, micro_idx, lay_idx):
    start_at = (micro_idx, lay_idx) + (0,) * (buf_arr.ndim - 2)
    return lax.dynamic_slice(buf_arr, start_at, (1, 1) + buf_arr.shape[2:])[0, 0]


def write_slot(buf_arr, new_val, micro_idx, lay_idx, keep_new):
    start_at = (micro_idx, lay_idx) + (0,) * (buf_arr.ndim - 2)
    old_val = lax.dynamic_slice(buf_arr, start_at, (1, 1) + buf_arr.shape[2:])[0, 0]
    merged = jnp.where(keep_new, new_val, old_val)
    return lax.dynamic_update_slice(buf_arr, merged[None, None], start_at)


def solution(mesh):
    n_stage = mesh.shape["stage"]
    fwd_perm = [(idx, idx + 1) for idx in range(n_stage - 1)]
    bwd_perm = [(idx + 1, idx) for idx in range(n_stage - 1)]

    def per_device(tokens_in, targets, w_qkv, w_out, w_up, w_down):
        n_micro, seq_len, d_model = tokens_in.shape
        n_layer = w_qkv.shape[1]
        heads_loc = w_qkv.shape[3]
        head_dim = w_qkv.shape[5]
        ff_loc = w_up.shape[3]
        stage_idx = lax.axis_index("stage")
        is_first = stage_idx == 0
        is_last = stage_idx == n_stage - 1
        n_tick = n_micro + n_stage - 1
        inv_count = 1.0 / (n_micro * seq_len * d_model)
        layer_ws = [(w_qkv[0, lay_idx], w_out[0, lay_idx], w_up[0, lay_idx], w_down[0, lay_idx]) for lay_idx in range(n_layer)]
        zero_saves = (
            jnp.zeros((n_micro, n_layer, seq_len, d_model), jnp.bfloat16),
            jnp.zeros((n_micro, n_layer, seq_len, heads_loc, 3, head_dim), jnp.bfloat16),
            jnp.zeros((n_micro, n_layer, seq_len, d_model), jnp.bfloat16),
            jnp.zeros((n_micro, n_layer, seq_len, ff_loc), jnp.bfloat16),
        )
        zero_grad_y = jnp.zeros((n_micro, 1, seq_len, d_model), jnp.bfloat16)

        def fwd_tick(tick_idx, loop_carry):
            recv_act, saves, grad_y, loss_acc = loop_carry
            micro_idx = tick_idx - stage_idx
            is_valid = (micro_idx >= 0) & (micro_idx < n_micro)
            safe_idx = jnp.clip(micro_idx, 0, n_micro - 1)
            x_mb = lax.dynamic_index_in_dim(tokens_in, safe_idx, 0, keepdims=False)
            hidden = jnp.where(is_first, x_mb, recv_act)
            saves = list(saves)
            for lay_idx in range(n_layer):
                hidden, saved = layer_fwd(hidden, *layer_ws[lay_idx])
                saves = [write_slot(buf_arr, new_val, safe_idx, lay_idx, is_valid) for buf_arr, new_val in zip(saves, saved)]
            t_mb = lax.dynamic_index_in_dim(targets, safe_idx, 0, keepdims=False)
            err_vec = hidden.astype(jnp.float32) - t_mb.astype(jnp.float32)
            use_loss = is_valid & is_last
            loss_acc = loss_acc + jnp.where(use_loss, 0.5 * jnp.sum(err_vec * err_vec) * inv_count, 0.0)
            grad_y = write_slot(grad_y, (err_vec * inv_count).astype(jnp.bfloat16), safe_idx, 0, use_loss)
            recv_act = lax.ppermute(hidden, "stage", fwd_perm)
            return recv_act, tuple(saves), grad_y, loss_acc

        fwd_init = (jnp.zeros((seq_len, d_model), jnp.bfloat16), zero_saves, zero_grad_y, jnp.zeros((), jnp.float32))
        _, saves, grad_y, loss_acc = lax.fori_loop(0, n_tick, fwd_tick, fwd_init)

        def bwd_tick(tick_idx, loop_carry):
            recv_grad, grad_acc = loop_carry
            micro_idx = tick_idx - (n_stage - 1 - stage_idx)
            is_valid = (micro_idx >= 0) & (micro_idx < n_micro)
            safe_idx = jnp.clip(micro_idx, 0, n_micro - 1)
            grad_h = jnp.where(is_last, read_slot(grad_y, safe_idx, 0), recv_grad)
            grad_h = jnp.where(is_valid, grad_h, jnp.zeros_like(grad_h))
            new_acc = list(grad_acc)
            for lay_idx in reversed(range(n_layer)):
                saved = tuple(read_slot(buf_arr, safe_idx, lay_idx) for buf_arr in saves)
                grad_h, layer_g = layer_bwd(grad_h, saved, *layer_ws[lay_idx])
                new_acc[lay_idx] = tuple(acc_g + new_g for acc_g, new_g in zip(grad_acc[lay_idx], layer_g))
            recv_grad = lax.ppermute(grad_h, "stage", bwd_perm)
            return recv_grad, tuple(new_acc)

        zero_acc = tuple(tuple(jnp.zeros(weight.shape, jnp.float32) for weight in lay_w) for lay_w in layer_ws)
        _, grad_acc = lax.fori_loop(0, n_tick, bwd_tick, (jnp.zeros((seq_len, d_model), jnp.bfloat16), zero_acc))
        grad_list = tuple(jnp.stack([grad_acc[lay_idx][pos] for lay_idx in range(n_layer)])[None] for pos in range(4))
        loss_all = lax.psum(loss_acc, "stage").reshape(1)
        return grad_list + (loss_all,)

    tok_spec = P(None, "data", None)
    qkv_spec = P("stage", None, None, "model", None, None)
    out_spec = P("stage", None, "model", None, None)
    up_spec = P("stage", None, None, "model")
    down_spec = P("stage", None, "model", None)
    g_qkv_spec = P(("data", "stage"), None, None, "model", None, None)
    g_out_spec = P(("data", "stage"), None, "model", None, None)
    g_up_spec = P(("data", "stage"), None, None, "model")
    g_down_spec = P(("data", "stage"), None, "model", None)
    return jax.shard_map(per_device, mesh=mesh, in_specs=(tok_spec, tok_spec, qkv_spec, out_spec, up_spec, down_spec), out_specs=(g_qkv_spec, g_out_spec, g_up_spec, g_down_spec, P("data")), check_vma=False)
```

profile of v0, /device:TPU:96, one launch (start us, length us, event | category | flops | bytes accessed | tf_op | source)
XLA Modules:
  0.0 2957.8 jit_solution(12651584088194795924)
XLA Ops:
  18.5 1412.2 %while.51 = (s32[]{:T(128)}, bf16[1024,512]{1,0:T(8,128)(2,1)S(1)}, bf16[4,1,1024,512]{3,2,1,0:T(8,128)(2,1)}, bf16[4,1,1024,2,3,64]{2,5,4,3,1,0:T(8,128)(2,1)},...) while((s32[]{:T(128)}, bf16[1024,512]{1,0:T(8,128)(2,1)S(1)}, ...), condition=%wide.region_8.9_spmd, body=%wide.region_0.8_spmd.sunk | while | flops 2188250112 | bytes 95994976 | solution.py:124
  40.9 41.0 %all-reduce.5.cloned.1.call-done = bf16[1024,512]{1,0:T(8,128)(2,1)} async-done(((bf16[1024,512]{1,0:T(8,128)(2,1)}), bf16[1024,512]{1,0:T(8,128)(2,1)}) %all-reduce.5.cloned.1.call-update) | async-done | bytes 1048592 | tf_op jit(solution)/shard_map/while/body/eval_jaxpr/psum | solution.py:32
  88.7 42.0 %all-reduce.7.cloned.1.call-done = bf16[1024,512]{1,0:T(8,128)(2,1)} async-done(((bf16[1024,512]{1,0:T(8,128)(2,1)}), bf16[1024,512]{1,0:T(8,128)(2,1)}) %all-reduce.7.cloned.1.call-update) | async-done | bytes 1048592 | tf_op jit(solution)/shard_map/while/body/eval_jaxpr/psum | solution.py:37
  161.5 49.5 %all-reduce.5.cloned.1.call-done = bf16[1024,512]{1,0:T(8,128)(2,1)} async-done(((bf16[1024,512]{1,0:T(8,128)(2,1)}), bf16[1024,512]{1,0:T(8,128)(2,1)}) %all-reduce.5.cloned.1.call-update) | async-done | bytes 1048592 | tf_op jit(solution)/shard_map/while/body/eval_jaxpr/psum | solution.py:32
  217.9 42.0 %all-reduce.7.cloned.1.call-done = bf16[1024,512]{1,0:T(8,128)(2,1)} async-done(((bf16[1024,512]{1,0:T(8,128)(2,1)}), bf16[1024,512]{1,0:T(8,128)(2,1)}) %all-reduce.7.cloned.1.call-update) | async-done | bytes 1048592 | tf_op jit(solution)/shard_map/while/body/eval_jaxpr/psum | solution.py:37
  290.8 49.5 %all-reduce.5.cloned.1.call-done = bf16[1024,512]{1,0:T(8,128)(2,1)} async-done(((bf16[1024,512]{1,0:T(8,128)(2,1)}), bf16[1024,512]{1,0:T(8,128)(2,1)}) %all-reduce.5.cloned.1.call-update) | async-done | bytes 1048592 | tf_op jit(solution)/shard_map/while/body/eval_jaxpr/psum | solution.py:32
  347.1 42.1 %all-reduce.7.cloned.1.call-done = bf16[1024,512]{1,0:T(8,128)(2,1)} async-done(((bf16[1024,512]{1,0:T(8,128)(2,1)}), bf16[1024,512]{1,0:T(8,128)(2,1)}) %all-reduce.7.cloned.1.call-update) | async-done | bytes 1048592 | tf_op jit(solution)/shard_map/while/body/eval_jaxpr/psum | solution.py:37
  420.1 49.5 %all-reduce.5.cloned.1.call-done = bf16[1024,512]{1,0:T(8,128)(2,1)} async-done(((bf16[1024,512]{1,0:T(8,128)(2,1)}), bf16[1024,512]{1,0:T(8,128)(2,1)}) %all-reduce.5.cloned.1.call-update) | async-done | bytes 1048592 | tf_op jit(solution)/shard_map/while/body/eval_jaxpr/psum | solution.py:32
  476.4 42.1 %all-reduce.7.cloned.1.call-done = bf16[1024,512]{1,0:T(8,128)(2,1)} async-done(((bf16[1024,512]{1,0:T(8,128)(2,1)}), bf16[1024,512]{1,0:T(8,128)(2,1)}) %all-reduce.7.cloned.1.call-update) | async-done | bytes 1048592 | tf_op jit(solution)/shard_map/while/body/eval_jaxpr/psum | solution.py:37
  549.3 49.5 %all-reduce.5.cloned.1.call-done = bf16[1024,512]{1,0:T(8,128)(2,1)} async-done(((bf16[1024,512]{1,0:T(8,128)(2,1)}), bf16[1024,512]{1,0:T(8,128)(2,1)}) %all-reduce.5.cloned.1.call-update) | async-done | bytes 1048592 | tf_op jit(solution)/shard_map/while/body/eval_jaxpr/psum | solution.py:32
  605.7 42.1 %all-reduce.7.cloned.1.call-done = bf16[1024,512]{1,0:T(8,128)(2,1)} async-done(((bf16[1024,512]{1,0:T(8,128)(2,1)}), bf16[1024,512]{1,0:T(8,128)(2,1)}) %all-reduce.7.cloned.1.call-update) | async-done | bytes 1048592 | tf_op jit(solution)/shard_map/while/body/eval_jaxpr/psum | solution.py:37
  678.5 49.4 %all-reduce.5.cloned.1.call-done = bf16[1024,512]{1,0:T(8,128)(2,1)} async-done(((bf16[1024,512]{1,0:T(8,128)(2,1)}), bf16[1024,512]{1,0:T(8,128)(2,1)}) %all-reduce.5.cloned.1.call-update) | async-done | bytes 1048592 | tf_op jit(solution)/shard_map/while/body/eval_jaxpr/psum | solution.py:32
  734.8 42.0 %all-reduce.7.cloned.1.call-done = bf16[1024,512]{1,0:T(8,128)(2,1)} async-done(((bf16[1024,512]{1,0:T(8,128)(2,1)}), bf16[1024,512]{1,0:T(8,128)(2,1)}) %all-reduce.7.cloned.1.call-update) | async-done | bytes 1048592 | tf_op jit(solution)/shard_map/while/body/eval_jaxpr/psum | solution.py:37
  807.6 49.4 %all-reduce.5.cloned.1.call-done = bf16[1024,512]{1,0:T(8,128)(2,1)} async-done(((bf16[1024,512]{1,0:T(8,128)(2,1)}), bf16[1024,512]{1,0:T(8,128)(2,1)}) %all-reduce.5.cloned.1.call-update) | async-done | bytes 1048592 | tf_op jit(solution)/shard_map/while/body/eval_jaxpr/psum | solution.py:32
  863.9 42.0 %all-reduce.7.cloned.1.call-done = bf16[1024,512]{1,0:T(8,128)(2,1)} async-done(((bf16[1024,512]{1,0:T(8,128)(2,1)}), bf16[1024,512]{1,0:T(8,128)(2,1)}) %all-reduce.7.cloned.1.call-update) | async-done | bytes 1048592 | tf_op jit(solution)/shard_map/while/body/eval_jaxpr/psum | solution.py:37
  936.7 49.4 %all-reduce.5.cloned.1.call-done = bf16[1024,512]{1,0:T(8,128)(2,1)} async-done(((bf16[1024,512]{1,0:T(8,128)(2,1)}), bf16[1024,512]{1,0:T(8,128)(2,1)}) %all-reduce.5.cloned.1.call-update) | async-done | bytes 1048592 | tf_op jit(solution)/shard_map/while/body/eval_jaxpr/psum | solution.py:32
  992.9 42.0 %all-reduce.7.cloned.1.call-done = bf16[1024,512]{1,0:T(8,128)(2,1)} async-done(((bf16[1024,512]{1,0:T(8,128)(2,1)}), bf16[1024,512]{1,0:T(8,128)(2,1)}) %all-reduce.7.cloned.1.call-update) | async-done | bytes 1048592 | tf_op jit(solution)/shard_map/while/body/eval_jaxpr/psum | solution.py:37
  1065.7 49.4 %all-reduce.5.cloned.1.call-done = bf16[1024,512]{1,0:T(8,128)(2,1)} async-done(((bf16[1024,512]{1,0:T(8,128)(2,1)}), bf16[1024,512]{1,0:T(8,128)(2,1)}) %all-reduce.5.cloned.1.call-update) | async-done | bytes 1048592 | tf_op jit(solution)/shard_map/while/body/eval_jaxpr/psum | solution.py:32
  1122.0 42.0 %all-reduce.7.cloned.1.call-done = bf16[1024,512]{1,0:T(8,128)(2,1)} async-done(((bf16[1024,512]{1,0:T(8,128)(2,1)}), bf16[1024,512]{1,0:T(8,128)(2,1)}) %all-reduce.7.cloned.1.call-update) | async-done | bytes 1048592 | tf_op jit(solution)/shard_map/while/body/eval_jaxpr/psum | solution.py:37
  1194.8 49.4 %all-reduce.5.cloned.1.call-done = bf16[1024,512]{1,0:T(8,128)(2,1)} async-done(((bf16[1024,512]{1,0:T(8,128)(2,1)}), bf16[1024,512]{1,0:T(8,128)(2,1)}) %all-reduce.5.cloned.1.call-update) | async-done | bytes 1048592 | tf_op jit(solution)/shard_map/while/body/eval_jaxpr/psum | solution.py:32
  1251.0 42.0 %all-reduce.7.cloned.1.call-done = bf16[1024,512]{1,0:T(8,128)(2,1)} async-done(((bf16[1024,512]{1,0:T(8,128)(2,1)}), bf16[1024,512]{1,0:T(8,128)(2,1)}) %all-reduce.7.cloned.1.call-update) | async-done | bytes 1048592 | tf_op jit(solution)/shard_map/while/body/eval_jaxpr/psum | solution.py:37
  1323.8 49.4 %all-reduce.5.cloned.1.call-done = bf16[1024,512]{1,0:T(8,128)(2,1)} async-done(((bf16[1024,512]{1,0:T(8,128)(2,1)}), bf16[1024,512]{1,0:T(8,128)(2,1)}) %all-reduce.5.cloned.1.call-update) | async-done | bytes 1048592 | tf_op jit(solution)/shard_map/while/body/eval_jaxpr/psum | solution.py:32
  1380.1 42.0 %all-reduce.7.cloned.1.call-done = bf16[1024,512]{1,0:T(8,128)(2,1)} async-done(((bf16[1024,512]{1,0:T(8,128)(2,1)}), bf16[1024,512]{1,0:T(8,128)(2,1)}) %all-reduce.7.cloned.1.call-update) | async-done | bytes 1048592 | tf_op jit(solution)/shard_map/while/body/eval_jaxpr/psum | solution.py:37
  1431.8 1501.3 %while.52 = (s32[]{:T(128)}, bf16[1024,512]{1,0:T(8,128)(2,1)}, f32[512,2,3,64]{0,3,2,1:T(8,128)}, f32[2,64,512]{2,1,0:T(8,128)S(1)}, f32[512,512]{1,0:T(8,128)}...) while((s32[]{:T(128)}, bf16[1024,512]{1,0:T(8,128)(2,1)}, ...), condition=%wide.region_19.20_spmd.clone, body=%wide.region_9.19_spmd.clone.sunk | while | flops 4924519424 | bytes 184230704 | solution.py:142
  1446.9 44.8 %all-reduce.9.cloned.1.call-done = bf16[1024,512]{1,0:T(8,128)(2,1)} async-done(((bf16[1024,512]{1,0:T(8,128)(2,1)}), bf16[1024,512]{1,0:T(8,128)(2,1)}) %all-reduce.9.cloned.1.call-update) | async-done | bytes 1048592 | tf_op jit(solution)/shard_map/while/body/eval_jaxpr/psum | solution.py:50
  1519.4 38.7 %all-reduce.11.cloned.1.call-done = bf16[1024,512]{1,0:T(8,128)(2,1)} async-done(((bf16[1024,512]{1,0:T(8,128)(2,1)}), bf16[1024,512]{1,0:T(8,128)(2,1)}) %all-reduce.11.cloned.1.call-update) | async-done | bytes 1048592 | tf_op jit(solution)/shard_map/while/body/eval_jaxpr/psum | solution.py:60
  1589.0 38.5 %all-reduce.9.cloned.1.call-done = bf16[1024,512]{1,0:T(8,128)(2,1)} async-done(((bf16[1024,512]{1,0:T(8,128)(2,1)}), bf16[1024,512]{1,0:T(8,128)(2,1)}) %all-reduce.9.cloned.1.call-update) | async-done | bytes 1048592 | tf_op jit(solution)/shard_map/while/body/eval_jaxpr/psum | solution.py:50
  1636.9 6.6 fusion.221
  1655.7 38.3 %all-reduce.11.cloned.1.call-done = bf16[1024,512]{1,0:T(8,128)(2,1)} async-done(((bf16[1024,512]{1,0:T(8,128)(2,1)}), bf16[1024,512]{1,0:T(8,128)(2,1)}) %all-reduce.11.cloned.1.call-update) | async-done | bytes 1048592 | tf_op jit(solution)/shard_map/while/body/eval_jaxpr/psum | solution.py:60
  1724.9 38.5 %all-reduce.9.cloned.1.call-done = bf16[1024,512]{1,0:T(8,128)(2,1)} async-done(((bf16[1024,512]{1,0:T(8,128)(2,1)}), bf16[1024,512]{1,0:T(8,128)(2,1)}) %all-reduce.9.cloned.1.call-update) | async-done | bytes 1048592 | tf_op jit(solution)/shard_map/while/body/eval_jaxpr/psum | solution.py:50
  1791.6 38.3 %all-reduce.11.cloned.1.call-done = bf16[1024,512]{1,0:T(8,128)(2,1)} async-done(((bf16[1024,512]{1,0:T(8,128)(2,1)}), bf16[1024,512]{1,0:T(8,128)(2,1)}) %all-reduce.11.cloned.1.call-update) | async-done | bytes 1048592 | tf_op jit(solution)/shard_map/while/body/eval_jaxpr/psum | solution.py:60
  1860.9 38.5 %all-reduce.9.cloned.1.call-done = bf16[1024,512]{1,0:T(8,128)(2,1)} async-done(((bf16[1024,512]{1,0:T(8,128)(2,1)}), bf16[1024,512]{1,0:T(8,128)(2,1)}) %all-reduce.9.cloned.1.call-update) | async-done | bytes 1048592 | tf_op jit(solution)/shard_map/while/body/eval_jaxpr/psum | solution.py:50
  1927.5 38.3 %all-reduce.11.cloned.1.call-done = bf16[1024,512]{1,0:T(8,128)(2,1)} async-done(((bf16[1024,512]{1,0:T(8,128)(2,1)}), bf16[1024,512]{1,0:T(8,128)(2,1)}) %all-reduce.11.cloned.1.call-update) | async-done | bytes 1048592 | tf_op jit(solution)/shard_map/while/body/eval_jaxpr/psum | solution.py:60
  1996.8 38.5 %all-reduce.9.cloned.1.call-done = bf16[1024,512]{1,0:T(8,128)(2,1)} async-done(((bf16[1024,512]{1,0:T(8,128)(2,1)}), bf16[1024,512]{1,0:T(8,128)(2,1)}) %all-reduce.9.cloned.1.call-update) | async-done | bytes 1048592 | tf_op jit(solution)/shard_map/while/body/eval_jaxpr/psum | solution.py:50
  2063.4 38.3 %all-reduce.11.cloned.1.call-done = bf16[1024,512]{1,0:T(8,128)(2,1)} async-done(((bf16[1024,512]{1,0:T(8,128)(2,1)}), bf16[1024,512]{1,0:T(8,128)(2,1)}) %all-reduce.11.cloned.1.call-update) | async-done | bytes 1048592 | tf_op jit(solution)/shard_map/while/body/eval_jaxpr/psum | solution.py:60
  2132.7 38.5 %all-reduce.9.cloned.1.call-done = bf16[1024,512]{1,0:T(8,128)(2,1)} async-done(((bf16[1024,512]{1,0:T(8,128)(2,1)}), bf16[1024,512]{1,0:T(8,128)(2,1)}) %all-reduce.9.cloned.1.call-update) | async-done | bytes 1048592 | tf_op jit(solution)/shard_map/while/body/eval_jaxpr/psum | solution.py:50
  2199.3 38.3 %all-reduce.11.cloned.1.call-done = bf16[1024,512]{1,0:T(8,128)(2,1)} async-done(((bf16[1024,512]{1,0:T(8,128)(2,1)}), bf16[1024,512]{1,0:T(8,128)(2,1)}) %all-reduce.11.cloned.1.call-update) | async-done | bytes 1048592 | tf_op jit(solution)/shard_map/while/body/eval_jaxpr/psum | solution.py:60
  2268.6 38.5 %all-reduce.9.cloned.1.call-done = bf16[1024,512]{1,0:T(8,128)(2,1)} async-done(((bf16[1024,512]{1,0:T(8,128)(2,1)}), bf16[1024,512]{1,0:T(8,128)(2,1)}) %all-reduce.9.cloned.1.call-update) | async-done | bytes 1048592 | tf_op jit(solution)/shard_map/while/body/eval_jaxpr/psum | solution.py:50
  2335.2 38.3 %all-reduce.11.cloned.1.call-done = bf16[1024,512]{1,0:T(8,128)(2,1)} async-done(((bf16[1024,512]{1,0:T(8,128)(2,1)}), bf16[1024,512]{1,0:T(8,128)(2,1)}) %all-reduce.11.cloned.1.call-update) | async-done | bytes 1048592 | tf_op jit(solution)/shard_map/while/body/eval_jaxpr/psum | solution.py:60
  2404.5 38.5 %all-reduce.9.cloned.1.call-done = bf16[1024,512]{1,0:T(8,128)(2,1)} async-done(((bf16[1024,512]{1,0:T(8,128)(2,1)}), bf16[1024,512]{1,0:T(8,128)(2,1)}) %all-reduce.9.cloned.1.call-update) | async-done | bytes 1048592 | tf_op jit(solution)/shard_map/while/body/eval_jaxpr/psum | solution.py:50
  2471.1 38.4 %all-reduce.11.cloned.1.call-done = bf16[1024,512]{1,0:T(8,128)(2,1)} async-done(((bf16[1024,512]{1,0:T(8,128)(2,1)}), bf16[1024,512]{1,0:T(8,128)(2,1)}) %all-reduce.11.cloned.1.call-update) | async-done | bytes 1048592 | tf_op jit(solution)/shard_map/while/body/eval_jaxpr/psum | solution.py:60
  2540.4 38.5 %all-reduce.9.cloned.1.call-done = bf16[1024,512]{1,0:T(8,128)(2,1)} async-done(((bf16[1024,512]{1,0:T(8,128)(2,1)}), bf16[1024,512]{1,0:T(8,128)(2,1)}) %all-reduce.9.cloned.1.call-update) | async-done | bytes 1048592 | tf_op jit(solution)/shard_map/while/body/eval_jaxpr/psum | solution.py:50
  2607.1 38.3 %all-reduce.11.cloned.1.call-done = bf16[1024,512]{1,0:T(8,128)(2,1)} async-done(((bf16[1024,512]{1,0:T(8,128)(2,1)}), bf16[1024,512]{1,0:T(8,128)(2,1)}) %all-reduce.11.cloned.1.call-update) | async-done | bytes 1048592 | tf_op jit(solution)/shard_map/while/body/eval_jaxpr/psum | solution.py:60
  2676.4 38.5 %all-reduce.9.cloned.1.call-done = bf16[1024,512]{1,0:T(8,128)(2,1)} async-done(((bf16[1024,512]{1,0:T(8,128)(2,1)}), bf16[1024,512]{1,0:T(8,128)(2,1)}) %all-reduce.9.cloned.1.call-update) | async-done | bytes 1048592 | tf_op jit(solution)/shard_map/while/body/eval_jaxpr/psum | solution.py:50
  2743.0 38.4 %all-reduce.11.cloned.1.call-done = bf16[1024,512]{1,0:T(8,128)(2,1)} async-done(((bf16[1024,512]{1,0:T(8,128)(2,1)}), bf16[1024,512]{1,0:T(8,128)(2,1)}) %all-reduce.11.cloned.1.call-update) | async-done | bytes 1048592 | tf_op jit(solution)/shard_map/while/body/eval_jaxpr/psum | solution.py:60
  2812.3 38.5 %all-reduce.9.cloned.1.call-done = bf16[1024,512]{1,0:T(8,128)(2,1)} async-done(((bf16[1024,512]{1,0:T(8,128)(2,1)}), bf16[1024,512]{1,0:T(8,128)(2,1)}) %all-reduce.9.cloned.1.call-update) | async-done | bytes 1048592 | tf_op jit(solution)/shard_map/while/body/eval_jaxpr/psum | solution.py:50
  2878.9 38.3 %all-reduce.11.cloned.1.call-done = bf16[1024,512]{1,0:T(8,128)(2,1)} async-done(((bf16[1024,512]{1,0:T(8,128)(2,1)}), bf16[1024,512]{1,0:T(8,128)(2,1)}) %all-reduce.11.cloned.1.call-update) | async-done | bytes 1048592 | tf_op jit(solution)/shard_map/while/body/eval_jaxpr/psum | solution.py:60
  2933.1 18.2 psum.63
  (1070 shorter events, 1057.5 us)
Async XLA Ops:
  18.5 63.3 %all-reduce.5.cloned.1.call-start = ((), (), s32[]{:S(2)}) async-start(), calls=%async_computation | async-start | bytes 2097152 | tf_op jit(solution)/shard_map/while/body/eval_jaxpr/psum | solution.py:32
  38.1 92.6 %all-reduce.7.cloned.1.call-start = ((), (), s32[]{:S(2)}) async-start(), calls=%async_computation.1 | async-start | bytes 2097152 | tf_op jit(solution)/shard_map/while/body/eval_jaxpr/psum | solution.py:37
  139.4 71.7 %all-reduce.5.cloned.1.call-start = ((), (), s32[]{:S(2)}) async-start(), calls=%async_computation | async-start | bytes 2097152 | tf_op jit(solution)/shard_map/while/body/eval_jaxpr/psum | solution.py:32
  158.8 101.1 %all-reduce.7.cloned.1.call-start = ((), (), s32[]{:S(2)}) async-start(), calls=%async_computation.1 | async-start | bytes 2097152 | tf_op jit(solution)/shard_map/while/body/eval_jaxpr/psum | solution.py:37
  268.6 71.7 %all-reduce.5.cloned.1.call-start = ((), (), s32[]{:S(2)}) async-start(), calls=%async_computation | async-start | bytes 2097152 | tf_op jit(solution)/shard_map/while/body/eval_jaxpr/psum | solution.py:32
  288.1 101.1 %all-reduce.7.cloned.1.call-start = ((), (), s32[]{:S(2)}) async-start(), calls=%async_computation.1 | async-start | bytes 2097152 | tf_op jit(solution)/shard_map/while/body/eval_jaxpr/psum | solution.py:37
  397.9 71.7 %all-reduce.5.cloned.1.call-start = ((), (), s32[]{:S(2)}) async-start(), calls=%async_computation | async-start | bytes 2097152 | tf_op jit(solution)/shard_map/while/body/eval_jaxpr/psum | solution.py:32
  417.3 101.1 %all-reduce.7.cloned.1.call-start = ((), (), s32[]{:S(2)}) async-start(), calls=%async_computation.1 | async-start | bytes 2097152 | tf_op jit(solution)/shard_map/while/body/eval_jaxpr/psum | solution.py:37
  527.1 71.7 %all-reduce.5.cloned.1.call-start = ((), (), s32[]{:S(2)}) async-start(), calls=%async_computation | async-start | bytes 2097152 | tf_op jit(solution)/shard_map/while/body/eval_jaxpr/psum | solution.py:32
  546.6 101.1 %all-reduce.7.cloned.1.call-start = ((), (), s32[]{:S(2)}) async-start(), calls=%async_computation.1 | async-start | bytes 2097152 | tf_op jit(solution)/shard_map/while/body/eval_jaxpr/psum | solution.py:37
  656.4 71.6 %all-reduce.5.cloned.1.call-start = ((), (), s32[]{:S(2)}) async-start(), calls=%async_computation | async-start | bytes 2097152 | tf_op jit(solution)/shard_map/while/body/eval_jaxpr/psum | solution.py:32
  675.8 100.9 %all-reduce.7.cloned.1.call-start = ((), (), s32[]{:S(2)}) async-start(), calls=%async_computation.1 | async-start | bytes 2097152 | tf_op jit(solution)/shard_map/while/body/eval_jaxpr/psum | solution.py:37
  785.4 71.6 %all-reduce.5.cloned.1.call-start = ((), (), s32[]{:S(2)}) async-start(), calls=%async_computation | async-start | bytes 2097152 | tf_op jit(solution)/shard_map/while/body/eval_jaxpr/psum | solution.py:32
  804.9 100.9 %all-reduce.7.cloned.1.call-start = ((), (), s32[]{:S(2)}) async-start(), calls=%async_computation.1 | async-start | bytes 2097152 | tf_op jit(solution)/shard_map/while/body/eval_jaxpr/psum | solution.py:37
  914.5 71.6 %all-reduce.5.cloned.1.call-start = ((), (), s32[]{:S(2)}) async-start(), calls=%async_computation | async-start | bytes 2097152 | tf_op jit(solution)/shard_map/while/body/eval_jaxpr/psum | solution.py:32
  933.9 100.9 %all-reduce.7.cloned.1.call-start = ((), (), s32[]{:S(2)}) async-start(), calls=%async_computation.1 | async-start | bytes 2097152 | tf_op jit(solution)/shard_map/while/body/eval_jaxpr/psum | solution.py:37
  1043.6 71.6 %all-reduce.5.cloned.1.call-start = ((), (), s32[]{:S(2)}) async-start(), calls=%async_computation | async-start | bytes 2097152 | tf_op jit(solution)/shard_map/while/body/eval_jaxpr/psum | solution.py:32
  1063.0 100.9 %all-reduce.7.cloned.1.call-start = ((), (), s32[]{:S(2)}) async-start(), calls=%async_computation.1 | async-start | bytes 2097152 | tf_op jit(solution)/shard_map/while/body/eval_jaxpr/psum | solution.py:37
  1172.6 71.6 %all-reduce.5.cloned.1.call-start = ((), (), s32[]{:S(2)}) async-start(), calls=%async_computation | async-start | bytes 2097152 | tf_op jit(solution)/shard_map/while/body/eval_jaxpr/psum | solution.py:32
  1192.1 100.9 %all-reduce.7.cloned.1.call-start = ((), (), s32[]{:S(2)}) async-start(), calls=%async_computation.1 | async-start | bytes 2097152 | tf_op jit(solution)/shard_map/while/body/eval_jaxpr/psum | solution.py:37
  1301.7 71.6 %all-reduce.5.cloned.1.call-start = ((), (), s32[]{:S(2)}) async-start(), calls=%async_computation | async-start | bytes 2097152 | tf_op jit(solution)/shard_map/while/body/eval_jaxpr/psum | solution.py:32
  1321.1 100.9 %all-reduce.7.cloned.1.call-start = ((), (), s32[]{:S(2)}) async-start(), calls=%async_computation.1 | async-start | bytes 2097152 | tf_op jit(solution)/shard_map/while/body/eval_jaxpr/psum | solution.py:37
  1431.8 59.9 %all-reduce.9.cloned.1.call-start = ((), (), s32[]{:S(2)}) async-start(), calls=%async_computation.2 | async-start | bytes 2097152 | tf_op jit(solution)/shard_map/while/body/eval_jaxpr/psum | solution.py:50
  1439.5 118.6 %all-reduce.11.cloned.1.call-start = ((), (), s32[]{:S(2)}) async-start(), calls=%async_computation.3 | async-start | bytes 2097152 | tf_op jit(solution)/shard_map/while/body/eval_jaxpr/psum | solution.py:60
  1562.5 10.6 collective-permute-start.1
  1574.0 53.6 %all-reduce.9.cloned.1.call-start = ((), (), s32[]{:S(2)}) async-start(), calls=%async_computation.2 | async-start | bytes 2097152 | tf_op jit(solution)/shard_map/while/body/eval_jaxpr/psum | solution.py:50
  1581.7 112.3 %all-reduce.11.cloned.1.call-start = ((), (), s32[]{:S(2)}) async-start(), calls=%async_computation.3 | async-start | bytes 2097152 | tf_op jit(solution)/shard_map/while/body/eval_jaxpr/psum | solution.py:60
  1709.9 53.6 %all-reduce.9.cloned.1.call-start = ((), (), s32[]{:S(2)}) async-start(), calls=%async_computation.2 | async-start | bytes 2097152 | tf_op jit(solution)/shard_map/while/body/eval_jaxpr/psum | solution.py:50
  1717.6 112.4 %all-reduce.11.cloned.1.call-start = ((), (), s32[]{:S(2)}) async-start(), calls=%async_computation.3 | async-start | bytes 2097152 | tf_op jit(solution)/shard_map/while/body/eval_jaxpr/psum | solution.py:60
  1834.3 10.6 collective-permute-start.1
  1845.8 53.6 %all-reduce.9.cloned.1.call-start = ((), (), s32[]{:S(2)}) async-start(), calls=%async_computation.2 | async-start | bytes 2097152 | tf_op jit(solution)/shard_map/while/body/eval_jaxpr/psum | solution.py:50
  1853.5 112.3 %all-reduce.11.cloned.1.call-start = ((), (), s32[]{:S(2)}) async-start(), calls=%async_computation.3 | async-start | bytes 2097152 | tf_op jit(solution)/shard_map/while/body/eval_jaxpr/psum | solution.py:60
  1981.7 53.6 %all-reduce.9.cloned.1.call-start = ((), (), s32[]{:S(2)}) async-start(), calls=%async_computation.2 | async-start | bytes 2097152 | tf_op jit(solution)/shard_map/while/body/eval_jaxpr/psum | solution.py:50
  1989.4 112.4 %all-reduce.11.cloned.1.call-start = ((), (), s32[]{:S(2)}) async-start(), calls=%async_computation.3 | async-start | bytes 2097152 | tf_op jit(solution)/shard_map/while/body/eval_jaxpr/psum | solution.py:60
  2106.2 10.6 collective-permute-start.1
  2117.6 53.6 %all-reduce.9.cloned.1.call-start = ((), (), s32[]{:S(2)}) async-start(), calls=%async_computation.2 | async-start | bytes 2097152 | tf_op jit(solution)/shard_map/while/body/eval_jaxpr/psum | solution.py:50
  2125.3 112.3 %all-reduce.11.cloned.1.call-start = ((), (), s32[]{:S(2)}) async-start(), calls=%async_computation.3 | async-start | bytes 2097152 | tf_op jit(solution)/shard_map/while/body/eval_jaxpr/psum | solution.py:60
  2253.5 53.6 %all-reduce.9.cloned.1.call-start = ((), (), s32[]{:S(2)}) async-start(), calls=%async_computation.2 | async-start | bytes 2097152 | tf_op jit(solution)/shard_map/while/body/eval_jaxpr/psum | solution.py:50
  2261.2 112.4 %all-reduce.11.cloned.1.call-start = ((), (), s32[]{:S(2)}) async-start(), calls=%async_computation.3 | async-start | bytes 2097152 | tf_op jit(solution)/shard_map/while/body/eval_jaxpr/psum | solution.py:60
  2378.0 10.6 collective-permute-start.1
  2389.4 53.6 %all-reduce.9.cloned.1.call-start = ((), (), s32[]{:S(2)}) async-start(), calls=%async_computation.2 | async-start | bytes 2097152 | tf_op jit(solution)/shard_map/while/body/eval_jaxpr/psum | solution.py:50
  2397.1 112.4 %all-reduce.11.cloned.1.call-start = ((), (), s32[]{:S(2)}) async-start(), calls=%async_computation.3 | async-start | bytes 2097152 | tf_op jit(solution)/shard_map/while/body/eval_jaxpr/psum | solution.py:60
  2525.3 53.6 %all-reduce.9.cloned.1.call-start = ((), (), s32[]{:S(2)}) async-start(), calls=%async_computation.2 | async-start | bytes 2097152 | tf_op jit(solution)/shard_map/while/body/eval_jaxpr/psum | solution.py:50
  2533.0 112.4 %all-reduce.11.cloned.1.call-start = ((), (), s32[]{:S(2)}) async-start(), calls=%async_computation.3 | async-start | bytes 2097152 | tf_op jit(solution)/shard_map/while/body/eval_jaxpr/psum | solution.py:60
  2661.3 53.6 %all-reduce.9.cloned.1.call-start = ((), (), s32[]{:S(2)}) async-start(), calls=%async_computation.2 | async-start | bytes 2097152 | tf_op jit(solution)/shard_map/while/body/eval_jaxpr/psum | solution.py:50
  2669.0 112.4 %all-reduce.11.cloned.1.call-start = ((), (), s32[]{:S(2)}) async-start(), calls=%async_computation.3 | async-start | bytes 2097152 | tf_op jit(solution)/shard_map/while/body/eval_jaxpr/psum | solution.py:60
  2797.2 53.6 %all-reduce.9.cloned.1.call-start = ((), (), s32[]{:S(2)}) async-start(), calls=%async_computation.2 | async-start | bytes 2097152 | tf_op jit(solution)/shard_map/while/body/eval_jaxpr/psum | solution.py:50
  2804.9 112.4 %all-reduce.11.cloned.1.call-start = ((), (), s32[]{:S(2)}) async-start(), calls=%async_computation.3 | async-start | bytes 2097152 | tf_op jit(solution)/shard_map/while/body/eval_jaxpr/psum | solution.py:60
  (229 other events, 1603.6 us)
Sparse Core Ops, SparseCore 0:
  38.3 43.5 all-reduce.4
  88.8 41.8 all-reduce.6
  158.9 52.1 all-reduce.4
  218.0 41.8 all-reduce.6
  288.2 52.0 all-reduce.4
  347.2 41.9 all-reduce.6
  417.5 52.0 all-reduce.4
  476.5 41.8 all-reduce.6
  546.7 52.0 all-reduce.4
  605.8 41.8 all-reduce.6
  675.9 51.9 all-reduce.4
  734.9 41.8 all-reduce.6
  805.0 51.9 all-reduce.4
  864.0 41.8 all-reduce.6
  934.1 51.9 all-reduce.4
  993.0 41.8 all-reduce.6
  1063.1 51.9 all-reduce.4
  1122.1 41.8 all-reduce.6
  1192.2 51.9 all-reduce.4
  1251.1 41.8 all-reduce.6
  1321.2 51.9 all-reduce.4
  1380.2 41.8 all-reduce.6
  1439.6 51.9 all-reduce.8
  1516.2 41.8 all-reduce.10
  1581.8 45.7 all-reduce.8
  1652.1 41.8 all-reduce.10
  1717.7 45.7 all-reduce.8
  1788.1 41.8 all-reduce.10
  1853.6 45.7 all-reduce.8
  1924.0 41.8 all-reduce.10
  1989.5 45.7 all-reduce.8
  2059.9 41.8 all-reduce.10
  2125.4 45.7 all-reduce.8
  2195.8 41.8 all-reduce.10
  2261.3 45.7 all-reduce.8
  2331.7 41.8 all-reduce.10
  2397.3 45.7 all-reduce.8
  2467.6 41.8 all-reduce.10
  2533.2 45.7 all-reduce.8
  2603.5 41.8 all-reduce.10
  2669.1 45.7 all-reduce.8
  2739.4 41.8 all-reduce.10
  2805.0 45.7 all-reduce.8
  2875.4 41.8 all-reduce.10
where the time goes:
time: 2970 us; the launch traced here: 2960 us
  waiting for transfers between devices  1850 us (62%)
  matrix products  619 us (21%)
  other arithmetic  281 us (9%)
  local copies, waits for them, and re-layouts  131 us (4%)
  starting transfers between devices  30.9 us (1%)
    psum x11, waiting for transfers between devices, layer_fwd(): branch_a = lax.psum(part_a, 'model')  535 us
    psum x11, waiting for transfers between devices, layer_fwd(): branch_m = lax.psum(part_m, 'model')  462 us
    psum x11, waiting for transfers between devices, layer_bwd(): grad_n2 = lax.psum(part_n2, 'model')  430 us
    psum x11, waiting for transfers between devices, layer_bwd(): grad_n1 = lax.psum(part_n1, 'model')  422 us
    dot_general x22, matrix products, attn_core(): jnp.einsum('qhe,khe->hqk', queries, keys_in, preferred_element_type=jnp.f...  129 us
    sub x22, matrix products, attn_core(): prob_bf = jax.nn.softmax(scores, axis=-1).astype(jnp.bfloat16)  114 us
    dynamic_update_slice x44, other arithmetic, write_slot(): return lax.dynamic_update_slice(buf_arr, merged[None, None], start_at)  104 us
    dynamic_slice x44, local copies, waits for them, and re-layouts, write_slot(): lax.dynamic_slice(buf_arr, start_at, (1, 1) + buf_arr.shape[2:])[0, 0]  70.8 us
  transfers between devices with their start and end apart: 66, of which 44 were waited for; matrix products, arithmetic and copies ran while one was open for 10% of the time, Pallas kernels for 0%

commit v1 on v0

v1 whole, which is shorter than its diff:
```python
import functools
import math

import jax
import jax.numpy as jnp
from jax import lax
from jax.experimental import pallas as pl
from jax.experimental.pallas import tpu as pltpu
from jax.sharding import PartitionSpec as P

F32 = jnp.float32
BF16 = jnp.bfloat16
MESH = pl.DeviceIdType.MESH
CHUNK = 256
NEG = -1e30
GELU_C = math.sqrt(2.0 / math.pi)
GELU_A = 0.044715

W_QT, W_OT, W_UT, W_DT, W_D, W_U, W_O, W_Q = range(8)


def dot(lhs, rhs):
    return jnp.dot(lhs, rhs, preferred_element_type=F32)


def dot_t(lhs, rhs):
    return lax.dot_general(lhs, rhs, (((1,), (1,)), ((), ())), preferred_element_type=F32)


def inv_rms(x32):
    return lax.rsqrt(jnp.mean(x32 * x32, axis=0, keepdims=True) + 1e-6)


def norm_pull(x32, inv, g32):
    mean_gx = jnp.mean(g32 * x32, axis=0, keepdims=True)
    return g32 * inv - x32 * (inv * inv * inv * mean_gx)


def gelu(u):
    inner = jnp.tanh(GELU_C * (u + GELU_A * (u * u * u)))
    return u * (0.5 * (1.0 + inner))


def gelu_grad(u):
    u2 = u * u
    inner = jnp.tanh(GELU_C * (u + GELU_A * (u2 * u)))
    cdf = 0.5 * (1.0 + inner)
    return cdf + u * (0.5 * GELU_C) * (1.0 - inner * inner) * (1.0 + (3.0 * GELU_A) * u2)


def step_kernel(cfg, x_hbm, t_hbm, wqT_in, woT_in, wuT_in, wdT_in, wd_in, wu_in, wo_in, wq_in,
                gq_out, go_out, gu_out, gd_out, loss_out, rq, ro, ru, rd,
                wqT, woT, wuT, wdT, wd, wu, wo, wq,
                xin, hbuf, n1buf, qkv, qkvn, obuf, mbuf, n2buf, ubuf, zbuf, pbuf, dybuf, dvacc, dkacc, sscr,
                ybuf, dobuf, losst, lossv, stage_buf, go_buf, radd,
                ag_send, ag_recv, ag_loc, xsem, fsend, frecv, bsend, brecv, lsend, lrecv, lfsend, lfrecv,
                rs_send, rs_recv, ld_sem, out_sem):
    ns, nm, nc, tc, dm_, hl, hd, fl = cfg
    heads = nm * hl
    qrows = hl * 3 * hd
    orows = hl * hd
    inv_d = 1.0 / (nm * nc * tc * dm_)
    scale = hd ** -0.5
    exp_c = scale * math.log2(math.e)
    me = lax.axis_index("model")
    st = lax.axis_index("stage")
    nxt = lax.rem(st + 1, ns)
    prv = lax.rem(st + ns - 1, ns)
    first = st == 0
    last = st == ns - 1

    def peer(k):
        return lax.rem(me + k, nm)

    bar = pltpu.get_barrier_semaphore()
    pl.semaphore_signal(bar, inc=1, device_id={"stage": nxt}, device_id_type=MESH)
    pl.semaphore_signal(bar, inc=1, device_id={"stage": prv}, device_id_type=MESH)
    for k in range(1, nm):
        pl.semaphore_signal(bar, inc=1, device_id={"model": peer(k)}, device_id_type=MESH)
    pl.semaphore_wait(bar, 2 + nm - 1)

    def rowsl(start, size, mult):
        return pl.ds(pl.multiple_of(start, mult), size)

    w_src = (wqT_in, woT_in, wuT_in, wdT_in, wd_in, wu_in, wo_in, wq_in)

    def w_dst(idx, who):
        if idx == W_QT:
            return wqT.at[rowsl(who * qrows, qrows, qrows), :]
        if idx == W_OT:
            return woT.at[:, rowsl(who * orows, orows, orows)]
        if idx == W_UT:
            return wuT.at[rowsl(who * fl, fl, fl), :]
        if idx == W_DT:
            return wdT.at[who]
        if idx == W_D:
            return wd.at[rowsl(who * fl, fl, fl), :]
        if idx == W_U:
            return wu.at[who]
        if idx == W_O:
            return wo.at[rowsl(who * orows, orows, orows), :]
        return wq.at[:, rowsl(who * qrows, qrows, qrows)]

    def w_send(idx, k):
        return pltpu.make_async_remote_copy(
            src_ref=w_src[idx], dst_ref=w_dst(idx, me), send_sem=ag_send.at[idx, k - 1],
            recv_sem=ag_recv.at[idx, k - 1], device_id={"model": peer(k)}, device_id_type=MESH)

    def w_recv(idx, k):
        return pltpu.make_async_remote_copy(
            src_ref=w_src[idx], dst_ref=w_dst(idx, peer(nm - k)), send_sem=ag_send.at[idx, k - 1],
            recv_sem=ag_recv.at[idx, k - 1], device_id={"model": peer(k)}, device_id_type=MESH)

    def w_local(idx):
        return pltpu.make_async_copy(w_src[idx], w_dst(idx, me), ag_loc.at[idx])

    def x_copy(c):
        return pltpu.make_async_copy(x_hbm.at[me, pl.ds(c * tc, tc), :], xin.at[c], xsem.at[c])

    def t_copy(c):
        return pltpu.make_async_copy(t_hbm.at[me, pl.ds(c * tc, tc), :], xin.at[c], xsem.at[c])

    @pl.when(first)
    def _():
        for c in range(nc):
            x_copy(c).start()

    @pl.when(last)
    def _():
        for c in range(nc):
            t_copy(c).start()

    for idx in range(8):
        w_local(idx).start()
        for k in range(1, nm):
            w_send(idx, k).start()

    def w_wait(idx):
        w_local(idx).wait()
        for k in range(1, nm):
            w_recv(idx, k).wait_recv()

    def f_copy(c):
        return pltpu.make_async_remote_copy(
            src_ref=ybuf.at[c], dst_ref=hbuf.at[c], send_sem=fsend.at[c], recv_sem=frecv.at[c],
            device_id={"stage": nxt}, device_id_type=MESH)

    def b_copy(c):
        return pltpu.make_async_remote_copy(
            src_ref=ybuf.at[c], dst_ref=dybuf.at[c], send_sem=bsend.at[c], recv_sem=brecv.at[c],
            device_id={"stage": prv}, device_id_type=MESH)

    lossv[...] = jnp.zeros_like(lossv)

    def head_rows(p, h, part):
        return pl.ds(pl.multiple_of(p * (2 * 3 * hd) + (h * 3 + part) * hd, hd), hd)

    k_lane = (0, 2 * 2 * hd)
    v_lane = (2 * hd, 2 * 2 * hd)
    two = 2 * hd

    def pad_k(val, h):
        zero = jnp.zeros_like(val)
        return jnp.concatenate([zero, val] if h == 0 else [val, zero], axis=0)

    def pad_v(val, h):
        zero = jnp.zeros_like(val)
        return jnp.concatenate([val, zero] if h == 0 else [zero, val], axis=0)

    def causal(shape):
        return lax.broadcasted_iota(jnp.int32, shape, 0) <= lax.broadcasted_iota(jnp.int32, shape, 1)

    @pl.loop(0, nc)
    def _(c):
        @pl.when(first)
        def _():
            x_copy(c).wait()
            hbuf[c] = jnp.transpose(xin[c])

        @pl.when(jnp.logical_not(first))
        def _():
            f_copy(c).wait_recv()

        @pl.when(c == 0)
        def _():
            w_wait(W_QT)

        h32 = hbuf[c].astype(F32)
        n1 = (h32 * inv_rms(h32)).astype(BF16)
        n1buf[c] = n1
        for r in range(nm):
            rows = pl.ds(r * qrows, qrows)
            blk = dot(wqT[rows, :], n1).astype(BF16)
            qkv[c, rows, :] = blk
            qkvn[r, pl.ds(pl.multiple_of(c * tc, tc), tc), :] = jnp.transpose(blk)

        for cc in range(nc):
            @pl.when(c == cc)
            def _():
                @pl.loop(0, heads // 2)
                def _(p):
                    for h in range(2):
                        q_t = qkv[cc, head_rows(p, h, 0), :]
                        qz = pad_k(q_t, h)
                        mx = None
                        for j in range(cc + 1):
                            s = dot(qkvn[p, pl.ds(j * tc, tc), pl.ds(k_lane[h], two)], qz)
                            if j == cc:
                                s = jnp.where(causal(s.shape), s, NEG)
                            sscr[pl.ds(j * tc, tc), :] = s
                            bm = jnp.max(s, axis=0, keepdims=True)
                            mx = bm if mx is None else jnp.maximum(mx, bm)
                        den = None
                        for j in range(cc + 1):
                            e = jnp.exp2((sscr[pl.ds(j * tc, tc), :] - mx) * exp_c)
                            sscr[pl.ds(j * tc, tc), :] = e
                            es = jnp.sum(e, axis=0, keepdims=True)
                            den = es if den is None else den + es
                        inv = 1.0 / den
                        o_t = None
                        for j in range(cc + 1):
                            pr = (sscr[pl.ds(j * tc, tc), :] * inv).astype(BF16)
                            pbuf[cc * (cc + 1) // 2 + j, p * 2 + h] = pr
                            part = dot(qkv[j, head_rows(p, h, 2), :], pr)
                            o_t = part if o_t is None else o_t + part
                        obuf[cc, pl.ds(pl.multiple_of((p * 2 + h) * hd, hd), hd), :] = o_t.astype(BF16)

        @pl.when(c == 0)
        def _():
            w_wait(W_OT)

        a = dot(woT[...], obuf[c]).astype(BF16)
        m32 = (hbuf[c].astype(F32) + a.astype(F32)).astype(BF16).astype(F32)
        mbuf[c] = m32.astype(BF16)
        n2 = (m32 * inv_rms(m32)).astype(BF16)
        n2buf[c] = n2

        @pl.when(c == 0)
        def _():
            w_wait(W_UT)
            w_wait(W_DT)

        acc = None
        for f in range(nm):
            rows = pl.ds(f * fl, fl)
            u = dot(wuT[rows, :], n2buf[c]).astype(BF16)
            ubuf[c, rows, :] = u
            z = gelu(u.astype(F32)).astype(BF16)
            zbuf[c, rows, :] = z
            part = dot(wdT[f], z)
            acc = part if acc is None else acc + part
        y32 = (mbuf[c].astype(F32) + acc.astype(BF16).astype(F32)).astype(BF16)
        ybuf[c] = y32

        @pl.when(jnp.logical_not(last))
        def _():
            f_copy(c).start()

        @pl.when(last)
        def _():
            t_copy(c).wait()
            err = ybuf[c].astype(F32) - jnp.transpose(xin[c]).astype(F32)
            lossv[...] += jnp.sum((err * err).reshape(dm_ // 8, 8, tc), axis=0)
            dybuf[c] = (err * inv_d).astype(BF16)

    def l_copy(k):
        return pltpu.make_async_remote_copy(
            src_ref=losst.at[nm], dst_ref=losst.at[3 - k if nm == 4 else nm - 1 - k], send_sem=lsend.at[k - 1],
            recv_sem=lrecv.at[k - 1], device_id={"model": peer(k)}, device_id_type=MESH)

    def lf_copy():
        return pltpu.make_async_remote_copy(
            src_ref=losst.at[nm + 1], dst_ref=losst.at[nm + 1], send_sem=lfsend, recv_sem=lfrecv,
            device_id={"stage": prv}, device_id_type=MESH)

    @pl.when(last)
    def _():
        tot = jnp.sum(lossv[...]) * (0.5 * inv_d)
        losst[nm] = jnp.full(losst.shape[1:], tot, F32)
        for k in range(1, nm):
            l_copy(k).start()

    @pl.loop(0, nc)
    def _(i):
        c = nc - 1 - i

        @pl.when(jnp.logical_not(last))
        def _():
            b_copy(c).wait_recv()

        @pl.when(i == 0)
        def _():
            w_wait(W_D)
            w_wait(W_U)
            w_wait(W_O)
            w_wait(W_Q)

        acc = None
        for f in range(nm):
            rows = pl.ds(f * fl, fl)
            dz = dot(wd[rows, :], dybuf[c]).astype(BF16).astype(F32)
            du = (dz * gelu_grad(ubuf[c, rows, :].astype(F32))).astype(BF16)
            ubuf[c, rows, :] = du
            part = dot(wu[f], du)
            acc = part if acc is None else acc + part
        dn2 = acc.astype(BF16).astype(F32)
        m32 = mbuf[c].astype(F32)
        pull = norm_pull(m32, inv_rms(m32), dn2).astype(BF16)
        dmid = (dybuf[c].astype(F32) + pull.astype(F32)).astype(BF16)
        mbuf[c] = dmid
        dobuf[...] = dot(wo[...], dmid).astype(BF16)

        for cc in range(nc):
            @pl.when(c == cc)
            def _():
                @pl.loop(0, heads // 2)
                def _(p):
                    dq = [None, None]
                    qz = []
                    dz_v = []
                    dsum = []
                    for h in range(2):
                        orow = pl.ds(pl.multiple_of((p * 2 + h) * hd, hd), hd)
                        do_t = dobuf[orow, :]
                        dsum.append(jnp.sum(do_t.astype(F32) * obuf[cc, orow, :].astype(F32), axis=0, keepdims=True))
                        dz_v.append(pad_v(do_t, h))
                        qz.append(pad_v(qkv[cc, head_rows(p, h, 0), :], h))
                    for j in range(cc + 1):
                        dv_new = None
                        dk_new = None
                        for h in range(2):
                            pr = pbuf[cc * (cc + 1) // 2 + j, p * 2 + h]
                            dp = dot(qkvn[p, pl.ds(j * tc, tc), pl.ds(v_lane[h], two)], dz_v[h]).astype(BF16).astype(F32)
                            ds = (pr.astype(F32) * (dp - dsum[h])).astype(BF16)
                            dv_h = dot_t(pr, dz_v[h])
                            dk_h = dot_t(ds, qz[h])
                            dv_new = dv_h if dv_new is None else dv_new + dv_h
                            dk_new = dk_h if dk_new is None else dk_new + dk_h
                            dq_h = dot(qkv[j, head_rows(p, h, 1), :], ds)
                            dq[h] = dq_h if dq[h] is None else dq[h] + dq_h
                        rows = pl.ds(j * tc, tc)
                        if cc < nc - 1:
                            dv_new = dv_new + dvacc[p, rows, :]
                            dk_new = dk_new + dkacc[p, rows, :]
                        if j < cc:
                            dvacc[p, rows, :] = dv_new
                            dkacc[p, rows, :] = dk_new
                        else:
                            dv_t = jnp.transpose(dv_new).astype(BF16)
                            dk_t = (jnp.transpose(dk_new) * scale).astype(BF16)
                            for h in range(2):
                                qkv[cc, head_rows(p, h, 0), :] = (dq[h] * scale).astype(BF16)
                                qkv[cc, head_rows(p, h, 1), :] = dk_t[h * hd:(h + 1) * hd, :]
                                qkv[cc, head_rows(p, h, 2), :] = dv_t[h * hd:(h + 1) * hd, :]

        dn1 = dot(wq[...], qkv[c]).astype(BF16).astype(F32)
        h32 = hbuf[c].astype(F32)
        pull1 = norm_pull(h32, inv_rms(h32), dn1).astype(BF16)

        @pl.when(jnp.logical_not(last))
        def _():
            f_copy(c).wait_send()

        ybuf[c] = (mbuf[c].astype(F32) + pull1.astype(F32)).astype(BF16)

        @pl.when(jnp.logical_not(first))
        def _():
            b_copy(c).start()

    @pl.when(last)
    def _():
        for k in range(1, nm):
            l_copy(k).wait_recv()
        vals = [losst[nm]] + [losst[k - 1] for k in range(1, nm)]
        tot = jnp.zeros_like(vals[0])
        for who in range(nm):
            pick = vals[0]
            for k in range(1, nm):
                pick = jnp.where(peer(k) == who, vals[k], pick)
            tot = tot + pick
        losst[nm + 1] = tot

    @pl.when(jnp.logical_not(last))
    def _():
        lf_copy().wait_recv()

    @pl.when(jnp.logical_not(first))
    def _():
        lf_copy().start()

    loss_out[...] = losst[nm + 1]

    def wgrad(mat, d):
        acc = None
        for c in range(nc):
            if mat == 0:
                part = dot_t(qkv[c, rowsl(d * qrows, qrows, qrows), :], n1buf[c])
            elif mat == 1:
                part = dot_t(obuf[c, rowsl(d * orows, orows, orows), :], mbuf[c])
            elif mat == 2:
                part = dot_t(n2buf[c], ubuf[c, rowsl(d * fl, fl, fl), :])
            else:
                part = dot_t(zbuf[c, rowsl(d * fl, fl, fl), :], dybuf[c])
            acc = part if acc is None else acc + part
        return acc

    sizes = (qrows, orows, dm_, fl)
    offs = (0, qrows, qrows + orows, qrows + orows + dm_)

    def rows_of(mat):
        return pl.ds(offs[mat], sizes[mat])

    recv_bufs = (rq, ro, ru, rd)
    outs = (gq_out, go_out, gu_out, gd_out)
    order = [2, 1, 3][: nm - 1] if nm == 4 else list(range(1, nm))

    def rs_copy(mat, k):
        return pltpu.make_async_remote_copy(
            src_ref=stage_buf.at[order.index(k), rows_of(mat)],
            dst_ref=recv_bufs[mat].at[nm - 1 - k], send_sem=rs_send.at[mat, k - 1],
            recv_sem=rs_recv.at[mat, nm - 1 - k], device_id={"model": peer(k)}, device_id_type=MESH)

    def rs_recv_copy(mat, slot):
        return pltpu.make_async_remote_copy(
            src_ref=stage_buf.at[0, rows_of(mat)],
            dst_ref=recv_bufs[mat].at[slot], send_sem=rs_send.at[mat, 0],
            recv_sem=rs_recv.at[mat, slot], device_id={"model": peer(1)}, device_id_type=MESH)

    mats = (3, 2, 0, 1)
    for k in order:
        for mat in mats:
            stage_buf[order.index(k), rows_of(mat)] = wgrad(mat, peer(k))
            rs_copy(mat, k).start()

    for mat in mats:
        go_buf[rows_of(mat)] = wgrad(mat, me)

    def load(mat, slot, r0, nr):
        return pltpu.make_async_copy(recv_bufs[mat].at[slot, pl.ds(r0, nr)], radd.at[pl.ds(0, nr)], ld_sem.at[0])

    def out_copy(mat):
        return pltpu.make_async_copy(go_buf.at[rows_of(mat)], outs[mat], out_sem.at[mat])

    slot_order = [nm - 1 - k for k in order]
    for pos, slot in enumerate(slot_order):
        for mat in mats:
            rs_recv_copy(mat, slot).wait_recv()
            for r0 in range(0, sizes[mat], 256):
                nr = min(256, sizes[mat] - r0)
                load(mat, slot, r0, nr).start()
                load(mat, slot, r0, nr).wait()
                go_buf[pl.ds(offs[mat] + r0, nr)] += radd[pl.ds(0, nr)]
            if pos == nm - 2:
                out_copy(mat).start()

    for mat in mats:
        out_copy(mat).wait()
    for idx in range(8):
        for k in range(1, nm):
            w_send(idx, k).wait_send()
    for k in order:
        for mat in mats:
            rs_copy(mat, k).wait_send()

    @pl.when(jnp.logical_not(first))
    def _():
        for c in range(nc):
            b_copy(c).wait_send()
        lf_copy().wait_send()

    @pl.when(last)
    def _():
        for k in range(1, nm):
            l_copy(k).wait_send()


def solution(mesh):
    ns = mesh.shape["stage"]
    nm = mesh.shape["model"]

    def per_device(tokens_in, targets, w_qkv, w_out, w_up, w_down):
        n_micro, seq_len, d_model = tokens_in.shape
        hl, hd, fl = w_qkv.shape[3], w_qkv.shape[5], w_up.shape[3]
        tc = min(CHUNK, seq_len // 2)
        nc = seq_len // tc
        assert n_micro == nm and w_qkv.shape[1] == 1 and hl == 2
        qrows, orows = hl * 3 * hd, hl * hd
        wqT = jnp.transpose(w_qkv[0, 0], (1, 2, 3, 0)).reshape(qrows, d_model)
        wq = jnp.transpose(wqT)
        wo = w_out[0, 0].reshape(orows, d_model)
        wu, wd = w_up[0, 0], w_down[0, 0]
        cfg = (ns, nm, nc, tc, d_model, hl, hd, fl)
        heads = nm * hl
        any_spec = pl.BlockSpec(memory_space=pl.ANY)
        rsum = qrows + orows + d_model + fl
        f32 = lambda *shape: jax.ShapeDtypeStruct(shape, F32)
        out_shape = (f32(qrows, d_model), f32(orows, d_model), f32(d_model, fl), f32(fl, d_model), f32(8, 128),
                     f32(nm - 1, qrows, d_model), f32(nm - 1, orows, d_model), f32(nm - 1, d_model, fl), f32(nm - 1, fl, d_model))
        vb = lambda *shape: pltpu.VMEM(shape, BF16)
        vf = lambda *shape: pltpu.VMEM(shape, F32)
        dma = lambda *shape: pltpu.SemaphoreType.DMA(shape)
        seqb = nc * tc
        scratch = [
            vb(nm * qrows, d_model), vb(d_model, nm * orows), vb(nm * fl, d_model), vb(nm, d_model, fl),
            vb(nm * fl, d_model), vb(nm, d_model, fl), vb(nm * orows, d_model), vb(d_model, nm * qrows),
            vb(nc, tc, d_model), vb(nc, d_model, tc), vb(nc, d_model, tc), vb(nc, nm * qrows, tc), vb(nm, seqb, qrows),
            vb(nc, nm * orows, tc), vb(nc, d_model, tc), vb(nc, d_model, tc), vb(nc, nm * fl, tc), vb(nc, nm * fl, tc),
            vb(nc * (nc + 1) // 2, heads, tc, tc), vb(nc, d_model, tc), vf(heads // 2, seqb, 2 * hd), vf(heads // 2, seqb, 2 * hd),
            vf(seqb, tc), vb(nc, d_model, tc), vb(nm * orows, tc), vf(nm + 2, 8, 128), vf(8, tc),
            vf(nm - 1, rsum, d_model), vf(rsum, d_model), vf(256, d_model),
            dma(8, nm - 1), dma(8, nm - 1), dma(8), dma(nc), dma(nc), dma(nc), dma(nc), dma(nc),
            dma(nm - 1), dma(nm - 1), pltpu.SemaphoreType.DMA, pltpu.SemaphoreType.DMA,
            dma(4, nm - 1), dma(4, nm - 1), dma(1), dma(4),
        ]
        res = pl.pallas_call(
            functools.partial(step_kernel, cfg),
            out_shape=out_shape,
            in_specs=[any_spec] * 10,
            out_specs=[any_spec] * 4 + [pl.BlockSpec(memory_space=pltpu.VMEM)] + [any_spec] * 4,
            scratch_shapes=scratch,
            compiler_params=pltpu.CompilerParams(collective_id=0, has_side_effects=True, vmem_limit_bytes=67043328),
            name="train_step",
        )(tokens_in, targets, wqT, jnp.transpose(wo), jnp.transpose(wu), jnp.transpose(wd), wd, wu, wo, wq)
        g_qkv = jnp.transpose(res[0].reshape(hl, 3, hd, d_model), (3, 0, 1, 2))[None, None]
        g_out = res[1].reshape(1, 1, hl, hd, d_model)
        return g_qkv, g_out, res[2][None, None], res[3][None, None], res[4][0, :1]

    tok_spec = P(None, "data", None)
    qkv_spec = P("stage", None, None, "model", None, None)
    out_spec = P("stage", None, "model", None, None)
    up_spec = P("stage", None, None, "model")
    down_spec = P("stage", None, "model", None)
    g_qkv_spec = P(("data", "stage"), None, None, "model", None, None)
    g_out_spec = P(("data", "stage"), None, "model", None, None)
    g_up_spec = P(("data", "stage"), None, None, "model")
    g_down_spec = P(("data", "stage"), None, "model", None)
    return jax.shard_map(per_device, mesh=mesh, in_specs=(tok_spec, tok_spec, qkv_spec, out_spec, up_spec, down_spec), out_specs=(g_qkv_spec, g_out_spec, g_up_spec, g_down_spec, P("data")), check_vma=False)
```

time: 2970 us -> 465 us (0.16)
  waiting for transfers between devices: 1850 us -> 0 us
  matrix products: 619 us -> 0 us
  Pallas kernels: 0 us -> 446 us
  other arithmetic: 281 us -> 0 us
  local copies, waits for them, and re-layouts: 131 us -> 16 us
  starting transfers between devices: 30.9 us -> 0 us
    psum x44 -> x0, waiting for transfers between devices: 1850 us -> none  [the longest x11 535 us: layer_fwd(): branch_a = lax.psum(part_a, 'model')]
    dot_general x154 -> x0, matrix products: 474 us -> none  [the longest x22 129 us: attn_core(): jnp.einsum('qhe,khe->hqk', queries, keys_in, preferred_element_type=jnp.f...]
    pallas_call x0 -> x1, Pallas kernels: none -> 446 us  [per_device(): pl.pallas_call(functools.partial(step_kernel, cfg), out_shape=out_shape,...]
    sub x22 -> x0, matrix products: 114 us -> none  [attn_core(): prob_bf = jax.nn.softmax(scores, axis=-1).astype(jnp.bfloat16)]
    dynamic_update_slice x44 -> x0, other arithmetic: 104 us -> none  [write_slot(): return lax.dynamic_update_slice(buf_arr, merged[None, None], start_at)]
    reduce_sum x55 -> x0, other arithmetic: 82.2 us -> none  [the longest x44 52.6 us: rms_norm(): inv_rms = lax.rsqrt(jnp.mean(hid32 * hid32, axis=-1, keepdims=True) + 1e-06)]
    dynamic_slice x44 -> x0, local copies, waits for them, and re-layouts: 70.8 us -> none  [write_slot(): lax.dynamic_slice(buf_arr, start_at, (1, 1) + buf_arr.shape[2:])[0, 0]]
    convert_element_type x22 -> x0, other arithmetic: 48.2 us -> none  [the longest x11 24.1 us: layer_bwd(): (grad_mid.astype(jnp.float32) + norm1_pull(grad_n1)[0].astype(jnp.float32...]
  transfers between devices with their start and end apart: 66 -> 0, of which waited for: 44 -> 0; matrix products, arithmetic and copies ran while one was open for 10% -> 0% of each run, Pallas kernels for 0% -> 0%
where the time goes in v1:
time: 465 us; the launch traced here: 462 us
  Pallas kernels  446 us (96%)
  local copies, waits for them, and re-layouts  16 us (3%)
    pallas_call x1, Pallas kernels, per_device(): pl.pallas_call(functools.partial(step_kernel, cfg), out_shape=out_shape,...  446 us

profile of v1, /device:TPU:96, one launch (start us, length us, event | category | flops | bytes accessed | tf_op | source)
XLA Modules:
  0.0 462.5 jit_solution(13110895189889250702)
XLA Ops:
  0.6 1.7 copy.17.woT_in
  2.3 1.9 copy.16
  4.2 2.0 copy.19.wdT_in
  6.3 2.0 copy.18.wuT_in
  8.3 445.9 %train_step.1 = (f32[384,512]{1,0:T(8,128)}, f32[128,512]{1,0:T(8,128)}, f32[512,512]{1,0:T(8,128)}, f32[512,512]{1,0:T(8,128)}, f32[8,128]{1,0:T(8,128)}, /*ind...) custom-call(bf16[4,1024,512]{2,1,0:T(8,128)(2,1)} %x_hbm.1, ...), custom_call_target="tpu_custom_call" | custom-call | tf_op jit(solution)/shard_map/train_step/pallas_call | solution.py:515
  454.2 0.0 copy-start
  454.2 1.3 slice.3
  455.5 2.1 copy.24
  457.6 1.7 copy.25
  459.2 2.3 copy.26
  461.5 0.0 copy-done
  461.5 1.0 copy.27
Async XLA Ops:
  454.2 7.3 %copy-start = (f32[512,512]{1,0:T(8,128)S(1)}, f32[512,512]{1,0:T(8,128)}, u32[]{:S(2)}) copy-start(f32[512,512]{1,0:T(8,128)} %get-tuple-element.13) | copy-start | bytes 3145732

commit v2 on v1

--- a/solution.py
+++ b/solution.py
@@ -16,7 +16,7 @@
 GELU_C = math.sqrt(2.0 / math.pi)
 GELU_A = 0.044715
 
-W_QT, W_OT, W_UT, W_DT, W_D, W_U, W_O, W_Q = range(8)
+W_Q, W_O, W_U, W_D = range(4)
 
 
 def dot(lhs, rhs):
@@ -48,12 +48,12 @@
     return cdf + u * (0.5 * GELU_C) * (1.0 - inner * inner) * (1.0 + (3.0 * GELU_A) * u2)
 
 
-def step_kernel(cfg, x_hbm, t_hbm, wqT_in, woT_in, wuT_in, wdT_in, wd_in, wu_in, wo_in, wq_in,
-                gq_out, go_out, gu_out, gd_out, loss_out, rq, ro, ru, rd,
+def step_kernel(cfg, x_hbm, t_hbm, wqT_in, wo_in, wu_in, wd_in,
+                gq_out, go_out, gu_out, gd_out, loss_out, far_p, far_m, near_p, near_m,
                 wqT, woT, wuT, wdT, wd, wu, wo, wq,
                 xin, hbuf, n1buf, qkv, qkvn, obuf, mbuf, n2buf, ubuf, zbuf, pbuf, dybuf, dvacc, dkacc, sscr,
-                ybuf, dobuf, losst, lossv, stage_buf, go_buf, radd,
-                ag_send, ag_recv, ag_loc, xsem, fsend, frecv, bsend, brecv, lsend, lrecv, lfsend, lfrecv,
+                ybuf, dobuf, losst, lossv, stage_buf, radd,
+                ag_send, ag_recv, ag_loc, go_sem, xsem, fsend, frecv, bsend, brecv, lsend, lrecv, lfsend, lfrecv,
                 rs_send, rs_recv, ld_sem, out_sem):
     ns, nm, nc, tc, dm_, hl, hd, fl = cfg
     heads = nm * hl
@@ -82,37 +82,54 @@
     def rowsl(start, size, mult):
         return pl.ds(pl.multiple_of(start, mult), size)
 
-    w_src = (wqT_in, woT_in, wuT_in, wdT_in, wd_in, wu_in, wo_in, wq_in)
-
-    def w_dst(idx, who):
-        if idx == W_QT:
-            return wqT.at[rowsl(who * qrows, qrows, qrows), :]
-        if idx == W_OT:
-            return woT.at[:, rowsl(who * orows, orows, orows)]
-        if idx == W_UT:
-            return wuT.at[rowsl(who * fl, fl, fl), :]
-        if idx == W_DT:
-            return wdT.at[who]
-        if idx == W_D:
-            return wd.at[rowsl(who * fl, fl, fl), :]
-        if idx == W_U:
-            return wu.at[who]
-        if idx == W_O:
-            return wo.at[rowsl(who * orows, orows, orows), :]
-        return wq.at[:, rowsl(who * qrows, qrows, qrows)]
-
-    def w_send(idx, k):
-        return pltpu.make_async_remote_copy(
-            src_ref=w_src[idx], dst_ref=w_dst(idx, me), send_sem=ag_send.at[idx, k - 1],
-            recv_sem=ag_recv.at[idx, k - 1], device_id={"model": peer(k)}, device_id_type=MESH)
-
-    def w_recv(idx, k):
-        return pltpu.make_async_remote_copy(
-            src_ref=w_src[idx], dst_ref=w_dst(idx, peer(nm - k)), send_sem=ag_send.at[idx, k - 1],
-            recv_sem=ag_recv.at[idx, k - 1], device_id={"model": peer(k)}, device_id_type=MESH)
+    plus, minus, far = 1, nm - 1, 2
+
+    def w_rows(idx, who, half=None):
+        size = (qrows, orows, fl, fl)[idx]
+        if idx in (W_Q, W_U):
+            buf = wqT if idx == W_Q else wuT
+            if half is None:
+                return buf.at[rowsl(who * size, size, size), :]
+            return buf.at[rowsl(who * size + half * (size // 2), size // 2, size // 2), :]
+        view = woT.at[:, rowsl(who * size, size, size)] if idx == W_O else wdT.at[who]
+        return view if half is None else view.at[pl.ds(half * (dm_ // 2), dm_ // 2), :]
+
+    def w_copy(idx, way):
+        to = plus if way in (0, 2) else minus
+        if way < 2:
+            src = wqT_in if idx == W_Q else w_rows(idx, me)
+            dst = w_rows(idx, me)
+        else:
+            src = dst = w_rows(idx, peer(minus if way == 2 else plus), way - 2)
+        return pltpu.make_async_remote_copy(
+            src_ref=src, dst_ref=dst, send_sem=ag_send.at[idx, way], recv_sem=ag_recv.at[idx, way],
+            device_id={"model": peer(to)}, device_id_type=MESH)
+
+    def w_arrival(idx, way):
+        who = peer((minus, plus, far, far)[way])
+        ref = w_rows(idx, who) if way < 2 else w_rows(idx, who, way - 2)
+        return pltpu.make_async_remote_copy(
+            src_ref=ref, dst_ref=ref, send_sem=ag_send.at[idx, way], recv_sem=ag_recv.at[idx, way],
+            device_id={"model": peer(plus)}, device_id_type=MESH)
 
     def w_local(idx):
-        return pltpu.make_async_copy(w_src[idx], w_dst(idx, me), ag_loc.at[idx])
+        src = (wqT_in, wo_in, wu_in, wd_in)[idx]
+        dst = (w_rows(W_Q, me), wo.at[rowsl(me * orows, orows, orows), :], wu.at[me], wd.at[rowsl(me * fl, fl, fl), :])[idx]
+        return pltpu.make_async_copy(src, dst, ag_loc.at[idx])
+
+    def w_own(idx):
+        for way in range(2):
+            w_copy(idx, way).start()
+
+    def w_forward(idx):
+        for way in range(2):
+            w_arrival(idx, way).wait_recv()
+        for way in range(2, 4):
+            w_copy(idx, way).start()
+
+    def w_wait(idx):
+        for way in range(2, 4):
+            w_arrival(idx, way).wait_recv()
 
     def x_copy(c):
         return pltpu.make_async_copy(x_hbm.at[me, pl.ds(c * tc, tc), :], xin.at[c], xsem.at[c])
@@ -130,15 +147,56 @@
         for c in range(nc):
             t_copy(c).start()
 
-    for idx in range(8):
+    for idx in range(4):
         w_local(idx).start()
-        for k in range(1, nm):
-            w_send(idx, k).start()
-
-    def w_wait(idx):
-        w_local(idx).wait()
-        for k in range(1, nm):
-            w_recv(idx, k).wait_recv()
+
+    odd = lax.rem(st, 2) == 1
+    early = st < 2
+
+    @pl.when(odd)
+    def _():
+        pl.semaphore_wait(go_sem, 1)
+
+    w_own(W_Q)
+    w_local(W_O).wait()
+    woT[:, rowsl(me * orows, orows, orows)] = jnp.transpose(wo[rowsl(me * orows, orows, orows), :])
+    w_own(W_O)
+    w_local(W_U).wait()
+    wuT[rowsl(me * fl, fl, fl), :] = jnp.transpose(wu[me])
+    w_local(W_Q).wait()
+    w_forward(W_Q)
+    w_own(W_U)
+    w_local(W_D).wait()
+    wdT[me] = jnp.transpose(wd[rowsl(me * fl, fl, fl), :])
+    w_forward(W_O)
+    w_own(W_D)
+
+    def pass_go():
+        @pl.when(jnp.logical_not(odd))
+        def _():
+            pl.semaphore_signal(go_sem, inc=1, device_id={"stage": nxt}, device_id_type=MESH)
+
+    def natural_weights():
+        @pl.loop(0, nm)
+        def _(f):
+            wu[f] = jnp.transpose(wuT[rowsl(f * fl, fl, fl), :])
+            wd[rowsl(f * fl, fl, fl), :] = jnp.transpose(wdT[f])
+            wo[rowsl(f * orows, orows, orows), :] = jnp.transpose(woT[:, rowsl(f * orows, orows, orows)])
+            wq[:, rowsl(f * qrows, qrows, qrows)] = jnp.transpose(wqT[rowsl(f * qrows, qrows, qrows), :])
+
+    late = st >= max(2, ns // 2)
+
+    @pl.when(jnp.logical_not(early))
+    def _():
+        w_forward(W_U)
+        w_forward(W_D)
+        pass_go()
+        for idx in range(4):
+            w_wait(idx)
+
+    @pl.when(late)
+    def _():
+        natural_weights()
 
     def f_copy(c):
         return pltpu.make_async_remote_copy(
@@ -170,8 +228,7 @@
     def causal(shape):
         return lax.broadcasted_iota(jnp.int32, shape, 0) <= lax.broadcasted_iota(jnp.int32, shape, 1)
 
-    @pl.loop(0, nc)
-    def _(c):
+    def attention_step(c):
         @pl.when(first)
         def _():
             x_copy(c).wait()
@@ -181,9 +238,9 @@
         def _():
             f_copy(c).wait_recv()
 
-        @pl.when(c == 0)
-        def _():
-            w_wait(W_QT)
+        @pl.when(early & (c == 0))
+        def _():
+            w_wait(W_Q)
 
         h32 = hbuf[c].astype(F32)
         n1 = (h32 * inv_rms(h32)).astype(BF16)
@@ -225,20 +282,12 @@
                             o_t = part if o_t is None else o_t + part
                         obuf[cc, pl.ds(pl.multiple_of((p * 2 + h) * hd, hd), hd), :] = o_t.astype(BF16)
 
-        @pl.when(c == 0)
-        def _():
-            w_wait(W_OT)
-
+    def mlp_step(c):
         a = dot(woT[...], obuf[c]).astype(BF16)
         m32 = (hbuf[c].astype(F32) + a.astype(F32)).astype(BF16).astype(F32)
         mbuf[c] = m32.astype(BF16)
         n2 = (m32 * inv_rms(m32)).astype(BF16)
         n2buf[c] = n2
-
-        @pl.when(c == 0)
-        def _():
-            w_wait(W_UT)
-            w_wait(W_DT)
 
         acc = None
         for f in range(nm):
@@ -263,6 +312,38 @@
             lossv[...] += jnp.sum((err * err).reshape(dm_ // 8, 8, tc), axis=0)
             dybuf[c] = (err * inv_d).astype(BF16)
 
+    @pl.loop(0, 2 * nc)
+    def _(n):
+        attn_turn = jnp.where(early, jnp.where(n < nc, 1, 0), 1 - lax.rem(n, 2))
+        c = jnp.where(early, lax.rem(n, nc), n // 2)
+
+        @pl.when(early & (n == 2))
+        def _():
+            w_forward(W_U)
+
+        @pl.when(early & (n == min(3, nc)))
+        def _():
+            w_forward(W_D)
+            pass_go()
+
+        @pl.when(attn_turn == 1)
+        def _():
+            attention_step(c)
+
+        @pl.when(early & (n == nc))
+        def _():
+            w_wait(W_O)
+            w_wait(W_U)
+            w_wait(W_D)
+
+        @pl.when(attn_turn == 0)
+        def _():
+            mlp_step(c)
+
+    @pl.when(jnp.logical_not(late))
+    def _():
+        natural_weights()
+
     def l_copy(k):
         return pltpu.make_async_remote_copy(
             src_ref=losst.at[nm], dst_ref=losst.at[3 - k if nm == 4 else nm - 1 - k], send_sem=lsend.at[k - 1],
@@ -287,13 +368,6 @@
         @pl.when(jnp.logical_not(last))
         def _():
             b_copy(c).wait_recv()
-
-        @pl.when(i == 0)
-        def _():
-            w_wait(W_D)
-            w_wait(W_U)
-            w_wait(W_O)
-            w_wait(W_Q)
 
         acc = None
         for f in range(nm):
@@ -410,57 +484,81 @@
     def rows_of(mat):
         return pl.ds(offs[mat], sizes[mat])
 
-    recv_bufs = (rq, ro, ru, rd)
     outs = (gq_out, go_out, gu_out, gd_out)
-    order = [2, 1, 3][: nm - 1] if nm == 4 else list(range(1, nm))
-
-    def rs_copy(mat, k):
-        return pltpu.make_async_remote_copy(
-            src_ref=stage_buf.at[order.index(k), rows_of(mat)],
-            dst_ref=recv_bufs[mat].at[nm - 1 - k], send_sem=rs_send.at[mat, k - 1],
-            recv_sem=rs_recv.at[mat, nm - 1 - k], device_id={"model": peer(k)}, device_id_type=MESH)
-
-    def rs_recv_copy(mat, slot):
-        return pltpu.make_async_remote_copy(
-            src_ref=stage_buf.at[0, rows_of(mat)],
-            dst_ref=recv_bufs[mat].at[slot], send_sem=rs_send.at[mat, 0],
-            recv_sem=rs_recv.at[mat, slot], device_id={"model": peer(1)}, device_id_type=MESH)
+
+    def half_of(mat, half):
+        return pl.ds(offs[mat] + half * (sizes[mat] // 2), sizes[mat] // 2)
+
+    def far_copy(mat, half):
+        buf = (far_p, far_m)[half]
+        rows = pl.ds(offs[mat] // 2, sizes[mat] // 2)
+        return pltpu.make_async_remote_copy(
+            src_ref=stage_buf.at[0, half_of(mat, half)], dst_ref=buf.at[rows], send_sem=rs_send.at[mat, half],
+            recv_sem=rs_recv.at[mat, half], device_id={"model": peer((plus, minus)[half])}, device_id_type=MESH)
+
+    def near_copy(mat, side, half):
+        buf = (near_p, near_m)[side]
+        return pltpu.make_async_remote_copy(
+            src_ref=stage_buf.at[1 + side, half_of(mat, half)], dst_ref=buf.at[half_of(mat, half)],
+            send_sem=rs_send.at[mat, 2 + 2 * side + half], recv_sem=rs_recv.at[mat, 2 + 2 * side + half],
+            device_id={"model": peer((plus, minus)[side])}, device_id_type=MESH)
 
     mats = (3, 2, 0, 1)
-    for k in order:
-        for mat in mats:
-            stage_buf[order.index(k), rows_of(mat)] = wgrad(mat, peer(k))
-            rs_copy(mat, k).start()
-
-    for mat in mats:
-        go_buf[rows_of(mat)] = wgrad(mat, me)
-
-    def load(mat, slot, r0, nr):
-        return pltpu.make_async_copy(recv_bufs[mat].at[slot, pl.ds(r0, nr)], radd.at[pl.ds(0, nr)], ld_sem.at[0])
+    for mat in mats:
+        stage_buf[0, rows_of(mat)] = wgrad(mat, peer(far))
+        for half in range(2):
+            far_copy(mat, half).start()
+    for mat in mats:
+        for side in range(2):
+            stage_buf[1 + side, rows_of(mat)] = wgrad(mat, peer((plus, minus)[side]))
+            near_copy(mat, side, 1 - side).start()
+
+    def load(src, nr):
+        return pltpu.make_async_copy(src, radd.at[pl.ds(0, nr)], ld_sem.at[0])
+
+    for mat in mats:
+        nr = sizes[mat] // 2
+        for half in range(2):
+            far_copy(mat, half).wait_recv()
+            src = (far_p, far_m)[half].at[pl.ds(offs[mat] // 2, nr)]
+            load(src, nr).start()
+            load(src, nr).wait()
+            stage_buf[1 + half, half_of(mat, half)] += radd[pl.ds(0, nr)]
+            near_copy(mat, half, half).start()
+
+    for mat in mats:
+        for half in range(2):
+            far_copy(mat, half).wait_send()
+        stage_buf[0, rows_of(mat)] = wgrad(mat, me)
 
     def out_copy(mat):
-        return pltpu.make_async_copy(go_buf.at[rows_of(mat)], outs[mat], out_sem.at[mat])
-
-    slot_order = [nm - 1 - k for k in order]
-    for pos, slot in enumerate(slot_order):
-        for mat in mats:
-            rs_recv_copy(mat, slot).wait_recv()
-            for r0 in range(0, sizes[mat], 256):
-                nr = min(256, sizes[mat] - r0)
-                load(mat, slot, r0, nr).start()
-                load(mat, slot, r0, nr).wait()
-                go_buf[pl.ds(offs[mat] + r0, nr)] += radd[pl.ds(0, nr)]
-            if pos == nm - 2:
-                out_copy(mat).start()
+        return pltpu.make_async_copy(stage_buf.at[0, rows_of(mat)], outs[mat], out_sem.at[mat])
+
+    def add_near(mat, side, half):
+        nr = sizes[mat] // 2
+        near_copy(mat, side, half).wait_recv()
+        src = (near_p, near_m)[side].at[half_of(mat, half)]
+        load(src, nr).start()
+        load(src, nr).wait()
+        stage_buf[0, half_of(mat, half)] += radd[pl.ds(0, nr)]
+
+    for mat in mats:
+        for side in range(2):
+            add_near(mat, side, 1 - side)
+    for mat in mats:
+        for side in range(2):
+            add_near(mat, side, side)
+        out_copy(mat).start()
 
     for mat in mats:
         out_copy(mat).wait()
-    for idx in range(8):
-        for k in range(1, nm):
-            w_send(idx, k).wait_send()
-    for k in order:
-        for mat in mats:
-            rs_copy(mat, k).wait_send()
+    for idx in range(4):
+        for way in range(4):
+            w_copy(idx, way).wait_send()
+    for mat in mats:
+        for half in range(2):
+            for side in range(2):
+                near_copy(mat, side, half).wait_send()
 
     @pl.when(jnp.logical_not(first))
     def _():
@@ -483,10 +581,9 @@
         hl, hd, fl = w_qkv.shape[3], w_qkv.shape[5], w_up.shape[3]
         tc = min(CHUNK, seq_len // 2)
         nc = seq_len // tc
-        assert n_micro == nm and w_qkv.shape[1] == 1 and hl == 2
+        assert n_micro == nm == 4 and w_qkv.shape[1] == 1 and hl == 2
         qrows, orows = hl * 3 * hd, hl * hd
         wqT = jnp.transpose(w_qkv[0, 0], (1, 2, 3, 0)).reshape(qrows, d_model)
-        wq = jnp.transpose(wqT)
         wo = w_out[0, 0].reshape(orows, d_model)
         wu, wd = w_up[0, 0], w_down[0, 0]
         cfg = (ns, nm, nc, tc, d_model, hl, hd, fl)
@@ -495,7 +592,7 @@
         rsum = qrows + orows + d_model + fl
         f32 = lambda *shape: jax.ShapeDtypeStruct(shape, F32)
         out_shape = (f32(qrows, d_model), f32(orows, d_model), f32(d_model, fl), f32(fl, d_model), f32(8, 128),
-                     f32(nm - 1, qrows, d_model), f32(nm - 1, orows, d_model), f32(nm - 1, d_model, fl), f32(nm - 1, fl, d_model))
+                     f32(rsum // 2, d_model), f32(rsum // 2, d_model), f32(rsum, d_model), f32(rsum, d_model))
         vb = lambda *shape: pltpu.VMEM(shape, BF16)
         vf = lambda *shape: pltpu.VMEM(shape, F32)
         dma = lambda *shape: pltpu.SemaphoreType.DMA(shape)
@@ -507,20 +604,20 @@
             vb(nc, nm * orows, tc), vb(nc, d_model, tc), vb(nc, d_model, tc), vb(nc, nm * fl, tc), vb(nc, nm * fl, tc),
             vb(nc * (nc + 1) // 2, heads, tc, tc), vb(nc, d_model, tc), vf(heads // 2, seqb, 2 * hd), vf(heads // 2, seqb, 2 * hd),
             vf(seqb, tc), vb(nc, d_model, tc), vb(nm * orows, tc), vf(nm + 2, 8, 128), vf(8, tc),
-            vf(nm - 1, rsum, d_model), vf(rsum, d_model), vf(256, d_model),
-            dma(8, nm - 1), dma(8, nm - 1), dma(8), dma(nc), dma(nc), dma(nc), dma(nc), dma(nc),
+            vf(3, rsum, d_model), vf(256, d_model),
+            dma(4, 4), dma(4, 4), dma(4), pltpu.SemaphoreType.REGULAR, dma(nc), dma(nc), dma(nc), dma(nc), dma(nc),
             dma(nm - 1), dma(nm - 1), pltpu.SemaphoreType.DMA, pltpu.SemaphoreType.DMA,
-            dma(4, nm - 1), dma(4, nm - 1), dma(1), dma(4),
+            dma(4, 6), dma(4, 6), dma(1), dma(4),
         ]
         res = pl.pallas_call(
             functools.partial(step_kernel, cfg),
             out_shape=out_shape,
-            in_specs=[any_spec] * 10,
+            in_specs=[any_spec] * 6,
             out_specs=[any_spec] * 4 + [pl.BlockSpec(memory_space=pltpu.VMEM)] + [any_spec] * 4,
             scratch_shapes=scratch,
             compiler_params=pltpu.CompilerParams(collective_id=0, has_side_effects=True, vmem_limit_bytes=67043328),
             name="train_step",
-        )(tokens_in, targets, wqT, jnp.transpose(wo), jnp.transpose(wu), jnp.transpose(wd), wd, wu, wo, wq)
+        )(tokens_in, targets, wqT, wo, wu, wd)
         g_qkv = jnp.transpose(res[0].reshape(hl, 3, hd, d_model), (3, 0, 1, 2))[None, None]
         g_out = res[1].reshape(1, 1, hl, hd, d_model)
         return g_qkv, g_out, res[2][None, None], res[3][None, None], res[4][0, :1]

time: 465 us -> 394 us (0.85)
  Pallas kernels: 446 us -> 384 us
  local copies, waits for them, and re-layouts: 16 us -> 8.28 us
    pallas_call x1, Pallas kernels: 446 us -> 384 us  [per_device(): pl.pallas_call(functools.partial(step_kernel, cfg), out_shape=out_shape,...]
    transpose x3 -> x0, local copies, waits for them, and re-layouts: 5.76 us -> none  [the longest x1 2.05 us: per_device(): jnp.transpose(wd)]
where the time goes in v2:
time: 394 us; the launch traced here: 393 us
  Pallas kernels  384 us (97%)
  local copies, waits for them, and re-layouts  8.28 us (2%)
    pallas_call x1, Pallas kernels, per_device(): pl.pallas_call(functools.partial(step_kernel, cfg), out_shape=out_shape,...  384 us

profile of v2, /device:TPU:96, one launch (start us, length us, event | category | flops | bytes accessed | tf_op | source)
XLA Modules:
  0.0 393.1 jit_solution(11783913384628911311)
XLA Ops:
  0.6 384.1 %train_step.1 = (f32[384,512]{1,0:T(8,128)}, f32[128,512]{1,0:T(8,128)}, f32[512,512]{1,0:T(8,128)}, f32[512,512]{1,0:T(8,128)}, f32[8,128]{1,0:T(8,128)}, /*ind...) custom-call(bf16[4,1024,512]{2,1,0:T(8,128)(2,1)} %x_hbm.1, ...), custom_call_target="tpu_custom_call" | custom-call | tf_op jit(solution)/shard_map/train_step/pallas_call | solution.py:612
  384.8 0.0 copy-start
  384.8 1.3 slice.3
  386.1 2.1 copy.15
  388.2 1.7 copy.16
  389.8 2.3 copy.17
  392.1 0.0 copy-done
  392.1 1.0 copy.18
Async XLA Ops:
  384.8 7.3 %copy-start = (f32[512,512]{1,0:T(8,128)S(1)}, f32[512,512]{1,0:T(8,128)}, u32[]{:S(2)}) copy-start(f32[512,512]{1,0:T(8,128)} %get-tuple-element.13) | copy-start | bytes 3145732

commit v3 on v2

--- a/solution.py
+++ b/solution.py
@@ -37,15 +37,16 @@
 
 
 def gelu(u):
-    inner = jnp.tanh(GELU_C * (u + GELU_A * (u * u * u)))
-    return u * (0.5 * (1.0 + inner))
+    tanh = jnp.tanh(u * (GELU_C + (GELU_C * GELU_A) * (u * u)))
+    half = 0.5 * u
+    return half + half * tanh
 
 
 def gelu_grad(u):
     u2 = u * u
-    inner = jnp.tanh(GELU_C * (u + GELU_A * (u2 * u)))
-    cdf = 0.5 * (1.0 + inner)
-    return cdf + u * (0.5 * GELU_C) * (1.0 - inner * inner) * (1.0 + (3.0 * GELU_A) * u2)
+    sig = 0.5 + 0.5 * jnp.tanh(u * (GELU_C + (GELU_C * GELU_A) * u2))
+    slope = u * (2.0 * GELU_C + (6.0 * GELU_C * GELU_A) * u2)
+    return sig * (1.0 + slope * (1.0 - sig))
 
 
 def step_kernel(cfg, x_hbm, t_hbm, wqT_in, wo_in, wu_in, wd_in,
@@ -91,7 +92,7 @@
             if half is None:
                 return buf.at[rowsl(who * size, size, size), :]
             return buf.at[rowsl(who * size + half * (size // 2), size // 2, size // 2), :]
-        view = woT.at[:, rowsl(who * size, size, size)] if idx == W_O else wdT.at[who]
+        view = (woT if idx == W_O else wdT).at[:, rowsl(who * size, size, size)]
         return view if half is None else view.at[pl.ds(half * (dm_ // 2), dm_ // 2), :]
 
     def w_copy(idx, way):
@@ -114,7 +115,7 @@
 
     def w_local(idx):
         src = (wqT_in, wo_in, wu_in, wd_in)[idx]
-        dst = (w_rows(W_Q, me), wo.at[rowsl(me * orows, orows, orows), :], wu.at[me], wd.at[rowsl(me * fl, fl, fl), :])[idx]
+        dst = (w_rows(W_Q, me), wo.at[rowsl(me * orows, orows, orows), :], wu.at[:, rowsl(me * fl, fl, fl)], wd.at[rowsl(me * fl, fl, fl), :])[idx]
         return pltpu.make_async_copy(src, dst, ag_loc.at[idx])
 
     def w_own(idx):
@@ -162,12 +163,12 @@
     woT[:, rowsl(me * orows, orows, orows)] = jnp.transpose(wo[rowsl(me * orows, orows, orows), :])
     w_own(W_O)
     w_local(W_U).wait()
-    wuT[rowsl(me * fl, fl, fl), :] = jnp.transpose(wu[me])
+    wuT[rowsl(me * fl, fl, fl), :] = jnp.transpose(wu[:, rowsl(me * fl, fl, fl)])
     w_local(W_Q).wait()
     w_forward(W_Q)
     w_own(W_U)
     w_local(W_D).wait()
-    wdT[me] = jnp.transpose(wd[rowsl(me * fl, fl, fl), :])
+    wdT[:, rowsl(me * fl, fl, fl)] = jnp.transpose(wd[rowsl(me * fl, fl, fl), :])
     w_forward(W_O)
     w_own(W_D)
 
@@ -179,8 +180,8 @@
     def natural_weights():
         @pl.loop(0, nm)
         def _(f):
-            wu[f] = jnp.transpose(wuT[rowsl(f * fl, fl, fl), :])
-            wd[rowsl(f * fl, fl, fl), :] = jnp.transpose(wdT[f])
+            wu[:, rowsl(f * fl, fl, fl)] = jnp.transpose(wuT[rowsl(f * fl, fl, fl), :])
+            wd[rowsl(f * fl, fl, fl), :] = jnp.transpose(wdT[:, rowsl(f * fl, fl, fl)])
             wo[rowsl(f * orows, orows, orows), :] = jnp.transpose(woT[:, rowsl(f * orows, orows, orows)])
             wq[:, rowsl(f * qrows, qrows, qrows)] = jnp.transpose(wqT[rowsl(f * qrows, qrows, qrows), :])
 
@@ -211,7 +212,7 @@
     lossv[...] = jnp.zeros_like(lossv)
 
     def head_rows(p, h, part):
-        return pl.ds(pl.multiple_of(p * (2 * 3 * hd) + (h * 3 + part) * hd, hd), hd)
+        return pl.ds(p * (2 * 3 * hd) + (h * 3 + part) * hd, hd)
 
     k_lane = (0, 2 * 2 * hd)
     v_lane = (2 * hd, 2 * 2 * hd)
@@ -225,8 +226,110 @@
         zero = jnp.zeros_like(val)
         return jnp.concatenate([val, zero] if h == 0 else [zero, val], axis=0)
 
-    def causal(shape):
-        return lax.broadcasted_iota(jnp.int32, shape, 0) <= lax.broadcasted_iota(jnp.int32, shape, 1)
+    def causal(shape, row0):
+        return lax.broadcasted_iota(jnp.int32, shape, 0) + row0 <= lax.broadcasted_iota(jnp.int32, shape, 1)
+
+    def attention(cc):
+        nk = (cc + 1) * tc
+        slots = min(heads, sscr.shape[0] // nk)
+        ahead = min(4, slots - 1)
+        sub = tc // 2
+
+        def front(head):
+            p, h = head // 2, head % 2
+            base = (head % slots) * nk
+            qz = pad_k(qkv[cc, head_rows(p, h, 0), :], h)
+            tops, sums = [], []
+            for j in range(cc + 1):
+                s = dot(qkvn[p, pl.ds(j * tc, tc), pl.ds(k_lane[h], two)], qz)
+                for r in range(0, tc, sub):
+                    part = s[r:r + sub]
+                    if j == cc:
+                        part = jnp.where(causal(part.shape, r), part, NEG)
+                    top = jnp.max(part, axis=0, keepdims=True)
+                    e = jnp.exp2((part - top) * exp_c)
+                    sscr[pl.ds(base + j * tc + r, sub), :] = e
+                    tops.append(top)
+                    sums.append(jnp.sum(e, axis=0, keepdims=True))
+            mx = functools.reduce(jnp.maximum, tops)
+            scales = [jnp.exp2((top - mx) * exp_c) for top in tops]
+            inv = 1.0 / functools.reduce(jnp.add, [a * b for a, b in zip(scales, sums)])
+            return [a * inv for a in scales]
+
+        def back(head, factors):
+            p, h = head // 2, head % 2
+            base = (head % slots) * nk
+            o_t = None
+            for j in range(cc + 1):
+                parts = []
+                for i in range(2):
+                    pr = (sscr[pl.ds(base + j * tc + i * sub, sub), :] * factors[2 * j + i]).astype(BF16)
+                    pbuf[cc * (cc + 1) // 2 + j, head, pl.ds(i * sub, sub), :] = pr
+                    parts.append(pr)
+                part = dot(qkv[j, head_rows(p, h, 2), :], jnp.concatenate(parts, axis=0))
+                o_t = part if o_t is None else o_t + part
+            obuf[cc, pl.ds(head * hd, hd), :] = o_t.astype(BF16)
+
+        factors = {}
+        for head in range(ahead):
+            factors[head] = front(head)
+        for head in range(heads):
+            if head + ahead < heads:
+                factors[head + ahead] = front(head + ahead)
+            back(head, factors.pop(head))
+
+    def attention_grad(cc):
+        units = [(p, j) for p in range(heads // 2) for j in range(cc + 1)]
+        dqs = {}
+        held = {}
+
+        def of_head(p, h):
+            if (p, h) not in held:
+                rows = pl.ds((p * 2 + h) * hd, hd)
+                do_t = dobuf[rows, :]
+                dsum = jnp.sum(do_t.astype(F32) * obuf[cc, rows, :].astype(F32), axis=0, keepdims=True)
+                held[p, h] = (pad_v(do_t, h), dsum)
+            return held[p, h]
+
+        def front(p, j):
+            out = []
+            for h in range(2):
+                do_z, dsum = of_head(p, h)
+                pr = pbuf[cc * (cc + 1) // 2 + j, p * 2 + h]
+                dp = dot(qkvn[p, pl.ds(j * tc, tc), pl.ds(v_lane[h], two)], do_z).astype(BF16).astype(F32)
+                out.append((pr.astype(F32) * (dp - dsum)).astype(BF16))
+            return out
+
+        def back(p, j, ds):
+            dv_new = dk_new = None
+            for h in range(2):
+                do_z, _ = of_head(p, h)
+                dv_h = dot_t(pbuf[cc * (cc + 1) // 2 + j, p * 2 + h], do_z)
+                dk_h = dot_t(ds[h], pad_v(qkv[cc, head_rows(p, h, 0), :], h))
+                dv_new = dv_h if dv_new is None else dv_new + dv_h
+                dk_new = dk_h if dk_new is None else dk_new + dk_h
+                dq_h = dot(qkv[j, head_rows(p, h, 1), :], ds[h])
+                dqs[p, h] = dq_h if j == 0 else dqs[p, h] + dq_h
+            rows = pl.ds(j * tc, tc)
+            if cc < nc - 1:
+                dv_new = dv_new + dvacc[p, rows, :]
+                dk_new = dk_new + dkacc[p, rows, :]
+            if j < cc:
+                dvacc[p, rows, :] = dv_new
+                dkacc[p, rows, :] = dk_new
+                return
+            dv_t = jnp.transpose(dv_new).astype(BF16)
+            dk_t = (jnp.transpose(dk_new) * scale).astype(BF16)
+            for h in range(2):
+                qkv[cc, head_rows(p, h, 0), :] = (dqs[p, h] * scale).astype(BF16)
+                qkv[cc, head_rows(p, h, 1), :] = dk_t[h * hd:(h + 1) * hd, :]
+                qkv[cc, head_rows(p, h, 2), :] = dv_t[h * hd:(h + 1) * hd, :]
+
+        ds = front(*units[0])
+        for n, unit in enumerate(units):
+            later = front(*units[n + 1]) if n + 1 < len(units) else None
+            back(*unit, ds)
+            ds = later
 
     def attention_step(c):
         @pl.when(first)
@@ -252,35 +355,7 @@
             qkvn[r, pl.ds(pl.multiple_of(c * tc, tc), tc), :] = jnp.transpose(blk)
 
         for cc in range(nc):
-            @pl.when(c == cc)
-            def _():
-                @pl.loop(0, heads // 2)
-                def _(p):
-                    for h in range(2):
-                        q_t = qkv[cc, head_rows(p, h, 0), :]
-                        qz = pad_k(q_t, h)
-                        mx = None
-                        for j in range(cc + 1):
-                            s = dot(qkvn[p, pl.ds(j * tc, tc), pl.ds(k_lane[h], two)], qz)
-                            if j == cc:
-                                s = jnp.where(causal(s.shape), s, NEG)
-                            sscr[pl.ds(j * tc, tc), :] = s
-                            bm = jnp.max(s, axis=0, keepdims=True)
-                            mx = bm if mx is None else jnp.maximum(mx, bm)
-                        den = None
-                        for j in range(cc + 1):
-                            e = jnp.exp2((sscr[pl.ds(j * tc, tc), :] - mx) * exp_c)
-                            sscr[pl.ds(j * tc, tc), :] = e
-                            es = jnp.sum(e, axis=0, keepdims=True)
-                            den = es if den is None else den + es
-                        inv = 1.0 / den
-                        o_t = None
-                        for j in range(cc + 1):
-                            pr = (sscr[pl.ds(j * tc, tc), :] * inv).astype(BF16)
-                            pbuf[cc * (cc + 1) // 2 + j, p * 2 + h] = pr
-                            part = dot(qkv[j, head_rows(p, h, 2), :], pr)
-                            o_t = part if o_t is None else o_t + part
-                        obuf[cc, pl.ds(pl.multiple_of((p * 2 + h) * hd, hd), hd), :] = o_t.astype(BF16)
+            pl.when(c == cc)(functools.partial(attention, cc))
 
     def mlp_step(c):
         a = dot(woT[...], obuf[c]).astype(BF16)
@@ -289,15 +364,13 @@
         n2 = (m32 * inv_rms(m32)).astype(BF16)
         n2buf[c] = n2
 
-        acc = None
-        for f in range(nm):
-            rows = pl.ds(f * fl, fl)
+        blk = fl // 2
+        for f in range(2 * nm):
+            rows = pl.ds(f * blk, blk)
             u = dot(wuT[rows, :], n2buf[c]).astype(BF16)
             ubuf[c, rows, :] = u
-            z = gelu(u.astype(F32)).astype(BF16)
-            zbuf[c, rows, :] = z
-            part = dot(wdT[f], z)
-            acc = part if acc is None else acc + part
+            zbuf[c, rows, :] = gelu(u.astype(F32)).astype(BF16)
+        acc = dot(wdT[...], zbuf[c])
         y32 = (mbuf[c].astype(F32) + acc.astype(BF16).astype(F32)).astype(BF16)
         ybuf[c] = y32
 
@@ -369,14 +442,12 @@
         def _():
             b_copy(c).wait_recv()
 
-        acc = None
-        for f in range(nm):
-            rows = pl.ds(f * fl, fl)
+        blk = fl // 4
+        for f in range(4 * nm):
+            rows = pl.ds(f * blk, blk)
             dz = dot(wd[rows, :], dybuf[c]).astype(BF16).astype(F32)
-            du = (dz * gelu_grad(ubuf[c, rows, :].astype(F32))).astype(BF16)
-            ubuf[c, rows, :] = du
-            part = dot(wu[f], du)
-            acc = part if acc is None else acc + part
+            ubuf[c, rows, :] = (dz * gelu_grad(ubuf[c, rows, :].astype(F32))).astype(BF16)
+        acc = dot(wu[...], ubuf[c])
         dn2 = acc.astype(BF16).astype(F32)
         m32 = mbuf[c].astype(F32)
         pull = norm_pull(m32, inv_rms(m32), dn2).astype(BF16)
@@ -385,47 +456,7 @@
         dobuf[...] = dot(wo[...], dmid).astype(BF16)
 
         for cc in range(nc):
-            @pl.when(c == cc)
-            def _():
-                @pl.loop(0, heads // 2)
-                def _(p):
-                    dq = [None, None]
-                    qz = []
-                    dz_v = []
-                    dsum = []
-                    for h in range(2):
-                        orow = pl.ds(pl.multiple_of((p * 2 + h) * hd, hd), hd)
-                        do_t = dobuf[orow, :]
-                        dsum.append(jnp.sum(do_t.astype(F32) * obuf[cc, orow, :].astype(F32), axis=0, keepdims=True))
-                        dz_v.append(pad_v(do_t, h))
-                        qz.append(pad_v(qkv[cc, head_rows(p, h, 0), :], h))
-                    for j in range(cc + 1):
-                        dv_new = None
-                        dk_new = None
-                        for h in range(2):
-                            pr = pbuf[cc * (cc + 1) // 2 + j, p * 2 + h]
-                            dp = dot(qkvn[p, pl.ds(j * tc, tc), pl.ds(v_lane[h], two)], dz_v[h]).astype(BF16).astype(F32)
-                            ds = (pr.astype(F32) * (dp - dsum[h])).astype(BF16)
-                            dv_h = dot_t(pr, dz_v[h])
-                            dk_h = dot_t(ds, qz[h])
-                            dv_new = dv_h if dv_new is None else dv_new + dv_h
-                            dk_new = dk_h if dk_new is None else dk_new + dk_h
-                            dq_h = dot(qkv[j, head_rows(p, h, 1), :], ds)
-                            dq[h] = dq_h if dq[h] is None else dq[h] + dq_h
-                        rows = pl.ds(j * tc, tc)
-                        if cc < nc - 1:
-                            dv_new = dv_new + dvacc[p, rows, :]
-                            dk_new = dk_new + dkacc[p, rows, :]
-                        if j < cc:
-                            dvacc[p, rows, :] = dv_new
-                            dkacc[p, rows, :] = dk_new
-                        else:
-                            dv_t = jnp.transpose(dv_new).astype(BF16)
-                            dk_t = (jnp.transpose(dk_new) * scale).astype(BF16)
-                            for h in range(2):
-                                qkv[cc, head_rows(p, h, 0), :] = (dq[h] * scale).astype(BF16)
-                                qkv[cc, head_rows(p, h, 1), :] = dk_t[h * hd:(h + 1) * hd, :]
-                                qkv[cc, head_rows(p, h, 2), :] = dv_t[h * hd:(h + 1) * hd, :]
+            pl.when(c == cc)(functools.partial(attention_grad, cc))
 
         dn1 = dot(wq[...], qkv[c]).astype(BF16).astype(F32)
         h32 = hbuf[c].astype(F32)
@@ -598,12 +629,12 @@
         dma = lambda *shape: pltpu.SemaphoreType.DMA(shape)
         seqb = nc * tc
         scratch = [
-            vb(nm * qrows, d_model), vb(d_model, nm * orows), vb(nm * fl, d_model), vb(nm, d_model, fl),
-            vb(nm * fl, d_model), vb(nm, d_model, fl), vb(nm * orows, d_model), vb(d_model, nm * qrows),
+            vb(nm * qrows, d_model), vb(d_model, nm * orows), vb(nm * fl, d_model), vb(d_model, nm * fl),
+            vb(nm * fl, d_model), vb(d_model, nm * fl), vb(nm * orows, d_model), vb(d_model, nm * qrows),
             vb(nc, tc, d_model), vb(nc, d_model, tc), vb(nc, d_model, tc), vb(nc, nm * qrows, tc), vb(nm, seqb, qrows),
             vb(nc, nm * orows, tc), vb(nc, d_model, tc), vb(nc, d_model, tc), vb(nc, nm * fl, tc), vb(nc, nm * fl, tc),
             vb(nc * (nc + 1) // 2, heads, tc, tc), vb(nc, d_model, tc), vf(heads // 2, seqb, 2 * hd), vf(heads // 2, seqb, 2 * hd),
-            vf(seqb, tc), vb(nc, d_model, tc), vb(nm * orows, tc), vf(nm + 2, 8, 128), vf(8, tc),
+            vf(2 * seqb, tc), vb(nc, d_model, tc), vb(nm * orows, tc), vf(nm + 2, 8, 128), vf(8, tc),
             vf(3, rsum, d_model), vf(256, d_model),
             dma(4, 4), dma(4, 4), dma(4), pltpu.SemaphoreType.REGULAR, dma(nc), dma(nc), dma(nc), dma(nc), dma(nc),
             dma(nm - 1), dma(nm - 1), pltpu.SemaphoreType.DMA, pltpu.SemaphoreType.DMA,

time: 394 us -> 338 us (0.86)
  Pallas kernels: 384 us -> 328 us
    pallas_call x1, Pallas kernels: 384 us -> 328 us  [per_device(): pl.pallas_call(functools.partial(step_kernel, cfg), out_shape=out_shape,...]
where the time goes in v3:
time: 338 us; the launch traced here: 337 us
  Pallas kernels  328 us (97%)
  local copies, waits for them, and re-layouts  8.28 us (2%)
    pallas_call x1, Pallas kernels, per_device(): pl.pallas_call(functools.partial(step_kernel, cfg), out_shape=out_shape,...  328 us
    unnamed x6, local copies, waits for them, and re-layouts  7 us

profile of v3, /device:TPU:96, one launch (start us, length us, event | category | flops | bytes accessed | tf_op | source)
XLA Modules:
  0.0 337.0 jit_solution(18151984757802831380)
XLA Ops:
  0.6 328.1 %train_step.1 = (f32[384,512]{1,0:T(8,128)}, f32[128,512]{1,0:T(8,128)}, f32[512,512]{1,0:T(8,128)}, f32[512,512]{1,0:T(8,128)}, f32[8,128]{1,0:T(8,128)}, /*ind...) custom-call(bf16[4,1024,512]{2,1,0:T(8,128)(2,1)} %x_hbm.1, ...), custom_call_target="tpu_custom_call" | custom-call | tf_op jit(solution)/shard_map/train_step/pallas_call | solution.py:643
  328.7 0.0 copy-start
  328.7 1.3 slice.3
  330.0 2.1 copy.15
  332.1 1.7 copy.16
  333.8 2.3 copy.17
  336.0 0.0 copy-done
  336.0 1.0 copy.18
Async XLA Ops:
  328.7 7.3 %copy-start = (f32[512,512]{1,0:T(8,128)S(1)}, f32[512,512]{1,0:T(8,128)}, u32[]{:S(2)}) copy-start(f32[512,512]{1,0:T(8,128)} %get-tuple-element.13) | copy-start | bytes 3145732

commit v4 on v3

--- a/solution.py
+++ b/solution.py
@@ -50,12 +50,12 @@
 
 
 def step_kernel(cfg, x_hbm, t_hbm, wqT_in, wo_in, wu_in, wd_in,
-                gq_out, go_out, gu_out, gd_out, loss_out, far_p, far_m, near_p, near_m,
+                sum_out, loss_out, far_p, far_m, near_e, near_l, z_recv, z_fwd, dy_recv,
                 wqT, woT, wuT, wdT, wd, wu, wo, wq,
                 xin, hbuf, n1buf, qkv, qkvn, obuf, mbuf, n2buf, ubuf, zbuf, pbuf, dybuf, dvacc, dkacc, sscr,
-                ybuf, dobuf, losst, lossv, stage_buf, radd,
+                ybuf, dobuf, losst, lossv, stage_buf, radd, gdacc, zdy,
                 ag_send, ag_recv, ag_loc, go_sem, xsem, fsend, frecv, bsend, brecv, lsend, lrecv, lfsend, lfrecv,
-                rs_send, rs_recv, ld_sem, out_sem):
+                rs_send, rs_recv, ld_sem, out_sem, z_send, z_arr, dy_send, dy_arr):
     ns, nm, nc, tc, dm_, hl, hd, fl = cfg
     heads = nm * hl
     qrows = hl * 3 * hd
@@ -208,6 +208,42 @@
         return pltpu.make_async_remote_copy(
             src_ref=ybuf.at[c], dst_ref=dybuf.at[c], send_sem=bsend.at[c], recv_sem=brecv.at[c],
             device_id={"stage": prv}, device_id_type=MESH)
+
+    def ring_copy(src, dst, send, recv, way):
+        return pltpu.make_async_remote_copy(
+            src_ref=src, dst_ref=dst, send_sem=send, recv_sem=recv,
+            device_id={"model": peer((plus, minus)[way % 2])}, device_id_type=MESH)
+
+    hf = fl // 2
+
+    def z_copy(c, way):
+        if way < 2:
+            src, dst = zbuf.at[c, rowsl(peer((plus, minus)[way]) * fl, fl, fl), :], z_recv.at[way, c]
+        elif way < 4:
+            src, dst = zbuf.at[c, rowsl(peer(far) * fl + (way - 2) * hf, hf, hf), :], z_fwd.at[way - 2, c]
+        else:
+            src, dst = z_fwd.at[way - 4, c], z_recv.at[2, c, pl.ds((way - 4) * hf, hf)]
+        return ring_copy(src, dst, z_send.at[way, c], z_arr.at[way, c], way)
+
+    def z_forward(c):
+        for way in (2, 3):
+            z_copy(c, way).wait_recv()
+        for way in (4, 5):
+            z_copy(c, way).start()
+
+    def dy_copy(c, way):
+        if way < 2:
+            src, dst = dybuf.at[c], dy_recv.at[way, c]
+        else:
+            rows = pl.ds((way - 2) * (dm_ // 2), dm_ // 2)
+            src, dst = dy_recv.at[way - 2, c, rows], dy_recv.at[2, c, rows]
+        return ring_copy(src, dst, dy_send.at[way, c], dy_arr.at[way, c], way)
+
+    def dy_forward(c):
+        for way in (0, 1):
+            dy_copy(c, way).wait_recv()
+        for way in (2, 3):
+            dy_copy(c, way).start()
 
     lossv[...] = jnp.zeros_like(lossv)
 
@@ -370,6 +406,8 @@
             u = dot(wuT[rows, :], n2buf[c]).astype(BF16)
             ubuf[c, rows, :] = u
             zbuf[c, rows, :] = gelu(u.astype(F32)).astype(BF16)
+        for way in range(4):
+            z_copy(c, way).start()
         acc = dot(wdT[...], zbuf[c])
         y32 = (mbuf[c].astype(F32) + acc.astype(BF16).astype(F32)).astype(BF16)
         ybuf[c] = y32
@@ -416,6 +454,8 @@
     @pl.when(jnp.logical_not(late))
     def _():
         natural_weights()
+        for c in range(nc):
+            z_forward(c)
 
     def l_copy(k):
         return pltpu.make_async_remote_copy(
@@ -434,6 +474,8 @@
         for k in range(1, nm):
             l_copy(k).start()
 
+    delay = jnp.where(late, 2, 1)
+
     @pl.loop(0, nc)
     def _(i):
         c = nc - 1 - i
@@ -441,6 +483,9 @@
         @pl.when(jnp.logical_not(last))
         def _():
             b_copy(c).wait_recv()
+
+        for way in range(2):
+            dy_copy(c, way).start()
 
         blk = fl // 4
         for f in range(4 * nm):
@@ -471,6 +516,19 @@
         @pl.when(jnp.logical_not(first))
         def _():
             b_copy(c).start()
+
+        @pl.when(late)
+        def _():
+            z_forward(i)
+
+        @pl.when(c + delay < nc)
+        def _():
+            dy_forward(c + delay)
+
+    for c in range(2):
+        @pl.when(c < delay)
+        def _():
+            dy_forward(c)
 
     @pl.when(last)
     def _():
@@ -509,32 +567,26 @@
             acc = part if acc is None else acc + part
         return acc
 
-    sizes = (qrows, orows, dm_, fl)
-    offs = (0, qrows, qrows + orows, qrows + orows + dm_)
+    sizes = (qrows, orows, dm_)
+    offs = (0, qrows, qrows + orows)
 
     def rows_of(mat):
         return pl.ds(offs[mat], sizes[mat])
 
-    outs = (gq_out, go_out, gu_out, gd_out)
-
     def half_of(mat, half):
         return pl.ds(offs[mat] + half * (sizes[mat] // 2), sizes[mat] // 2)
 
     def far_copy(mat, half):
-        buf = (far_p, far_m)[half]
         rows = pl.ds(offs[mat] // 2, sizes[mat] // 2)
-        return pltpu.make_async_remote_copy(
-            src_ref=stage_buf.at[0, half_of(mat, half)], dst_ref=buf.at[rows], send_sem=rs_send.at[mat, half],
-            recv_sem=rs_recv.at[mat, half], device_id={"model": peer((plus, minus)[half])}, device_id_type=MESH)
+        return ring_copy(stage_buf.at[0, half_of(mat, half)], (far_p, far_m)[half].at[rows],
+                         rs_send.at[mat, half], rs_recv.at[mat, half], half)
 
     def near_copy(mat, side, half):
-        buf = (near_p, near_m)[side]
-        return pltpu.make_async_remote_copy(
-            src_ref=stage_buf.at[1 + side, half_of(mat, half)], dst_ref=buf.at[half_of(mat, half)],
-            send_sem=rs_send.at[mat, 2 + 2 * side + half], recv_sem=rs_recv.at[mat, 2 + 2 * side + half],
-            device_id={"model": peer((plus, minus)[side])}, device_id_type=MESH)
-
-    mats = (3, 2, 0, 1)
+        way = 2 + 2 * side + half
+        return ring_copy(stage_buf.at[1 + side, half_of(mat, half)], (near_l if side == half else near_e).at[half_of(mat, half)],
+                         rs_send.at[mat, way], rs_recv.at[mat, way], side)
+
+    mats = (2, 0, 1)
     for mat in mats:
         stage_buf[0, rows_of(mat)] = wgrad(mat, peer(far))
         for half in range(2):
@@ -562,27 +614,58 @@
             far_copy(mat, half).wait_send()
         stage_buf[0, rows_of(mat)] = wgrad(mat, me)
 
+    def zdy_load(n, buf):
+        slot, c = n // nc, lax.rem(n, nc)
+        return (pltpu.make_async_copy(z_recv.at[slot, c], zdy.at[buf, pl.ds(0, fl)], ld_sem.at[1 + buf]),
+                pltpu.make_async_copy(dy_recv.at[slot, c], zdy.at[buf, pl.ds(fl, dm_)], ld_sem.at[3 + buf]))
+
+    gdacc[...] = wgrad(3, me)
+    for c in range(nc):
+        for way in (0, 1, 4, 5):
+            z_copy(c, way).wait_recv()
+        for way in (2, 3):
+            dy_copy(c, way).wait_recv()
+    for cp in zdy_load(0, 0):
+        cp.start()
+
+    @pl.loop(0, 3 * nc)
+    def _(n):
+        buf = lax.rem(n, 2)
+
+        @pl.when(n + 1 < 3 * nc)
+        def _():
+            for cp in zdy_load(n + 1, 1 - buf):
+                cp.start()
+
+        for cp in zdy_load(n, buf):
+            cp.wait()
+        gdacc[...] += dot_t(zdy[buf, pl.ds(0, fl), :], zdy[buf, pl.ds(fl, dm_), :])
+
     def out_copy(mat):
-        return pltpu.make_async_copy(stage_buf.at[0, rows_of(mat)], outs[mat], out_sem.at[mat])
-
-    def add_near(mat, side, half):
+        if mat == 3:
+            return pltpu.make_async_copy(gdacc, sum_out.at[pl.ds(qrows + orows + dm_, fl)], out_sem.at[3])
+        return pltpu.make_async_copy(stage_buf.at[0, rows_of(mat)], sum_out.at[rows_of(mat)], out_sem.at[mat])
+
+    out_copy(3).start()
+    for mat in mats:
         nr = sizes[mat] // 2
-        near_copy(mat, side, half).wait_recv()
-        src = (near_p, near_m)[side].at[half_of(mat, half)]
-        load(src, nr).start()
-        load(src, nr).wait()
-        stage_buf[0, half_of(mat, half)] += radd[pl.ds(0, nr)]
-
+        for side in range(2):
+            near_copy(mat, side, 1 - side).wait_recv()
+            load(near_e.at[half_of(mat, 1 - side)], nr).start()
+            load(near_e.at[half_of(mat, 1 - side)], nr).wait()
+            stage_buf[0, half_of(mat, 1 - side)] += radd[pl.ds(0, nr)]
+        out_copy(mat).start()
     for mat in mats:
         for side in range(2):
-            add_near(mat, side, 1 - side)
-    for mat in mats:
-        for side in range(2):
-            add_near(mat, side, side)
-        out_copy(mat).start()
-
-    for mat in mats:
+            near_copy(mat, side, side).wait_recv()
+
+    for mat in range(4):
         out_copy(mat).wait()
+    for c in range(nc):
+        for way in range(6):
+            z_copy(c, way).wait_send()
+        for way in range(4):
+            dy_copy(c, way).wait_send()
     for idx in range(4):
         for way in range(4):
             w_copy(idx, way).wait_send()
@@ -601,6 +684,14 @@
     def _():
         for k in range(1, nm):
             l_copy(k).wait_send()
+
+
+def finish_kernel(sq, so, su, sd, lq, lo, lu, loss, gq, go, gu, gd, loss_out):
+    gq[...] = sq[...] + lq[...]
+    go[...] = so[...] + lo[...]
+    gu[...] = su[...] + lu[...]
+    gd[...] = sd[...]
+    loss_out[0] = loss[0, 0]
 
 
 def solution(mesh):
@@ -620,14 +711,15 @@
         cfg = (ns, nm, nc, tc, d_model, hl, hd, fl)
         heads = nm * hl
         any_spec = pl.BlockSpec(memory_space=pl.ANY)
-        rsum = qrows + orows + d_model + fl
         f32 = lambda *shape: jax.ShapeDtypeStruct(shape, F32)
-        out_shape = (f32(qrows, d_model), f32(orows, d_model), f32(d_model, fl), f32(fl, d_model), f32(8, 128),
-                     f32(rsum // 2, d_model), f32(rsum // 2, d_model), f32(rsum, d_model), f32(rsum, d_model))
+        rsum = qrows + orows + d_model
+        seqb = nc * tc
+        b16 = lambda *shape: jax.ShapeDtypeStruct(shape, BF16)
+        out_shape = (f32(rsum + fl, d_model), f32(8, 128), f32(rsum // 2, d_model), f32(rsum // 2, d_model), f32(rsum, d_model),
+                     f32(rsum, d_model), b16(3, nc, fl, tc), b16(2, nc, fl // 2, tc), b16(3, nc, d_model, tc))
         vb = lambda *shape: pltpu.VMEM(shape, BF16)
         vf = lambda *shape: pltpu.VMEM(shape, F32)
         dma = lambda *shape: pltpu.SemaphoreType.DMA(shape)
-        seqb = nc * tc
         scratch = [
             vb(nm * qrows, d_model), vb(d_model, nm * orows), vb(nm * fl, d_model), vb(d_model, nm * fl),
             vb(nm * fl, d_model), vb(d_model, nm * fl), vb(nm * orows, d_model), vb(d_model, nm * qrows),
@@ -635,23 +727,38 @@
             vb(nc, nm * orows, tc), vb(nc, d_model, tc), vb(nc, d_model, tc), vb(nc, nm * fl, tc), vb(nc, nm * fl, tc),
             vb(nc * (nc + 1) // 2, heads, tc, tc), vb(nc, d_model, tc), vf(heads // 2, seqb, 2 * hd), vf(heads // 2, seqb, 2 * hd),
             vf(2 * seqb, tc), vb(nc, d_model, tc), vb(nm * orows, tc), vf(nm + 2, 8, 128), vf(8, tc),
-            vf(3, rsum, d_model), vf(256, d_model),
+            vf(3, rsum, d_model), vf(256, d_model), vf(fl, d_model), vb(2, fl + d_model, tc),
             dma(4, 4), dma(4, 4), dma(4), pltpu.SemaphoreType.REGULAR, dma(nc), dma(nc), dma(nc), dma(nc), dma(nc),
             dma(nm - 1), dma(nm - 1), pltpu.SemaphoreType.DMA, pltpu.SemaphoreType.DMA,
-            dma(4, 6), dma(4, 6), dma(1), dma(4),
+            dma(3, 6), dma(3, 6), dma(5), dma(4), dma(6, nc), dma(6, nc), dma(4, nc), dma(4, nc),
         ]
         res = pl.pallas_call(
             functools.partial(step_kernel, cfg),
             out_shape=out_shape,
             in_specs=[any_spec] * 6,
-            out_specs=[any_spec] * 4 + [pl.BlockSpec(memory_space=pltpu.VMEM)] + [any_spec] * 4,
+            out_specs=[any_spec, pl.BlockSpec(memory_space=pltpu.VMEM)] + [any_spec] * 7,
             scratch_shapes=scratch,
             compiler_params=pltpu.CompilerParams(collective_id=0, has_side_effects=True, vmem_limit_bytes=67043328),
             name="train_step",
         )(tokens_in, targets, wqT, wo, wu, wd)
-        g_qkv = jnp.transpose(res[0].reshape(hl, 3, hd, d_model), (3, 0, 1, 2))[None, None]
-        g_out = res[1].reshape(1, 1, hl, hd, d_model)
-        return g_qkv, g_out, res[2][None, None], res[3][None, None], res[4][0, :1]
+        part, loss, late = res[0], res[1], res[5]
+        steps = 4
+
+        def spec(size, start):
+            rows = size // steps
+            return pl.BlockSpec((rows, d_model), lambda i: (start // rows + i, 0))
+
+        q_s, o_s, u_s = spec(qrows, 0), spec(orows, qrows), spec(d_model, qrows + orows)
+        g_qkv, g_out, g_up, g_down, loss = pl.pallas_call(
+            finish_kernel,
+            grid=(steps,),
+            out_shape=(f32(qrows, d_model), f32(orows, d_model), f32(d_model, fl), f32(fl, d_model), f32(1)),
+            in_specs=[q_s, o_s, u_s, spec(fl, rsum), q_s, o_s, u_s, pl.BlockSpec(memory_space=pltpu.SMEM)],
+            out_specs=[spec(qrows, 0), spec(orows, 0), spec(d_model, 0), spec(fl, 0), pl.BlockSpec(memory_space=pltpu.SMEM)],
+            name="finish",
+        )(part, part, part, part, late, late, late, loss)
+        g_qkv = jnp.transpose(g_qkv.reshape(hl, 3, hd, d_model), (3, 0, 1, 2))[None, None]
+        return g_qkv, g_out.reshape(1, 1, hl, hd, d_model), g_up[None, None], g_down[None, None], loss
 
     tok_spec = P(None, "data", None)
     qkv_spec = P("stage", None, None, "model", None, None)

time: 338 us -> 336 us (level)
  local copies, waits for them, and re-layouts: 8.28 us -> 0 us
  Pallas kernels: 328 us -> 335 us
    unnamed x6 -> x0, local copies, waits for them, and re-layouts: 7 us -> none
    pallas_call x0 -> x1, Pallas kernels: none -> 4.7 us  [per_device(): pl.pallas_call(finish_kernel, grid=(steps,), out_shape=(f32(qrows, d_mode...]
where the time goes in v4:
time: 336 us; the launch traced here: 335 us
  Pallas kernels  335 us (100%)
    pallas_call x1, Pallas kernels, per_device(): pl.pallas_call(functools.partial(step_kernel, cfg), out_shape=out_shape,...  330 us

profile of v4, /device:TPU:96, one launch (start us, length us, event | category | flops | bytes accessed | tf_op | source)
XLA Modules:
  0.0 335.4 jit_solution(7151078621516447556)
XLA Ops:
  0.6 329.9 %train_step.1 = (f32[1536,512]{1,0:T(8,128)}, f32[8,128]{1,0:T(8,128)}, f32[512,512]{1,0:T(8,128)}, f32[512,512]{1,0:T(8,128)}, f32[1024,512]{1,0:T(8,128)}, /*i...) custom-call(bf16[4,1024,512]{2,1,0:T(8,128)(2,1)} %x_hbm.1, ...), custom_call_target="tpu_custom_call" | custom-call | tf_op jit(solution)/shard_map/train_step/pallas_call | solution.py:735
  330.5 4.7 %finish.1 = (f32[384,512]{1,0:T(8,128)}, f32[128,512]{1,0:T(8,128)}, f32[512,512]{1,0:T(8,128)}, f32[512,512]{1,0:T(8,128)}, f32[1]{0:T(128)}) custom-call(f32[1536,512]{1,0:T(8,128)} %get-tuple-element.13.sq.so.su.sd, f32[1536,512]{1,0:T(8,128)} %get-tuple-element.13.sq.so.su.sd, f32[1536,512]{1,0:T(8,128)} %get-tuple-element.13.sq.so.su.sd, ...), custom_call_target="tpu_custom_call" | custom-call | tf_op jit(solution)/shard_map/finish/pallas_call | solution.py:752

commit v5 on v4

--- a/solution.py
+++ b/solution.py
@@ -406,8 +406,6 @@
             u = dot(wuT[rows, :], n2buf[c]).astype(BF16)
             ubuf[c, rows, :] = u
             zbuf[c, rows, :] = gelu(u.astype(F32)).astype(BF16)
-        for way in range(4):
-            z_copy(c, way).start()
         acc = dot(wdT[...], zbuf[c])
         y32 = (mbuf[c].astype(F32) + acc.astype(BF16).astype(F32)).astype(BF16)
         ybuf[c] = y32
@@ -451,9 +449,23 @@
         def _():
             mlp_step(c)
 
+    def z_start():
+        for c in range(nc):
+            for way in range(4):
+                z_copy(c, way).start()
+
+    z_last = st >= ns - 2
+
+    @pl.when(jnp.logical_not(z_last))
+    def _():
+        z_start()
+
     @pl.when(jnp.logical_not(late))
     def _():
         natural_weights()
+
+    @pl.when(jnp.logical_not(z_last))
+    def _():
         for c in range(nc):
             z_forward(c)
 
@@ -473,8 +485,6 @@
         losst[nm] = jnp.full(losst.shape[1:], tot, F32)
         for k in range(1, nm):
             l_copy(k).start()
-
-    delay = jnp.where(late, 2, 1)
 
     @pl.loop(0, nc)
     def _(i):
@@ -517,18 +527,15 @@
         def _():
             b_copy(c).start()
 
-        @pl.when(late)
-        def _():
-            z_forward(i)
-
-        @pl.when(c + delay < nc)
-        def _():
-            dy_forward(c + delay)
-
-    for c in range(2):
-        @pl.when(c < delay)
-        def _():
-            dy_forward(c)
+        @pl.when(i > 0)
+        def _():
+            dy_forward(c + 1)
+
+    dy_forward(0)
+
+    @pl.when(z_last)
+    def _():
+        z_start()
 
     @pl.when(last)
     def _():
@@ -618,6 +625,11 @@
         slot, c = n // nc, lax.rem(n, nc)
         return (pltpu.make_async_copy(z_recv.at[slot, c], zdy.at[buf, pl.ds(0, fl)], ld_sem.at[1 + buf]),
                 pltpu.make_async_copy(dy_recv.at[slot, c], zdy.at[buf, pl.ds(fl, dm_)], ld_sem.at[3 + buf]))
+
+    @pl.when(z_last)
+    def _():
+        for c in range(nc):
+            z_forward(c)
 
     gdacc[...] = wgrad(3, me)
     for c in range(nc):

time: 336 us -> 324 us (0.964)
  Pallas kernels: 335 us -> 323 us
    pallas_call x1, Pallas kernels: 330 us -> 318 us  [per_device(): pl.pallas_call(functools.partial(step_kernel, cfg), out_shape=out_shape,...]
where the time goes in v5:
time: 324 us
  Pallas kernels  323 us (100%)
    pallas_call x1, Pallas kernels, per_device(): pl.pallas_call(functools.partial(step_kernel, cfg), out_shape=out_shape,...  318 us

profile of v5, /device:TPU:96, one launch (start us, length us, event | category | flops | bytes accessed | tf_op | source)
XLA Modules:
  0.0 323.6 jit_solution(11994654507271458438)
XLA Ops:
  0.6 318.1 %train_step.1 = (f32[1536,512]{1,0:T(8,128)}, f32[8,128]{1,0:T(8,128)}, f32[512,512]{1,0:T(8,128)}, f32[512,512]{1,0:T(8,128)}, f32[1024,512]{1,0:T(8,128)}, /*i...) custom-call(bf16[4,1024,512]{2,1,0:T(8,128)(2,1)} %x_hbm.1, ...), custom_call_target="tpu_custom_call" | custom-call | tf_op jit(solution)/shard_map/train_step/pallas_call | solution.py:747
  318.7 4.7 %finish.1 = (f32[384,512]{1,0:T(8,128)}, f32[128,512]{1,0:T(8,128)}, f32[512,512]{1,0:T(8,128)}, f32[512,512]{1,0:T(8,128)}, f32[1]{0:T(128)}) custom-call(f32[1536,512]{1,0:T(8,128)} %get-tuple-element.13.sq.so.su.sd, f32[1536,512]{1,0:T(8,128)} %get-tuple-element.13.sq.so.su.sd, f32[1536,512]{1,0:T(8,128)} %get-tuple-element.13.sq.so.su.sd, ...), custom_call_target="tpu_custom_call" | custom-call | tf_op jit(solution)/shard_map/finish/pallas_call | solution.py:764

commit v6 on v5

--- a/solution.py
+++ b/solution.py
@@ -463,9 +463,6 @@
     @pl.when(jnp.logical_not(late))
     def _():
         natural_weights()
-
-    @pl.when(jnp.logical_not(z_last))
-    def _():
         for c in range(nc):
             z_forward(c)
 
@@ -532,10 +529,6 @@
             dy_forward(c + 1)
 
     dy_forward(0)
-
-    @pl.when(z_last)
-    def _():
-        z_start()
 
     @pl.when(last)
     def _():
@@ -603,6 +596,10 @@
             stage_buf[1 + side, rows_of(mat)] = wgrad(mat, peer((plus, minus)[side]))
             near_copy(mat, side, 1 - side).start()
 
+    @pl.when(z_last)
+    def _():
+        z_start()
+
     def load(src, nr):
         return pltpu.make_async_copy(src, radd.at[pl.ds(0, nr)], ld_sem.at[0])
 
@@ -626,7 +623,7 @@
         return (pltpu.make_async_copy(z_recv.at[slot, c], zdy.at[buf, pl.ds(0, fl)], ld_sem.at[1 + buf]),
                 pltpu.make_async_copy(dy_recv.at[slot, c], zdy.at[buf, pl.ds(fl, dm_)], ld_sem.at[3 + buf]))
 
-    @pl.when(z_last)
+    @pl.when(late)
     def _():
         for c in range(nc):
             z_forward(c)

time: 324 us -> 324 us (level)
  no operation moved by 1% of the time
where the time goes in v6:
time: 324 us
  Pallas kernels  323 us (100%)
    pallas_call x1, Pallas kernels, per_device(): pl.pallas_call(functools.partial(step_kernel, cfg), out_shape=out_shape,...  318 us

profile of v6, /device:TPU:96, one launch (start us, length us, event | category | flops | bytes accessed | tf_op | source)
XLA Modules:
  0.0 323.6 jit_solution(17591691163902080650)
XLA Ops:
  0.6 318.1 %train_step.1 = (f32[1536,512]{1,0:T(8,128)}, f32[8,128]{1,0:T(8,128)}, f32[512,512]{1,0:T(8,128)}, f32[512,512]{1,0:T(8,128)}, f32[1024,512]{1,0:T(8,128)}, /*i...) custom-call(bf16[4,1024,512]{2,1,0:T(8,128)(2,1)} %x_hbm.1, ...), custom_call_target="tpu_custom_call" | custom-call | tf_op jit(solution)/shard_map/train_step/pallas_call | solution.py:744
  318.7 4.7 %finish.1 = (f32[384,512]{1,0:T(8,128)}, f32[128,512]{1,0:T(8,128)}, f32[512,512]{1,0:T(8,128)}, f32[512,512]{1,0:T(8,128)}, f32[1]{0:T(128)}) custom-call(f32[1536,512]{1,0:T(8,128)} %get-tuple-element.13.sq.so.su.sd, f32[1536,512]{1,0:T(8,128)} %get-tuple-element.13.sq.so.su.sd, f32[1536,512]{1,0:T(8,128)} %get-tuple-element.13.sq.so.su.sd, ...), custom_call_target="tpu_custom_call" | custom-call | tf_op jit(solution)/shard_map/finish/pallas_call | solution.py:761

commit v7 on v6

--- a/solution.py
+++ b/solution.py
@@ -172,10 +172,9 @@
     w_forward(W_O)
     w_own(W_D)
 
-    def pass_go():
-        @pl.when(jnp.logical_not(odd))
-        def _():
-            pl.semaphore_signal(go_sem, inc=1, device_id={"stage": nxt}, device_id_type=MESH)
+    @pl.when(jnp.logical_not(odd))
+    def _():
+        pl.semaphore_signal(go_sem, inc=1, device_id={"stage": nxt}, device_id_type=MESH)
 
     def natural_weights():
         @pl.loop(0, nm)
@@ -191,7 +190,6 @@
     def _():
         w_forward(W_U)
         w_forward(W_D)
-        pass_go()
         for idx in range(4):
             w_wait(idx)
 
@@ -426,14 +424,13 @@
         attn_turn = jnp.where(early, jnp.where(n < nc, 1, 0), 1 - lax.rem(n, 2))
         c = jnp.where(early, lax.rem(n, nc), n // 2)
 
+        @pl.when(early & (n == 1))
+        def _():
+            w_forward(W_U)
+
         @pl.when(early & (n == 2))
         def _():
-            w_forward(W_U)
-
-        @pl.when(early & (n == min(3, nc)))
-        def _():
             w_forward(W_D)
-            pass_go()
 
         @pl.when(attn_turn == 1)
         def _():

time: 324 us -> 320 us (0.988)
  Pallas kernels: 323 us -> 319 us
    pallas_call x1, Pallas kernels: 318 us -> 314 us  [per_device(): pl.pallas_call(functools.partial(step_kernel, cfg), out_shape=out_shape,...]
where the time goes in v7:
time: 320 us; the launch traced here: 319 us
  Pallas kernels  319 us (100%)
    pallas_call x1, Pallas kernels, per_device(): pl.pallas_call(functools.partial(step_kernel, cfg), out_shape=out_shape,...  314 us

profile of v7, /device:TPU:96, one launch (start us, length us, event | category | flops | bytes accessed | tf_op | source)
XLA Modules:
  0.0 319.4 jit_solution(12538219982683851797)
XLA Ops:
  0.6 313.9 %train_step.1 = (f32[1536,512]{1,0:T(8,128)}, f32[8,128]{1,0:T(8,128)}, f32[512,512]{1,0:T(8,128)}, f32[512,512]{1,0:T(8,128)}, f32[1024,512]{1,0:T(8,128)}, /*i...) custom-call(bf16[4,1024,512]{2,1,0:T(8,128)(2,1)} %x_hbm.1, ...), custom_call_target="tpu_custom_call" | custom-call | tf_op jit(solution)/shard_map/train_step/pallas_call | solution.py:741
  314.6 4.7 %finish.1 = (f32[384,512]{1,0:T(8,128)}, f32[128,512]{1,0:T(8,128)}, f32[512,512]{1,0:T(8,128)}, f32[512,512]{1,0:T(8,128)}, f32[1]{0:T(128)}) custom-call(f32[1536,512]{1,0:T(8,128)} %get-tuple-element.13.sq.so.su.sd, f32[1536,512]{1,0:T(8,128)} %get-tuple-element.13.sq.so.su.sd, f32[1536,512]{1,0:T(8,128)} %get-tuple-element.13.sq.so.su.sd, ...), custom_call_target="tpu_custom_call" | custom-call | tf_op jit(solution)/shard_map/finish/pallas_call | solution.py:758

commit v8 on v7

--- a/solution.py
+++ b/solution.py
@@ -50,12 +50,12 @@
 
 
 def step_kernel(cfg, x_hbm, t_hbm, wqT_in, wo_in, wu_in, wd_in,
-                sum_out, loss_out, far_p, far_m, near_e, near_l, z_recv, z_fwd, dy_recv,
+                sum_out, loss_out, far_p, far_m, near_e, near_l, z_recv, z_fwd, dy_recv, gd_far, gd_near,
                 wqT, woT, wuT, wdT, wd, wu, wo, wq,
                 xin, hbuf, n1buf, qkv, qkvn, obuf, mbuf, n2buf, ubuf, zbuf, pbuf, dybuf, dvacc, dkacc, sscr,
                 ybuf, dobuf, losst, lossv, stage_buf, radd, gdacc, zdy,
                 ag_send, ag_recv, ag_loc, go_sem, xsem, fsend, frecv, bsend, brecv, lsend, lrecv, lfsend, lfrecv,
-                rs_send, rs_recv, ld_sem, out_sem, z_send, z_arr, dy_send, dy_arr):
+                rs_send, rs_recv, ld_sem, out_sem, z_send, z_arr, dy_send, dy_arr, gd_send, gd_recv):
     ns, nm, nc, tc, dm_, hl, hd, fl = cfg
     heads = nm * hl
     qrows = hl * 3 * hd
@@ -451,14 +451,9 @@
             for way in range(4):
                 z_copy(c, way).start()
 
-    z_last = st >= ns - 2
-
-    @pl.when(jnp.logical_not(z_last))
+    @pl.when(jnp.logical_not(late))
     def _():
         z_start()
-
-    @pl.when(jnp.logical_not(late))
-    def _():
         natural_weights()
         for c in range(nc):
             z_forward(c)
@@ -488,8 +483,10 @@
         def _():
             b_copy(c).wait_recv()
 
-        for way in range(2):
-            dy_copy(c, way).start()
+        @pl.when(jnp.logical_not(late))
+        def _():
+            for way in range(2):
+                dy_copy(c, way).start()
 
         blk = fl // 4
         for f in range(4 * nm):
@@ -521,11 +518,13 @@
         def _():
             b_copy(c).start()
 
-        @pl.when(i > 0)
+        @pl.when(jnp.logical_not(late) & (i > 0))
         def _():
             dy_forward(c + 1)
 
-    dy_forward(0)
+    @pl.when(jnp.logical_not(late))
+    def _():
+        dy_forward(0)
 
     @pl.when(last)
     def _():
@@ -593,12 +592,46 @@
             stage_buf[1 + side, rows_of(mat)] = wgrad(mat, peer((plus, minus)[side]))
             near_copy(mat, side, 1 - side).start()
 
-    @pl.when(z_last)
-    def _():
-        z_start()
+    hd2 = dm_ // 2
+
+    def gd_cols(half):
+        return pl.ds(half * hd2, hd2)
+
+    def gd_half(d, half):
+        return functools.reduce(jnp.add, [
+            dot_t(zbuf[c, rowsl(d * fl, fl, fl), :], dybuf[c, gd_cols(half), :]) for c in range(nc)])
+
+    def gd_far_copy(half):
+        return ring_copy(gdacc.at[:, gd_cols(half)], gd_far.at[half], gd_send.at[half], gd_recv.at[half], half)
+
+    def gd_slot(side, half):
+        return pl.ds((2 * side + half) * fl, fl)
+
+    def gd_near_copy(side, half):
+        way = 2 + 2 * side + half
+        return ring_copy(sscr.at[gd_slot(side, half)], gd_near.at[1 if side == half else 0, half],
+                         gd_send.at[way], gd_recv.at[way], side)
+
+    @pl.when(late)
+    def _():
+        for half in range(2):
+            gdacc[:, gd_cols(half)] = gd_half(peer(far), half)
+            gd_far_copy(half).start()
+        for side in range(2):
+            for half in (1 - side, side):
+                sscr[gd_slot(side, half), :] = gd_half(peer((plus, minus)[side]), half)
+            gd_near_copy(side, 1 - side).start()
 
     def load(src, nr):
         return pltpu.make_async_copy(src, radd.at[pl.ds(0, nr)], ld_sem.at[0])
+
+    def gd_add(src, ref):
+        nr = min(fl, radd.shape[0])
+        for r in range(0, fl, nr):
+            copy = pltpu.make_async_copy(src.at[pl.ds(r, nr)], radd.at[pl.ds(0, nr), pl.ds(0, hd2)], ld_sem.at[0])
+            copy.start()
+            copy.wait()
+            ref[pl.ds(r, nr), :] += radd[pl.ds(0, nr), pl.ds(0, hd2)]
 
     for mat in mats:
         nr = sizes[mat] // 2
@@ -610,6 +643,14 @@
             stage_buf[1 + half, half_of(mat, half)] += radd[pl.ds(0, nr)]
             near_copy(mat, half, half).start()
 
+    @pl.when(late)
+    def _():
+        for half in range(2):
+            gd_far_copy(half).wait_recv()
+            gd_add(gd_far.at[half], sscr.at[gd_slot(half, half)])
+            gd_near_copy(half, half).start()
+            gd_far_copy(half).wait_send()
+
     for mat in mats:
         for half in range(2):
             far_copy(mat, half).wait_send()
@@ -620,32 +661,38 @@
         return (pltpu.make_async_copy(z_recv.at[slot, c], zdy.at[buf, pl.ds(0, fl)], ld_sem.at[1 + buf]),
                 pltpu.make_async_copy(dy_recv.at[slot, c], zdy.at[buf, pl.ds(fl, dm_)], ld_sem.at[3 + buf]))
 
+    gdacc[...] = wgrad(3, me)
+
+    @pl.when(jnp.logical_not(late))
+    def _():
+        for c in range(nc):
+            for way in (0, 1, 4, 5):
+                z_copy(c, way).wait_recv()
+            for way in (2, 3):
+                dy_copy(c, way).wait_recv()
+        for cp in zdy_load(0, 0):
+            cp.start()
+
+        @pl.loop(0, 3 * nc)
+        def _(n):
+            buf = lax.rem(n, 2)
+
+            @pl.when(n + 1 < 3 * nc)
+            def _():
+                for cp in zdy_load(n + 1, 1 - buf):
+                    cp.start()
+
+            for cp in zdy_load(n, buf):
+                cp.wait()
+            gdacc[...] += dot_t(zdy[buf, pl.ds(0, fl), :], zdy[buf, pl.ds(fl, dm_), :])
+
     @pl.when(late)
     def _():
-        for c in range(nc):
-            z_forward(c)
-
-    gdacc[...] = wgrad(3, me)
-    for c in range(nc):
-        for way in (0, 1, 4, 5):
-            z_copy(c, way).wait_recv()
-        for way in (2, 3):
-            dy_copy(c, way).wait_recv()
-    for cp in zdy_load(0, 0):
-        cp.start()
-
-    @pl.loop(0, 3 * nc)
-    def _(n):
-        buf = lax.rem(n, 2)
-
-        @pl.when(n + 1 < 3 * nc)
-        def _():
-            for cp in zdy_load(n + 1, 1 - buf):
-                cp.start()
-
-        for cp in zdy_load(n, buf):
-            cp.wait()
-        gdacc[...] += dot_t(zdy[buf, pl.ds(0, fl), :], zdy[buf, pl.ds(fl, dm_), :])
+        for last_half in range(2):
+            for half in range(2):
+                side = half if last_half else 1 - half
+                gd_near_copy(side, half).wait_recv()
+                gd_add(gd_near.at[last_half, half], gdacc.at[:, gd_cols(half)])
 
     def out_copy(mat):
         if mat == 3:
@@ -667,11 +714,21 @@
 
     for mat in range(4):
         out_copy(mat).wait()
-    for c in range(nc):
-        for way in range(6):
-            z_copy(c, way).wait_send()
-        for way in range(4):
-            dy_copy(c, way).wait_send()
+
+    @pl.when(jnp.logical_not(late))
+    def _():
+        for c in range(nc):
+            for way in range(6):
+                z_copy(c, way).wait_send()
+            for way in range(4):
+                dy_copy(c, way).wait_send()
+
+    @pl.when(late)
+    def _():
+        for side in range(2):
+            for half in range(2):
+                gd_near_copy(side, half).wait_send()
+
     for idx in range(4):
         for way in range(4):
             w_copy(idx, way).wait_send()
@@ -709,7 +766,7 @@
         hl, hd, fl = w_qkv.shape[3], w_qkv.shape[5], w_up.shape[3]
         tc = min(CHUNK, seq_len // 2)
         nc = seq_len // tc
-        assert n_micro == nm == 4 and w_qkv.shape[1] == 1 and hl == 2
+        assert n_micro == nm == 4 and w_qkv.shape[1] == 1 and hl == 2 and d_model == 2 * tc
         qrows, orows = hl * 3 * hd, hl * hd
         wqT = jnp.transpose(w_qkv[0, 0], (1, 2, 3, 0)).reshape(qrows, d_model)
         wo = w_out[0, 0].reshape(orows, d_model)
@@ -722,7 +779,8 @@
         seqb = nc * tc
         b16 = lambda *shape: jax.ShapeDtypeStruct(shape, BF16)
         out_shape = (f32(rsum + fl, d_model), f32(8, 128), f32(rsum // 2, d_model), f32(rsum // 2, d_model), f32(rsum, d_model),
-                     f32(rsum, d_model), b16(3, nc, fl, tc), b16(2, nc, fl // 2, tc), b16(3, nc, d_model, tc))
+                     f32(rsum, d_model), b16(3, nc, fl, tc), b16(2, nc, fl // 2, tc), b16(3, nc, d_model, tc),
+                     f32(2, fl, d_model // 2), f32(2, 2, fl, d_model // 2))
         vb = lambda *shape: pltpu.VMEM(shape, BF16)
         vf = lambda *shape: pltpu.VMEM(shape, F32)
         dma = lambda *shape: pltpu.SemaphoreType.DMA(shape)
@@ -732,17 +790,17 @@
             vb(nc, tc, d_model), vb(nc, d_model, tc), vb(nc, d_model, tc), vb(nc, nm * qrows, tc), vb(nm, seqb, qrows),
             vb(nc, nm * orows, tc), vb(nc, d_model, tc), vb(nc, d_model, tc), vb(nc, nm * fl, tc), vb(nc, nm * fl, tc),
             vb(nc * (nc + 1) // 2, heads, tc, tc), vb(nc, d_model, tc), vf(heads // 2, seqb, 2 * hd), vf(heads // 2, seqb, 2 * hd),
-            vf(2 * seqb, tc), vb(nc, d_model, tc), vb(nm * orows, tc), vf(nm + 2, 8, 128), vf(8, tc),
+            vf(max(2 * seqb, 4 * fl), tc), vb(nc, d_model, tc), vb(nm * orows, tc), vf(nm + 2, 8, 128), vf(8, tc),
             vf(3, rsum, d_model), vf(256, d_model), vf(fl, d_model), vb(2, fl + d_model, tc),
             dma(4, 4), dma(4, 4), dma(4), pltpu.SemaphoreType.REGULAR, dma(nc), dma(nc), dma(nc), dma(nc), dma(nc),
             dma(nm - 1), dma(nm - 1), pltpu.SemaphoreType.DMA, pltpu.SemaphoreType.DMA,
-            dma(3, 6), dma(3, 6), dma(5), dma(4), dma(6, nc), dma(6, nc), dma(4, nc), dma(4, nc),
+            dma(3, 6), dma(3, 6), dma(5), dma(4), dma(6, nc), dma(6, nc), dma(4, nc), dma(4, nc), dma(6), dma(6),
         ]
         res = pl.pallas_call(
             functools.partial(step_kernel, cfg),
             out_shape=out_shape,
             in_specs=[any_spec] * 6,
-            out_specs=[any_spec, pl.BlockSpec(memory_space=pltpu.VMEM)] + [any_spec] * 7,
+            out_specs=[any_spec, pl.BlockSpec(memory_space=pltpu.VMEM)] + [any_spec] * 9,
             scratch_shapes=scratch,
             compiler_params=pltpu.CompilerParams(collective_id=0, has_side_effects=True, vmem_limit_bytes=67043328),
             name="train_step",

time: 320 us -> 320 us (level)
  no operation moved by 1% of the time
where the time goes in v8:
time: 320 us; the launch traced here: 319 us
  Pallas kernels  319 us (100%)
    pallas_call x1, Pallas kernels, per_device(): pl.pallas_call(functools.partial(step_kernel, cfg), out_shape=out_shape,...  314 us

profile of v8, /device:TPU:96, one launch (start us, length us, event | category | flops | bytes accessed | tf_op | source)
XLA Modules:
  0.0 319.4 jit_solution(8027565905917259808)
XLA Ops:
  0.6 313.9 %train_step.1 = (f32[1536,512]{1,0:T(8,128)}, f32[8,128]{1,0:T(8,128)}, f32[512,512]{1,0:T(8,128)}, f32[512,512]{1,0:T(8,128)}, f32[1024,512]{1,0:T(8,128)}, /*i...) custom-call(bf16[4,1024,512]{2,1,0:T(8,128)(2,1)} %x_hbm.1, ...), custom_call_target="tpu_custom_call" | custom-call | tf_op jit(solution)/shard_map/train_step/pallas_call | solution.py:799
  314.5 4.7 %finish.1 = (f32[384,512]{1,0:T(8,128)}, f32[128,512]{1,0:T(8,128)}, f32[512,512]{1,0:T(8,128)}, f32[512,512]{1,0:T(8,128)}, f32[1]{0:T(128)}) custom-call(f32[1536,512]{1,0:T(8,128)} %get-tuple-element.13.sq.so.su.sd, f32[1536,512]{1,0:T(8,128)} %get-tuple-element.13.sq.so.su.sd, f32[1536,512]{1,0:T(8,128)} %get-tuple-element.13.sq.so.su.sd, ...), custom_call_target="tpu_custom_call" | custom-call | tf_op jit(solution)/shard_map/finish/pallas_call | solution.py:816

commit v9 on v8

--- a/solution.py
+++ b/solution.py
@@ -453,6 +453,8 @@
 
     @pl.when(jnp.logical_not(late))
     def _():
+        for c in range(nc):
+            f_copy(c).wait_send()
         z_start()
         natural_weights()
         for c in range(nc):
@@ -483,7 +485,7 @@
         def _():
             b_copy(c).wait_recv()
 
-        @pl.when(jnp.logical_not(late))
+        @pl.when(jnp.logical_not(late) & (i == 0))
         def _():
             for way in range(2):
                 dy_copy(c, way).start()
@@ -501,6 +503,15 @@
         mbuf[c] = dmid
         dobuf[...] = dot(wo[...], dmid).astype(BF16)
 
+        @pl.when(jnp.logical_not(late) & (i > 0))
+        def _():
+            for way in range(2):
+                dy_copy(c, way).start()
+
+        @pl.when(first & (i > 0))
+        def _():
+            dy_forward(c + 1)
+
         for cc in range(nc):
             pl.when(c == cc)(functools.partial(attention_grad, cc))
 
@@ -508,7 +519,7 @@
         h32 = hbuf[c].astype(F32)
         pull1 = norm_pull(h32, inv_rms(h32), dn1).astype(BF16)
 
-        @pl.when(jnp.logical_not(last))
+        @pl.when(late & jnp.logical_not(last))
         def _():
             f_copy(c).wait_send()
 
@@ -517,14 +528,6 @@
         @pl.when(jnp.logical_not(first))
         def _():
             b_copy(c).start()
-
-        @pl.when(jnp.logical_not(late) & (i > 0))
-        def _():
-            dy_forward(c + 1)
-
-    @pl.when(jnp.logical_not(late))
-    def _():
-        dy_forward(0)
 
     @pl.when(last)
     def _():
@@ -591,6 +594,15 @@
         for side in range(2):
             stage_buf[1 + side, rows_of(mat)] = wgrad(mat, peer((plus, minus)[side]))
             near_copy(mat, side, 1 - side).start()
+
+    @pl.when(first)
+    def _():
+        dy_forward(0)
+
+    @pl.when(jnp.logical_not(late | first))
+    def _():
+        for c in reversed(range(nc)):
+            dy_forward(c)
 
     hd2 = dm_ // 2
 

time: 320 us -> 323 us (level)
  no operation moved by 1% of the time
where the time goes in v9:
time: 323 us; the launch traced here: 322 us
  Pallas kernels  321 us (99%)
    pallas_call x1, Pallas kernels, per_device(): pl.pallas_call(functools.partial(step_kernel, cfg), out_shape=out_shape,...  316 us

profile of v9, /device:TPU:96, one launch (start us, length us, event | category | flops | bytes accessed | tf_op | source)
XLA Modules:
  0.0 321.9 jit_solution(12263799187145379364)
XLA Ops:
  0.6 316.4 %train_step.1 = (f32[1536,512]{1,0:T(8,128)}, f32[8,128]{1,0:T(8,128)}, f32[512,512]{1,0:T(8,128)}, f32[512,512]{1,0:T(8,128)}, f32[1024,512]{1,0:T(8,128)}, /*i...) custom-call(bf16[4,1024,512]{2,1,0:T(8,128)(2,1)} %x_hbm.1, ...), custom_call_target="tpu_custom_call" | custom-call | tf_op jit(solution)/shard_map/train_step/pallas_call | solution.py:811
  317.0 4.7 %finish.1 = (f32[384,512]{1,0:T(8,128)}, f32[128,512]{1,0:T(8,128)}, f32[512,512]{1,0:T(8,128)}, f32[512,512]{1,0:T(8,128)}, f32[1]{0:T(128)}) custom-call(f32[1536,512]{1,0:T(8,128)} %get-tuple-element.13.sq.so.su.sd, f32[1536,512]{1,0:T(8,128)} %get-tuple-element.13.sq.so.su.sd, f32[1536,512]{1,0:T(8,128)} %get-tuple-element.13.sq.so.su.sd, ...), custom_call_target="tpu_custom_call" | custom-call | tf_op jit(solution)/shard_map/finish/pallas_call | solution.py:828

commit v10 on v9

--- a/solution.py
+++ b/solution.py
@@ -52,8 +52,8 @@
 def step_kernel(cfg, x_hbm, t_hbm, wqT_in, wo_in, wu_in, wd_in,
                 sum_out, loss_out, far_p, far_m, near_e, near_l, z_recv, z_fwd, dy_recv, gd_far, gd_near,
                 wqT, woT, wuT, wdT, wd, wu, wo, wq,
-                xin, hbuf, n1buf, qkv, qkvn, obuf, mbuf, n2buf, ubuf, zbuf, pbuf, dybuf, dvacc, dkacc, sscr,
-                ybuf, dobuf, losst, lossv, stage_buf, radd, gdacc, zdy,
+                xin, hbuf, n1buf, qkv, kn, vn, obuf, mbuf, n2buf, ubuf, zbuf, pbuf, dybuf, dvacc, dkacc, sscr,
+                ybuf, dobuf, losst, lossv, stage_buf, radd, gdacc, dsbuf, qsave,
                 ag_send, ag_recv, ag_loc, go_sem, xsem, fsend, frecv, bsend, brecv, lsend, lrecv, lfsend, lfrecv,
                 rs_send, rs_recv, ld_sem, out_sem, z_send, z_arr, dy_send, dy_arr, gd_send, gd_recv):
     ns, nm, nc, tc, dm_, hl, hd, fl = cfg
@@ -248,15 +248,7 @@
     def head_rows(p, h, part):
         return pl.ds(p * (2 * 3 * hd) + (h * 3 + part) * hd, hd)
 
-    k_lane = (0, 2 * 2 * hd)
-    v_lane = (2 * hd, 2 * 2 * hd)
-    two = 2 * hd
-
-    def pad_k(val, h):
-        zero = jnp.zeros_like(val)
-        return jnp.concatenate([zero, val] if h == 0 else [val, zero], axis=0)
-
-    def pad_v(val, h):
+    def pad_head(val, h):
         zero = jnp.zeros_like(val)
         return jnp.concatenate([val, zero] if h == 0 else [zero, val], axis=0)
 
@@ -272,10 +264,10 @@
         def front(head):
             p, h = head // 2, head % 2
             base = (head % slots) * nk
-            qz = pad_k(qkv[cc, head_rows(p, h, 0), :], h)
+            qz = pad_head(qkv[cc, head_rows(p, h, 0), :], h)
             tops, sums = [], []
             for j in range(cc + 1):
-                s = dot(qkvn[p, pl.ds(j * tc, tc), pl.ds(k_lane[h], two)], qz)
+                s = dot(kn[p, pl.ds(j * tc, tc), :], qz)
                 for r in range(0, tc, sub):
                     part = s[r:r + sub]
                     if j == cc:
@@ -322,7 +314,7 @@
                 rows = pl.ds((p * 2 + h) * hd, hd)
                 do_t = dobuf[rows, :]
                 dsum = jnp.sum(do_t.astype(F32) * obuf[cc, rows, :].astype(F32), axis=0, keepdims=True)
-                held[p, h] = (pad_v(do_t, h), dsum)
+                held[p, h] = (pad_head(do_t, h), dsum)
             return held[p, h]
 
         def front(p, j):
@@ -330,31 +322,25 @@
             for h in range(2):
                 do_z, dsum = of_head(p, h)
                 pr = pbuf[cc * (cc + 1) // 2 + j, p * 2 + h]
-                dp = dot(qkvn[p, pl.ds(j * tc, tc), pl.ds(v_lane[h], two)], do_z).astype(BF16).astype(F32)
-                out.append((pr.astype(F32) * (dp - dsum)).astype(BF16))
+                dp = dot(vn[p, pl.ds(j * tc, tc), :], do_z).astype(BF16).astype(F32)
+                ds = (pr.astype(F32) * (dp - dsum)).astype(BF16)
+                if j < cc:
+                    dsbuf[p * 2 + h, pl.ds(j * tc, tc), :] = ds
+                out.append(ds)
             return out
 
         def back(p, j, ds):
-            dv_new = dk_new = None
             for h in range(2):
-                do_z, _ = of_head(p, h)
-                dv_h = dot_t(pbuf[cc * (cc + 1) // 2 + j, p * 2 + h], do_z)
-                dk_h = dot_t(ds[h], pad_v(qkv[cc, head_rows(p, h, 0), :], h))
-                dv_new = dv_h if dv_new is None else dv_new + dv_h
-                dk_new = dk_h if dk_new is None else dk_new + dk_h
                 dq_h = dot(qkv[j, head_rows(p, h, 1), :], ds[h])
                 dqs[p, h] = dq_h if j == 0 else dqs[p, h] + dq_h
-            rows = pl.ds(j * tc, tc)
-            if cc < nc - 1:
-                dv_new = dv_new + dvacc[p, rows, :]
-                dk_new = dk_new + dkacc[p, rows, :]
             if j < cc:
-                dvacc[p, rows, :] = dv_new
-                dkacc[p, rows, :] = dk_new
                 return
+            dv_new, dk_new = kv_grad(cc, p, j, [of_head(p, h)[0] for h in range(2)], ds,
+                                     [qkv[cc, head_rows(p, h, 0), :] for h in range(2)])
             dv_t = jnp.transpose(dv_new).astype(BF16)
             dk_t = (jnp.transpose(dk_new) * scale).astype(BF16)
             for h in range(2):
+                qsave[pl.ds((p * 2 + h) * hd, hd), :] = qkv[cc, head_rows(p, h, 0), :]
                 qkv[cc, head_rows(p, h, 0), :] = (dqs[p, h] * scale).astype(BF16)
                 qkv[cc, head_rows(p, h, 1), :] = dk_t[h * hd:(h + 1) * hd, :]
                 qkv[cc, head_rows(p, h, 2), :] = dv_t[h * hd:(h + 1) * hd, :]
@@ -364,6 +350,30 @@
             later = front(*units[n + 1]) if n + 1 < len(units) else None
             back(*unit, ds)
             ds = later
+
+    def kv_grad(cc, p, j, do_z, ds, q_t):
+        dv_new = dk_new = None
+        for h in range(2):
+            dv_h = dot_t(pbuf[cc * (cc + 1) // 2 + j, p * 2 + h], do_z[h])
+            dk_h = dot_t(ds[h], pad_head(q_t[h], h))
+            dv_new = dv_h if dv_new is None else dv_new + dv_h
+            dk_new = dk_h if dk_new is None else dk_new + dk_h
+        rows = pl.ds(j * tc, tc)
+        if cc < nc - 1:
+            dv_new = dv_new + dvacc[p, rows, :]
+            dk_new = dk_new + dkacc[p, rows, :]
+        return dv_new, dk_new
+
+    def earlier_keys(cc):
+        for p in range(heads // 2):
+            heads_of = [pl.ds((p * 2 + h) * hd, hd) for h in range(2)]
+            do_z = [pad_head(dobuf[heads_of[h], :], h) for h in range(2)]
+            q_t = [qsave[heads_of[h], :] for h in range(2)]
+            for j in range(cc):
+                rows = pl.ds(j * tc, tc)
+                dv_new, dk_new = kv_grad(cc, p, j, do_z, [dsbuf[p * 2 + h, rows, :] for h in range(2)], q_t)
+                dvacc[p, rows, :] = dv_new
+                dkacc[p, rows, :] = dk_new
 
     def attention_step(c):
         @pl.when(first)
@@ -386,7 +396,9 @@
             rows = pl.ds(r * qrows, qrows)
             blk = dot(wqT[rows, :], n1).astype(BF16)
             qkv[c, rows, :] = blk
-            qkvn[r, pl.ds(pl.multiple_of(c * tc, tc), tc), :] = jnp.transpose(blk)
+            for part, ref in ((1, kn), (2, vn)):
+                both = jnp.concatenate([blk[(3 * h + part) * hd:(3 * h + part + 1) * hd] for h in range(2)], axis=0)
+                ref[r, pl.ds(pl.multiple_of(c * tc, tc), tc), :] = jnp.transpose(both)
 
         for cc in range(nc):
             pl.when(c == cc)(functools.partial(attention, cc))
@@ -476,6 +488,8 @@
         losst[nm] = jnp.full(losst.shape[1:], tot, F32)
         for k in range(1, nm):
             l_copy(k).start()
+
+    dy_inside = jnp.logical_not(late) & (first | odd)
 
     @pl.loop(0, nc)
     def _(i):
@@ -508,7 +522,7 @@
             for way in range(2):
                 dy_copy(c, way).start()
 
-        @pl.when(first & (i > 0))
+        @pl.when(dy_inside & (i > 0))
         def _():
             dy_forward(c + 1)
 
@@ -528,6 +542,9 @@
         @pl.when(jnp.logical_not(first))
         def _():
             b_copy(c).start()
+
+        for cc in range(1, nc):
+            pl.when(c == cc)(functools.partial(earlier_keys, cc))
 
     @pl.when(last)
     def _():
@@ -595,11 +612,11 @@
             stage_buf[1 + side, rows_of(mat)] = wgrad(mat, peer((plus, minus)[side]))
             near_copy(mat, side, 1 - side).start()
 
-    @pl.when(first)
+    @pl.when(dy_inside)
     def _():
         dy_forward(0)
 
-    @pl.when(jnp.logical_not(late | first))
+    @pl.when(jnp.logical_not(late | dy_inside))
     def _():
         for c in reversed(range(nc)):
             dy_forward(c)
@@ -670,8 +687,8 @@
 
     def zdy_load(n, buf):
         slot, c = n // nc, lax.rem(n, nc)
-        return (pltpu.make_async_copy(z_recv.at[slot, c], zdy.at[buf, pl.ds(0, fl)], ld_sem.at[1 + buf]),
-                pltpu.make_async_copy(dy_recv.at[slot, c], zdy.at[buf, pl.ds(fl, dm_)], ld_sem.at[3 + buf]))
+        return (pltpu.make_async_copy(z_recv.at[slot, c], dsbuf.at[2 * buf, pl.ds(0, fl)], ld_sem.at[1 + buf]),
+                pltpu.make_async_copy(dy_recv.at[slot, c], dsbuf.at[2 * buf + 1, pl.ds(0, dm_)], ld_sem.at[3 + buf]))
 
     gdacc[...] = wgrad(3, me)
 
@@ -696,22 +713,19 @@
 
             for cp in zdy_load(n, buf):
                 cp.wait()
-            gdacc[...] += dot_t(zdy[buf, pl.ds(0, fl), :], zdy[buf, pl.ds(fl, dm_), :])
-
-    @pl.when(late)
-    def _():
-        for last_half in range(2):
-            for half in range(2):
-                side = half if last_half else 1 - half
-                gd_near_copy(side, half).wait_recv()
-                gd_add(gd_near.at[last_half, half], gdacc.at[:, gd_cols(half)])
+            gdacc[...] += dot_t(dsbuf[2 * buf, pl.ds(0, fl), :], dsbuf[2 * buf + 1, pl.ds(0, dm_), :])
+
+    def gd_arrivals(last_half):
+        for half in range(2):
+            side = half if last_half else 1 - half
+            gd_near_copy(side, half).wait_recv()
+            gd_add(gd_near.at[last_half, half], gdacc.at[:, gd_cols(half)])
 
     def out_copy(mat):
         if mat == 3:
             return pltpu.make_async_copy(gdacc, sum_out.at[pl.ds(qrows + orows + dm_, fl)], out_sem.at[3])
         return pltpu.make_async_copy(stage_buf.at[0, rows_of(mat)], sum_out.at[rows_of(mat)], out_sem.at[mat])
 
-    out_copy(3).start()
     for mat in mats:
         nr = sizes[mat] // 2
         for side in range(2):
@@ -720,6 +734,13 @@
             load(near_e.at[half_of(mat, 1 - side)], nr).wait()
             stage_buf[0, half_of(mat, 1 - side)] += radd[pl.ds(0, nr)]
         out_copy(mat).start()
+
+    @pl.when(late)
+    def _():
+        gd_arrivals(0)
+        gd_arrivals(1)
+
+    out_copy(3).start()
     for mat in mats:
         for side in range(2):
             near_copy(mat, side, side).wait_recv()
@@ -799,11 +820,11 @@
         scratch = [
             vb(nm * qrows, d_model), vb(d_model, nm * orows), vb(nm * fl, d_model), vb(d_model, nm * fl),
             vb(nm * fl, d_model), vb(d_model, nm * fl), vb(nm * orows, d_model), vb(d_model, nm * qrows),
-            vb(nc, tc, d_model), vb(nc, d_model, tc), vb(nc, d_model, tc), vb(nc, nm * qrows, tc), vb(nm, seqb, qrows),
+            vb(nc, tc, d_model), vb(nc, d_model, tc), vb(nc, d_model, tc), vb(nc, nm * qrows, tc), vb(nm, seqb, orows), vb(nm, seqb, orows),
             vb(nc, nm * orows, tc), vb(nc, d_model, tc), vb(nc, d_model, tc), vb(nc, nm * fl, tc), vb(nc, nm * fl, tc),
             vb(nc * (nc + 1) // 2, heads, tc, tc), vb(nc, d_model, tc), vf(heads // 2, seqb, 2 * hd), vf(heads // 2, seqb, 2 * hd),
             vf(max(2 * seqb, 4 * fl), tc), vb(nc, d_model, tc), vb(nm * orows, tc), vf(nm + 2, 8, 128), vf(8, tc),
-            vf(3, rsum, d_model), vf(256, d_model), vf(fl, d_model), vb(2, fl + d_model, tc),
+            vf(3, rsum, d_model), vf(256, d_model), vf(fl, d_model), vb(heads, max((nc - 1) * tc, fl), tc), vb(nm * orows, tc),
             dma(4, 4), dma(4, 4), dma(4), pltpu.SemaphoreType.REGULAR, dma(nc), dma(nc), dma(nc), dma(nc), dma(nc),
             dma(nm - 1), dma(nm - 1), pltpu.SemaphoreType.DMA, pltpu.SemaphoreType.DMA,
             dma(3, 6), dma(3, 6), dma(5), dma(4), dma(6, nc), dma(6, nc), dma(4, nc), dma(4, nc), dma(6), dma(6),

time: 323 us -> 317 us (0.981)
  Pallas kernels: 321 us -> 315 us
    pallas_call x1, Pallas kernels: 316 us -> 310 us  [per_device(): pl.pallas_call(functools.partial(step_kernel, cfg), out_shape=out_shape,...]
where the time goes in v10:
time: 317 us; the launch traced here: 316 us
  Pallas kernels  315 us (99%)
    pallas_call x1, Pallas kernels, per_device(): pl.pallas_call(functools.partial(step_kernel, cfg), out_shape=out_shape,...  310 us

profile of v10, /device:TPU:96, one launch (start us, length us, event | category | flops | bytes accessed | tf_op | source)
XLA Modules:
  0.0 315.6 jit_solution(597481666141479532)
XLA Ops:
  0.6 310.1 %train_step.1 = (f32[1536,512]{1,0:T(8,128)}, f32[8,128]{1,0:T(8,128)}, f32[512,512]{1,0:T(8,128)}, f32[512,512]{1,0:T(8,128)}, f32[1024,512]{1,0:T(8,128)}, /*i...) custom-call(bf16[4,1024,512]{2,1,0:T(8,128)(2,1)} %x_hbm.1, ...), custom_call_target="tpu_custom_call" | custom-call | tf_op jit(solution)/shard_map/train_step/pallas_call | solution.py:832
  310.8 4.7 %finish.1 = (f32[384,512]{1,0:T(8,128)}, f32[128,512]{1,0:T(8,128)}, f32[512,512]{1,0:T(8,128)}, f32[512,512]{1,0:T(8,128)}, f32[1]{0:T(128)}) custom-call(f32[1536,512]{1,0:T(8,128)} %get-tuple-element.13.sq.so.su.sd, f32[1536,512]{1,0:T(8,128)} %get-tuple-element.13.sq.so.su.sd, f32[1536,512]{1,0:T(8,128)} %get-tuple-element.13.sq.so.su.sd, ...), custom_call_target="tpu_custom_call" | custom-call | tf_op jit(solution)/shard_map/finish/pallas_call | solution.py:849

commit v11 on v10

--- a/solution.py
+++ b/solution.py
@@ -602,25 +602,6 @@
         return ring_copy(stage_buf.at[1 + side, half_of(mat, half)], (near_l if side == half else near_e).at[half_of(mat, half)],
                          rs_send.at[mat, way], rs_recv.at[mat, way], side)
 
-    mats = (2, 0, 1)
-    for mat in mats:
-        stage_buf[0, rows_of(mat)] = wgrad(mat, peer(far))
-        for half in range(2):
-            far_copy(mat, half).start()
-    for mat in mats:
-        for side in range(2):
-            stage_buf[1 + side, rows_of(mat)] = wgrad(mat, peer((plus, minus)[side]))
-            near_copy(mat, side, 1 - side).start()
-
-    @pl.when(dy_inside)
-    def _():
-        dy_forward(0)
-
-    @pl.when(jnp.logical_not(late | dy_inside))
-    def _():
-        for c in reversed(range(nc)):
-            dy_forward(c)
-
     hd2 = dm_ // 2
 
     def gd_cols(half):
@@ -640,16 +621,6 @@
         way = 2 + 2 * side + half
         return ring_copy(sscr.at[gd_slot(side, half)], gd_near.at[1 if side == half else 0, half],
                          gd_send.at[way], gd_recv.at[way], side)
-
-    @pl.when(late)
-    def _():
-        for half in range(2):
-            gdacc[:, gd_cols(half)] = gd_half(peer(far), half)
-            gd_far_copy(half).start()
-        for side in range(2):
-            for half in (1 - side, side):
-                sscr[gd_slot(side, half), :] = gd_half(peer((plus, minus)[side]), half)
-            gd_near_copy(side, 1 - side).start()
 
     def load(src, nr):
         return pltpu.make_async_copy(src, radd.at[pl.ds(0, nr)], ld_sem.at[0])
@@ -661,6 +632,28 @@
             copy.start()
             copy.wait()
             ref[pl.ds(r, nr), :] += radd[pl.ds(0, nr), pl.ds(0, hd2)]
+
+    mats = (1, 0, 2)
+    for mat in mats:
+        stage_buf[0, rows_of(mat)] = wgrad(mat, peer(far))
+        for half in range(2):
+            far_copy(mat, half).start()
+
+    @pl.when(late)
+    def _():
+        for half in range(2):
+            gdacc[:, gd_cols(half)] = gd_half(peer(far), half)
+            gd_far_copy(half).start()
+
+    for mat in mats:
+        for side in range(2):
+            stage_buf[1 + side, rows_of(mat)] = wgrad(mat, peer((plus, minus)[side]))
+
+    @pl.when(late)
+    def _():
+        for side in range(2):
+            for half in range(2):
+                sscr[gd_slot(side, half), :] = gd_half(peer((plus, minus)[side]), half)
 
     for mat in mats:
         nr = sizes[mat] // 2
@@ -671,6 +664,8 @@
             load(src, nr).wait()
             stage_buf[1 + half, half_of(mat, half)] += radd[pl.ds(0, nr)]
             near_copy(mat, half, half).start()
+        for side in range(2):
+            near_copy(mat, side, 1 - side).start()
 
     @pl.when(late)
     def _():
@@ -678,7 +673,17 @@
             gd_far_copy(half).wait_recv()
             gd_add(gd_far.at[half], sscr.at[gd_slot(half, half)])
             gd_near_copy(half, half).start()
+            gd_near_copy(1 - half, half).start()
             gd_far_copy(half).wait_send()
+
+    @pl.when(dy_inside)
+    def _():
+        dy_forward(0)
+
+    @pl.when(jnp.logical_not(late | dy_inside))
+    def _():
+        for c in reversed(range(nc)):
+            dy_forward(c)
 
     for mat in mats:
         for half in range(2):

time: 317 us -> 333 us (1.050)
  Pallas kernels: 315 us -> 331 us
    pallas_call x1, Pallas kernels: 310 us -> 327 us  [per_device(): pl.pallas_call(functools.partial(step_kernel, cfg), out_shape=out_shape,...]
where the time goes in v11:
time: 333 us; the launch traced here: 332 us
  Pallas kernels  331 us (99%)
    pallas_call x1, Pallas kernels, per_device(): pl.pallas_call(functools.partial(step_kernel, cfg), out_shape=out_shape,...  327 us

profile of v11, /device:TPU:96, one launch (start us, length us, event | category | flops | bytes accessed | tf_op | source)
XLA Modules:
  0.0 332.2 jit_solution(18060683841082086463)
XLA Ops:
  0.6 326.7 %train_step.1 = (f32[1536,512]{1,0:T(8,128)}, f32[8,128]{1,0:T(8,128)}, f32[512,512]{1,0:T(8,128)}, f32[512,512]{1,0:T(8,128)}, f32[1024,512]{1,0:T(8,128)}, /*i...) custom-call(bf16[4,1024,512]{2,1,0:T(8,128)(2,1)} %x_hbm.1, ...), custom_call_target="tpu_custom_call" | custom-call | tf_op jit(solution)/shard_map/train_step/pallas_call | solution.py:837
  327.4 4.7 %finish.1 = (f32[384,512]{1,0:T(8,128)}, f32[128,512]{1,0:T(8,128)}, f32[512,512]{1,0:T(8,128)}, f32[512,512]{1,0:T(8,128)}, f32[1]{0:T(128)}) custom-call(f32[1536,512]{1,0:T(8,128)} %get-tuple-element.13.sq.so.su.sd, f32[1536,512]{1,0:T(8,128)} %get-tuple-element.13.sq.so.su.sd, f32[1536,512]{1,0:T(8,128)} %get-tuple-element.13.sq.so.su.sd, ...), custom_call_target="tpu_custom_call" | custom-call | tf_op jit(solution)/shard_map/finish/pallas_call | solution.py:854

commit v12 on v10

--- a/solution.py
+++ b/solution.py
@@ -55,7 +55,7 @@
                 xin, hbuf, n1buf, qkv, kn, vn, obuf, mbuf, n2buf, ubuf, zbuf, pbuf, dybuf, dvacc, dkacc, sscr,
                 ybuf, dobuf, losst, lossv, stage_buf, radd, gdacc, dsbuf, qsave,
                 ag_send, ag_recv, ag_loc, go_sem, xsem, fsend, frecv, bsend, brecv, lsend, lrecv, lfsend, lfrecv,
-                rs_send, rs_recv, ld_sem, out_sem, z_send, z_arr, dy_send, dy_arr, gd_send, gd_recv):
+                rs_send, rs_recv, ld_sem, out_sem, z_send, z_arr, dy_send, dy_arr, gd_send, gd_recv, pl_sem):
     ns, nm, nc, tc, dm_, hl, hd, fl = cfg
     heads = nm * hl
     qrows = hl * 3 * hd
@@ -164,13 +164,13 @@
     w_own(W_O)
     w_local(W_U).wait()
     wuT[rowsl(me * fl, fl, fl), :] = jnp.transpose(wu[:, rowsl(me * fl, fl, fl)])
-    w_local(W_Q).wait()
-    w_forward(W_Q)
     w_own(W_U)
     w_local(W_D).wait()
     wdT[:, rowsl(me * fl, fl, fl)] = jnp.transpose(wd[rowsl(me * fl, fl, fl), :])
+    w_own(W_D)
+    w_local(W_Q).wait()
+    w_forward(W_Q)
     w_forward(W_O)
-    w_own(W_D)
 
     @pl.when(jnp.logical_not(odd))
     def _():
@@ -651,9 +651,6 @@
                 sscr[gd_slot(side, half), :] = gd_half(peer((plus, minus)[side]), half)
             gd_near_copy(side, 1 - side).start()
 
-    def load(src, nr):
-        return pltpu.make_async_copy(src, radd.at[pl.ds(0, nr)], ld_sem.at[0])
-
     def gd_add(src, ref):
         nr = min(fl, radd.shape[0])
         for r in range(0, fl, nr):
@@ -662,15 +659,43 @@
             copy.wait()
             ref[pl.ds(r, nr), :] += radd[pl.ds(0, nr), pl.ds(0, hd2)]
 
-    for mat in mats:
+    pieces = [(mat, half) for mat in mats for half in range(2)]
+    cols = dvacc.shape[2]
+    n_cols = dm_ // cols
+
+    def piece_loads(n, kind):
+        mat, half = pieces[n]
         nr = sizes[mat] // 2
-        for half in range(2):
+        r0 = sum(sizes[m] // 2 for m, _ in pieces[:n])
+        src = near_e.at[half_of(mat, half)] if kind else (far_p, far_m)[half].at[pl.ds(offs[mat] // 2, nr)]
+        dst = dkacc if kind else dvacc
+        return [pltpu.make_async_copy(src.at[:, pl.ds(k * cols, cols)], dst.at[k, pl.ds(r0, nr), :], pl_sem.at[kind, n])
+                for k in range(n_cols)], dst, r0, nr
+
+    def piece_start(n, kind):
+        mat, half = pieces[n]
+        if kind:
+            near_copy(mat, 1 - half, half).wait_recv()
+        else:
             far_copy(mat, half).wait_recv()
-            src = (far_p, far_m)[half].at[pl.ds(offs[mat] // 2, nr)]
-            load(src, nr).start()
-            load(src, nr).wait()
-            stage_buf[1 + half, half_of(mat, half)] += radd[pl.ds(0, nr)]
-            near_copy(mat, half, half).start()
+        for copy in piece_loads(n, kind)[0]:
+            copy.start()
+
+    def piece_add(n, kind, slot):
+        mat, half = pieces[n]
+        copies, src, r0, nr = piece_loads(n, kind)
+        for copy in copies:
+            copy.wait()
+        rows = half_of(mat, half)
+        for k in range(n_cols):
+            stage_buf[slot, rows, pl.ds(k * cols, cols)] += src[k, pl.ds(r0, nr), :]
+
+    piece_start(0, 0)
+    for n, (mat, half) in enumerate(pieces):
+        if n + 1 < len(pieces):
+            piece_start(n + 1, 0)
+        piece_add(n, 0, 1 + half)
+        near_copy(mat, half, half).start()
 
     @pl.when(late)
     def _():
@@ -726,14 +751,13 @@
             return pltpu.make_async_copy(gdacc, sum_out.at[pl.ds(qrows + orows + dm_, fl)], out_sem.at[3])
         return pltpu.make_async_copy(stage_buf.at[0, rows_of(mat)], sum_out.at[rows_of(mat)], out_sem.at[mat])
 
-    for mat in mats:
-        nr = sizes[mat] // 2
-        for side in range(2):
-            near_copy(mat, side, 1 - side).wait_recv()
-            load(near_e.at[half_of(mat, 1 - side)], nr).start()
-            load(near_e.at[half_of(mat, 1 - side)], nr).wait()
-            stage_buf[0, half_of(mat, 1 - side)] += radd[pl.ds(0, nr)]
-        out_copy(mat).start()
+    piece_start(0, 1)
+    for n, (mat, half) in enumerate(pieces):
+        if n + 1 < len(pieces):
+            piece_start(n + 1, 1)
+        piece_add(n, 1, 0)
+        if half:
+            out_copy(mat).start()
 
     @pl.when(late)
     def _():
@@ -799,8 +823,8 @@
         hl, hd, fl = w_qkv.shape[3], w_qkv.shape[5], w_up.shape[3]
         tc = min(CHUNK, seq_len // 2)
         nc = seq_len // tc
-        assert n_micro == nm == 4 and w_qkv.shape[1] == 1 and hl == 2 and d_model == 2 * tc
         qrows, orows = hl * 3 * hd, hl * hd
+        assert n_micro == nm == 4 and w_qkv.shape[1] == 1 and hl == 2 and d_model == 2 * tc and qrows + orows + d_model <= seq_len
         wqT = jnp.transpose(w_qkv[0, 0], (1, 2, 3, 0)).reshape(qrows, d_model)
         wo = w_out[0, 0].reshape(orows, d_model)
         wu, wd = w_up[0, 0], w_down[0, 0]
@@ -827,7 +851,7 @@
             vf(3, rsum, d_model), vf(256, d_model), vf(fl, d_model), vb(heads, max((nc - 1) * tc, fl), tc), vb(nm * orows, tc),
             dma(4, 4), dma(4, 4), dma(4), pltpu.SemaphoreType.REGULAR, dma(nc), dma(nc), dma(nc), dma(nc), dma(nc),
             dma(nm - 1), dma(nm - 1), pltpu.SemaphoreType.DMA, pltpu.SemaphoreType.DMA,
-            dma(3, 6), dma(3, 6), dma(5), dma(4), dma(6, nc), dma(6, nc), dma(4, nc), dma(4, nc), dma(6), dma(6),
+            dma(3, 6), dma(3, 6), dma(5), dma(4), dma(6, nc), dma(6, nc), dma(4, nc), dma(4, nc), dma(6), dma(6), dma(2, 6),
         ]
         res = pl.pallas_call(
             functools.partial(step_kernel, cfg),

time: 317 us -> 315 us (level)
  no operation moved by 1% of the time
where the time goes in v12:
time: 315 us; the launch traced here: 314 us
  Pallas kernels  313 us (99%)
    pallas_call x1, Pallas kernels, per_device(): pl.pallas_call(functools.partial(step_kernel, cfg), out_shape=out_shape,...  309 us

profile of v12, /device:TPU:96, one launch (start us, length us, event | category | flops | bytes accessed | tf_op | source)
XLA Modules:
  0.0 314.1 jit_solution(11088143194816238649)
XLA Ops:
  0.6 308.6 %train_step.1 = (f32[1536,512]{1,0:T(8,128)}, f32[8,128]{1,0:T(8,128)}, f32[512,512]{1,0:T(8,128)}, f32[512,512]{1,0:T(8,128)}, f32[1024,512]{1,0:T(8,128)}, /*i...) custom-call(bf16[4,1024,512]{2,1,0:T(8,128)(2,1)} %x_hbm.1, ...), custom_call_target="tpu_custom_call" | custom-call | tf_op jit(solution)/shard_map/train_step/pallas_call | solution.py:856
  309.2 4.7 %finish.1 = (f32[384,512]{1,0:T(8,128)}, f32[128,512]{1,0:T(8,128)}, f32[512,512]{1,0:T(8,128)}, f32[512,512]{1,0:T(8,128)}, f32[1]{0:T(128)}) custom-call(f32[1536,512]{1,0:T(8,128)} %get-tuple-element.13.sq.so.su.sd, f32[1536,512]{1,0:T(8,128)} %get-tuple-element.13.sq.so.su.sd, f32[1536,512]{1,0:T(8,128)} %get-tuple-element.13.sq.so.su.sd, ...), custom_call_target="tpu_custom_call" | custom-call | tf_op jit(solution)/shard_map/finish/pallas_call | solution.py:873

commit v13 on v12

--- a/solution.py
+++ b/solution.py
@@ -52,7 +52,7 @@
 def step_kernel(cfg, x_hbm, t_hbm, wqT_in, wo_in, wu_in, wd_in,
                 sum_out, loss_out, far_p, far_m, near_e, near_l, z_recv, z_fwd, dy_recv, gd_far, gd_near,
                 wqT, woT, wuT, wdT, wd, wu, wo, wq,
-                xin, hbuf, n1buf, qkv, kn, vn, obuf, mbuf, n2buf, ubuf, zbuf, pbuf, dybuf, dvacc, dkacc, sscr,
+                xin, hbuf, n1buf, qkv, kn, vn, obuf, mbuf, n2buf, ubuf, zbuf, pbuf, dybuf, dvacc, dkacc,
                 ybuf, dobuf, losst, lossv, stage_buf, radd, gdacc, dsbuf, qsave,
                 ag_send, ag_recv, ag_loc, go_sem, xsem, fsend, frecv, bsend, brecv, lsend, lrecv, lfsend, lfrecv,
                 rs_send, rs_recv, ld_sem, out_sem, z_send, z_arr, dy_send, dy_arr, gd_send, gd_recv, pl_sem):
@@ -255,9 +255,20 @@
     def causal(shape, row0):
         return lax.broadcasted_iota(jnp.int32, shape, 0) + row0 <= lax.broadcasted_iota(jnp.int32, shape, 1)
 
+    n_st = stage_buf.shape[0]
+
+    def folded(slot, row, n):
+        fold = stage_buf.shape[1]
+        return stage_buf.at[slot, pl.ds(row % fold, n), pl.ds((row // fold) * tc, tc)]
+
+    def slope(c):
+        blk = fl // 2
+        for f in range(2 * nm):
+            folded(nc - 1 - c, f * blk, blk)[...] = gelu_grad(ubuf[c, pl.ds(f * blk, blk), :].astype(F32))
+
     def attention(cc):
         nk = (cc + 1) * tc
-        slots = min(heads, sscr.shape[0] // nk)
+        slots = min(heads, 2 * nc * tc // nk)
         ahead = min(4, slots - 1)
         sub = tc // 2
 
@@ -274,7 +285,7 @@
                         part = jnp.where(causal(part.shape, r), part, NEG)
                     top = jnp.max(part, axis=0, keepdims=True)
                     e = jnp.exp2((part - top) * exp_c)
-                    sscr[pl.ds(base + j * tc + r, sub), :] = e
+                    folded(n_st - 1, base + j * tc + r, sub)[...] = e
                     tops.append(top)
                     sums.append(jnp.sum(e, axis=0, keepdims=True))
             mx = functools.reduce(jnp.maximum, tops)
@@ -289,7 +300,7 @@
             for j in range(cc + 1):
                 parts = []
                 for i in range(2):
-                    pr = (sscr[pl.ds(base + j * tc + i * sub, sub), :] * factors[2 * j + i]).astype(BF16)
+                    pr = (folded(n_st - 1, base + j * tc + i * sub, sub)[...] * factors[2 * j + i]).astype(BF16)
                     pbuf[cc * (cc + 1) // 2 + j, head, pl.ds(i * sub, sub), :] = pr
                     parts.append(pr)
                 part = dot(qkv[j, head_rows(p, h, 2), :], jnp.concatenate(parts, axis=0))
@@ -431,6 +442,10 @@
             lossv[...] += jnp.sum((err * err).reshape(dm_ // 8, 8, tc), axis=0)
             dybuf[c] = (err * inv_d).astype(BF16)
 
+        @pl.when(last & (c > 0))
+        def _():
+            slope(c)
+
     @pl.loop(0, 2 * nc)
     def _(n):
         attn_turn = jnp.where(early, jnp.where(n < nc, 1, 0), 1 - lax.rem(n, 2))
@@ -463,14 +478,24 @@
             for way in range(4):
                 z_copy(c, way).start()
 
+    def slopes():
+        @pl.loop(0, nc)
+        def _(c):
+            slope(c)
+
     @pl.when(jnp.logical_not(late))
     def _():
         for c in range(nc):
             f_copy(c).wait_send()
         z_start()
         natural_weights()
+        slopes()
         for c in range(nc):
             z_forward(c)
+
+    @pl.when(late & jnp.logical_not(last))
+    def _():
+        slopes()
 
     def l_copy(k):
         return pltpu.make_async_remote_copy(
@@ -504,11 +529,15 @@
             for way in range(2):
                 dy_copy(c, way).start()
 
+        @pl.when(last & (c == 0))
+        def _():
+            slope(c)
+
         blk = fl // 4
         for f in range(4 * nm):
             rows = pl.ds(f * blk, blk)
             dz = dot(wd[rows, :], dybuf[c]).astype(BF16).astype(F32)
-            ubuf[c, rows, :] = (dz * gelu_grad(ubuf[c, rows, :].astype(F32))).astype(BF16)
+            ubuf[c, rows, :] = (dz * folded(i, f * blk, blk)[...]).astype(BF16)
         acc = dot(wu[...], ubuf[c])
         dn2 = acc.astype(BF16).astype(F32)
         m32 = mbuf[c].astype(F32)
@@ -634,11 +663,11 @@
         return ring_copy(gdacc.at[:, gd_cols(half)], gd_far.at[half], gd_send.at[half], gd_recv.at[half], half)
 
     def gd_slot(side, half):
-        return pl.ds((2 * side + half) * fl, fl)
+        return folded(n_st - 1, (2 * side + half) * fl, fl)
 
     def gd_near_copy(side, half):
         way = 2 + 2 * side + half
-        return ring_copy(sscr.at[gd_slot(side, half)], gd_near.at[1 if side == half else 0, half],
+        return ring_copy(gd_slot(side, half), gd_near.at[1 if side == half else 0, half],
                          gd_send.at[way], gd_recv.at[way], side)
 
     @pl.when(late)
@@ -648,7 +677,7 @@
             gd_far_copy(half).start()
         for side in range(2):
             for half in (1 - side, side):
-                sscr[gd_slot(side, half), :] = gd_half(peer((plus, minus)[side]), half)
+                gd_slot(side, half)[...] = gd_half(peer((plus, minus)[side]), half)
             gd_near_copy(side, 1 - side).start()
 
     def gd_add(src, ref):
@@ -701,7 +730,7 @@
     def _():
         for half in range(2):
             gd_far_copy(half).wait_recv()
-            gd_add(gd_far.at[half], sscr.at[gd_slot(half, half)])
+            gd_add(gd_far.at[half], gd_slot(half, half))
             gd_near_copy(half, half).start()
             gd_far_copy(half).wait_send()
 
@@ -824,7 +853,7 @@
         tc = min(CHUNK, seq_len // 2)
         nc = seq_len // tc
         qrows, orows = hl * 3 * hd, hl * hd
-        assert n_micro == nm == 4 and w_qkv.shape[1] == 1 and hl == 2 and d_model == 2 * tc and qrows + orows + d_model <= seq_len
+        assert n_micro == nm == 4 and w_qkv.shape[1] == 1 and hl == 2 and d_model == 2 * tc and qrows + orows + d_model == seq_len == 2 * fl and nc == 4
         wqT = jnp.transpose(w_qkv[0, 0], (1, 2, 3, 0)).reshape(qrows, d_model)
         wo = w_out[0, 0].reshape(orows, d_model)
         wu, wd = w_up[0, 0], w_down[0, 0]
@@ -847,8 +876,8 @@
             vb(nc, tc, d_model), vb(nc, d_model, tc), vb(nc, d_model, tc), vb(nc, nm * qrows, tc), vb(nm, seqb, orows), vb(nm, seqb, orows),
             vb(nc, nm * orows, tc), vb(nc, d_model, tc), vb(nc, d_model, tc), vb(nc, nm * fl, tc), vb(nc, nm * fl, tc),
             vb(nc * (nc + 1) // 2, heads, tc, tc), vb(nc, d_model, tc), vf(heads // 2, seqb, 2 * hd), vf(heads // 2, seqb, 2 * hd),
-            vf(max(2 * seqb, 4 * fl), tc), vb(nc, d_model, tc), vb(nm * orows, tc), vf(nm + 2, 8, 128), vf(8, tc),
-            vf(3, rsum, d_model), vf(256, d_model), vf(fl, d_model), vb(heads, max((nc - 1) * tc, fl), tc), vb(nm * orows, tc),
+            vb(nc, d_model, tc), vb(nm * orows, tc), vf(nm + 2, 8, 128), vf(8, tc),
+            vf(4, rsum, d_model), vf(256, d_model), vf(fl, d_model), vb(heads, max((nc - 1) * tc, fl), tc), vb(nm * orows, tc),
             dma(4, 4), dma(4, 4), dma(4), pltpu.SemaphoreType.REGULAR, dma(nc), dma(nc), dma(nc), dma(nc), dma(nc),
             dma(nm - 1), dma(nm - 1), pltpu.SemaphoreType.DMA, pltpu.SemaphoreType.DMA,
             dma(3, 6), dma(3, 6), dma(5), dma(4), dma(6, nc), dma(6, nc), dma(4, nc), dma(4, nc), dma(6), dma(6), dma(2, 6),

time: 315 us -> 327 us (1.038)
  Pallas kernels: 313 us -> 322 us
    pallas_call x1, Pallas kernels: 309 us -> 318 us  [per_device(): pl.pallas_call(functools.partial(step_kernel, cfg), out_shape=out_shape,...]
where the time goes in v13:
time: 327 us; the launch traced here: 323 us
  Pallas kernels  322 us (98%)
    pallas_call x1, Pallas kernels, per_device(): pl.pallas_call(functools.partial(step_kernel, cfg), out_shape=out_shape,...  318 us

profile of v13, /device:TPU:96, one launch (start us, length us, event | category | flops | bytes accessed | tf_op | source)
XLA Modules:
  0.0 323.5 jit_solution(13720357440978416726)
XLA Ops:
  0.6 317.7 %train_step.1 = (f32[1536,512]{1,0:T(8,128)}, f32[8,128]{1,0:T(8,128)}, f32[512,512]{1,0:T(8,128)}, f32[512,512]{1,0:T(8,128)}, f32[1024,512]{1,0:T(8,128)}, /*i...) custom-call(bf16[4,1024,512]{2,1,0:T(8,128)(2,1)} %x_hbm.1, ...), custom_call_target="tpu_custom_call" | custom-call | tf_op jit(solution)/shard_map/train_step/pallas_call | solution.py:885
  318.4 4.7 %finish.1 = (f32[384,512]{1,0:T(8,128)}, f32[128,512]{1,0:T(8,128)}, f32[512,512]{1,0:T(8,128)}, f32[512,512]{1,0:T(8,128)}, f32[1]{0:T(128)}) custom-call(f32[1536,512]{1,0:T(8,128)} %get-tuple-element.13.sq.so.su.sd, f32[1536,512]{1,0:T(8,128)} %get-tuple-element.13.sq.so.su.sd, f32[1536,512]{1,0:T(8,128)} %get-tuple-element.13.sq.so.su.sd, ...), custom_call_target="tpu_custom_call" | custom-call | tf_op jit(solution)/shard_map/finish/pallas_call | solution.py:902

commit v14 on v13

--- a/solution.py
+++ b/solution.py
@@ -262,9 +262,16 @@
         return stage_buf.at[slot, pl.ds(row % fold, n), pl.ds((row // fold) * tc, tc)]
 
     def slope(c):
-        blk = fl // 2
-        for f in range(2 * nm):
-            folded(nc - 1 - c, f * blk, blk)[...] = gelu_grad(ubuf[c, pl.ds(f * blk, blk), :].astype(F32))
+        blk = fl // 4
+        per = stage_buf.shape[1] // blk
+
+        @pl.loop(0, 4 * nm)
+        def _(f):
+            half = f // per
+            rows = pl.ds(pl.multiple_of((f - half * per) * blk, blk), blk)
+            cols = pl.ds(pl.multiple_of(half * tc, tc), tc)
+            u = ubuf[c, pl.ds(pl.multiple_of(f * blk, blk), blk), :].astype(F32)
+            stage_buf[nc - 1 - c, rows, cols] = gelu_grad(u)
 
     def attention(cc):
         nk = (cc + 1) * tc
@@ -478,24 +485,24 @@
             for way in range(4):
                 z_copy(c, way).start()
 
-    def slopes():
-        @pl.loop(0, nc)
-        def _(c):
-            slope(c)
-
     @pl.when(jnp.logical_not(late))
     def _():
         for c in range(nc):
             f_copy(c).wait_send()
         z_start()
         natural_weights()
-        slopes()
-        for c in range(nc):
+
+    @pl.when(jnp.logical_not(last))
+    def _():
+        @pl.loop(0, nc)
+        def _(c):
+            slope(c)
+
+    @pl.when(jnp.logical_not(late))
+    def _():
+        @pl.loop(0, nc)
+        def _(c):
             z_forward(c)
-
-    @pl.when(late & jnp.logical_not(last))
-    def _():
-        slopes()
 
     def l_copy(k):
         return pltpu.make_async_remote_copy(

time: 327 us -> 313 us (0.957)
  Pallas kernels: 322 us -> 311 us
    pallas_call x1, Pallas kernels: 318 us -> 306 us  [per_device(): pl.pallas_call(functools.partial(step_kernel, cfg), out_shape=out_shape,...]
where the time goes in v14:
time: 313 us; the launch traced here: 312 us
  Pallas kernels  311 us (99%)
    pallas_call x1, Pallas kernels, per_device(): pl.pallas_call(functools.partial(step_kernel, cfg), out_shape=out_shape,...  306 us

profile of v14, /device:TPU:96, one launch (start us, length us, event | category | flops | bytes accessed | tf_op | source)
XLA Modules:
  0.0 312.0 jit_solution(14229365248952756784)
XLA Ops:
  0.6 306.5 %train_step.1 = (f32[1536,512]{1,0:T(8,128)}, f32[8,128]{1,0:T(8,128)}, f32[512,512]{1,0:T(8,128)}, f32[512,512]{1,0:T(8,128)}, f32[1024,512]{1,0:T(8,128)}, /*i...) custom-call(bf16[4,1024,512]{2,1,0:T(8,128)(2,1)} %x_hbm.1, ...), custom_call_target="tpu_custom_call" | custom-call | tf_op jit(solution)/shard_map/train_step/pallas_call | solution.py:892
  307.1 4.7 %finish.1 = (f32[384,512]{1,0:T(8,128)}, f32[128,512]{1,0:T(8,128)}, f32[512,512]{1,0:T(8,128)}, f32[512,512]{1,0:T(8,128)}, f32[1]{0:T(128)}) custom-call(f32[1536,512]{1,0:T(8,128)} %get-tuple-element.13.sq.so.su.sd, f32[1536,512]{1,0:T(8,128)} %get-tuple-element.13.sq.so.su.sd, f32[1536,512]{1,0:T(8,128)} %get-tuple-element.13.sq.so.su.sd, ...), custom_call_target="tpu_custom_call" | custom-call | tf_op jit(solution)/shard_map/finish/pallas_call | solution.py:909

commit v15 on v14

--- a/solution.py
+++ b/solution.py
@@ -449,9 +449,6 @@
             lossv[...] += jnp.sum((err * err).reshape(dm_ // 8, 8, tc), axis=0)
             dybuf[c] = (err * inv_d).astype(BF16)
 
-        @pl.when(last & (c > 0))
-        def _():
-            slope(c)
 
     @pl.loop(0, 2 * nc)
     def _(n):
@@ -536,7 +533,7 @@
             for way in range(2):
                 dy_copy(c, way).start()
 
-        @pl.when(last & (c == 0))
+        @pl.when(last)
         def _():
             slope(c)
 
@@ -639,14 +636,22 @@
                          rs_send.at[mat, way], rs_recv.at[mat, way], side)
 
     mats = (2, 0, 1)
-    for mat in mats:
-        stage_buf[0, rows_of(mat)] = wgrad(mat, peer(far))
-        for half in range(2):
-            far_copy(mat, half).start()
-    for mat in mats:
-        for side in range(2):
-            stage_buf[1 + side, rows_of(mat)] = wgrad(mat, peer((plus, minus)[side]))
-            near_copy(mat, side, 1 - side).start()
+
+    @pl.loop(0, 3)
+    def _(slot):
+        who = lax.rem(me + jnp.where(slot == 0, far, jnp.where(slot == 1, plus, minus)), nm)
+        for mat in mats:
+            stage_buf[slot, rows_of(mat)] = wgrad(mat, who)
+
+            @pl.when(slot == 0)
+            def _():
+                for half in range(2):
+                    far_copy(mat, half).start()
+
+            for side in range(2):
+                @pl.when(slot == 1 + side)
+                def _():
+                    near_copy(mat, side, 1 - side).start()
 
     @pl.when(dy_inside)
     def _():
@@ -660,7 +665,7 @@
     hd2 = dm_ // 2
 
     def gd_cols(half):
-        return pl.ds(half * hd2, hd2)
+        return pl.ds(half * hd2, hd2) if isinstance(half, int) else pl.ds(pl.multiple_of(half * hd2, hd2), hd2)
 
     def gd_half(d, half):
         return functools.reduce(jnp.add, [
@@ -679,12 +684,20 @@
 
     @pl.when(late)
     def _():
+        @pl.loop(0, 2)
+        def _(half):
+            gdacc[:, gd_cols(half)] = gd_half(peer(far), half)
+
         for half in range(2):
-            gdacc[:, gd_cols(half)] = gd_half(peer(far), half)
             gd_far_copy(half).start()
+
+        @pl.loop(0, 4)
+        def _(n):
+            rows, cols = lax.rem(n, 2) * fl, (n // 2) * tc
+            stage_buf[n_st - 1, pl.ds(pl.multiple_of(rows, fl), fl), pl.ds(pl.multiple_of(cols, tc), tc)] = gd_half(
+                lax.rem(me + 1 + 2 * (n // 2), nm), lax.rem(n, 2))
+
         for side in range(2):
-            for half in (1 - side, side):
-                gd_slot(side, half)[...] = gd_half(peer((plus, minus)[side]), half)
             gd_near_copy(side, 1 - side).start()
 
     def gd_add(src, ref):
@@ -899,7 +912,7 @@
             name="train_step",
         )(tokens_in, targets, wqT, wo, wu, wd)
         part, loss, late = res[0], res[1], res[5]
-        steps = 4
+        steps = 2
 
         def spec(size, start):
             rows = size // steps

time: 313 us -> 312 us (level)
  no operation moved by 1% of the time
where the time goes in v15:
time: 312 us; the launch traced here: 311 us
  Pallas kernels  310 us (99%)
    pallas_call x1, Pallas kernels, per_device(): pl.pallas_call(functools.partial(step_kernel, cfg), out_shape=out_shape,...  306 us

profile of v15, /device:TPU:96, one launch (start us, length us, event | category | flops | bytes accessed | tf_op | source)
XLA Modules:
  0.0 311.0 jit_solution(18247333053763271956)
XLA Ops:
  0.6 306.4 %train_step.1 = (f32[1536,512]{1,0:T(8,128)}, f32[8,128]{1,0:T(8,128)}, f32[512,512]{1,0:T(8,128)}, f32[512,512]{1,0:T(8,128)}, f32[1024,512]{1,0:T(8,128)}, /*i...) custom-call(bf16[4,1024,512]{2,1,0:T(8,128)(2,1)} %x_hbm.1, ...), custom_call_target="tpu_custom_call" | custom-call | tf_op jit(solution)/shard_map/train_step/pallas_call | solution.py:905
  307.0 3.8 %finish.1 = (f32[384,512]{1,0:T(8,128)}, f32[128,512]{1,0:T(8,128)}, f32[512,512]{1,0:T(8,128)}, f32[512,512]{1,0:T(8,128)}, f32[1]{0:T(128)}) custom-call(f32[1536,512]{1,0:T(8,128)} %get-tuple-element.13.sq.so.su.sd, f32[1536,512]{1,0:T(8,128)} %get-tuple-element.13.sq.so.su.sd, f32[1536,512]{1,0:T(8,128)} %get-tuple-element.13.sq.so.su.sd, ...), custom_call_target="tpu_custom_call" | custom-call | tf_op jit(solution)/shard_map/finish/pallas_call | solution.py:922

commit v16 on v15

--- a/solution.py
+++ b/solution.py
@@ -168,13 +168,14 @@
     w_local(W_D).wait()
     wdT[:, rowsl(me * fl, fl, fl)] = jnp.transpose(wd[rowsl(me * fl, fl, fl), :])
     w_own(W_D)
+
+    @pl.when(jnp.logical_not(odd))
+    def _():
+        pl.semaphore_signal(go_sem, inc=1, device_id={"stage": nxt}, device_id_type=MESH)
+
     w_local(W_Q).wait()
     w_forward(W_Q)
     w_forward(W_O)
-
-    @pl.when(jnp.logical_not(odd))
-    def _():
-        pl.semaphore_signal(go_sem, inc=1, device_id={"stage": nxt}, device_id_type=MESH)
 
     def natural_weights():
         @pl.loop(0, nm)

time: 312 us -> 315 us (level)
  Pallas kernels: 310 us -> 314 us
    pallas_call x1, Pallas kernels: 306 us -> 310 us  [per_device(): pl.pallas_call(functools.partial(step_kernel, cfg), out_shape=out_shape,...]
where the time goes in v16:
time: 315 us; the launch traced here: 314 us
  Pallas kernels  314 us (100%)
    pallas_call x1, Pallas kernels, per_device(): pl.pallas_call(functools.partial(step_kernel, cfg), out_shape=out_shape,...  310 us

profile of v16, /device:TPU:96, one launch (start us, length us, event | category | flops | bytes accessed | tf_op | source)
XLA Modules:
  0.0 314.4 jit_solution(1738370856688786301)
XLA Ops:
  0.6 309.8 %train_step.1 = (f32[1536,512]{1,0:T(8,128)}, f32[8,128]{1,0:T(8,128)}, f32[512,512]{1,0:T(8,128)}, f32[512,512]{1,0:T(8,128)}, f32[1024,512]{1,0:T(8,128)}, /*i...) custom-call(bf16[4,1024,512]{2,1,0:T(8,128)(2,1)} %x_hbm.1, ...), custom_call_target="tpu_custom_call" | custom-call | tf_op jit(solution)/shard_map/train_step/pallas_call | solution.py:906
  310.4 3.8 %finish.1 = (f32[384,512]{1,0:T(8,128)}, f32[128,512]{1,0:T(8,128)}, f32[512,512]{1,0:T(8,128)}, f32[512,512]{1,0:T(8,128)}, f32[1]{0:T(128)}) custom-call(f32[1536,512]{1,0:T(8,128)} %get-tuple-element.13.sq.so.su.sd, f32[1536,512]{1,0:T(8,128)} %get-tuple-element.13.sq.so.su.sd, f32[1536,512]{1,0:T(8,128)} %get-tuple-element.13.sq.so.su.sd, ...), custom_call_target="tpu_custom_call" | custom-call | tf_op jit(solution)/shard_map/finish/pallas_call | solution.py:923

commit v17 on v15

--- a/solution.py
+++ b/solution.py
@@ -528,7 +528,7 @@
         def _():
             b_copy(c).wait_recv()
 
-        @pl.when(jnp.logical_not(late) & (i == 0))
+        @pl.when(jnp.logical_not(late) & ((i == 0) | dy_inside))
         def _():
             for way in range(2):
                 dy_copy(c, way).start()
@@ -550,7 +550,7 @@
         mbuf[c] = dmid
         dobuf[...] = dot(wo[...], dmid).astype(BF16)
 
-        @pl.when(jnp.logical_not(late) & (i > 0))
+        @pl.when(jnp.logical_not(late | dy_inside) & (i > 0))
         def _():
             for way in range(2):
                 dy_copy(c, way).start()

time: 312 us -> 310 us (level)
  no operation moved by 1% of the time
where the time goes in v17:
time: 310 us; the launch traced here: 309 us
  Pallas kernels  309 us (100%)
    pallas_call x1, Pallas kernels, per_device(): pl.pallas_call(functools.partial(step_kernel, cfg), out_shape=out_shape,...  305 us

profile of v17, /device:TPU:96, one launch (start us, length us, event | category | flops | bytes accessed | tf_op | source)
XLA Modules:
  0.0 309.5 jit_solution(1506708952689608905)
XLA Ops:
  0.6 304.9 %train_step.1 = (f32[1536,512]{1,0:T(8,128)}, f32[8,128]{1,0:T(8,128)}, f32[512,512]{1,0:T(8,128)}, f32[512,512]{1,0:T(8,128)}, f32[1024,512]{1,0:T(8,128)}, /*i...) custom-call(bf16[4,1024,512]{2,1,0:T(8,128)(2,1)} %x_hbm.1, ...), custom_call_target="tpu_custom_call" | custom-call | tf_op jit(solution)/shard_map/train_step/pallas_call | solution.py:905
  305.5 3.8 %finish.1 = (f32[384,512]{1,0:T(8,128)}, f32[128,512]{1,0:T(8,128)}, f32[512,512]{1,0:T(8,128)}, f32[512,512]{1,0:T(8,128)}, f32[1]{0:T(128)}) custom-call(f32[1536,512]{1,0:T(8,128)} %get-tuple-element.13.sq.so.su.sd, f32[1536,512]{1,0:T(8,128)} %get-tuple-element.13.sq.so.su.sd, f32[1536,512]{1,0:T(8,128)} %get-tuple-element.13.sq.so.su.sd, ...), custom_call_target="tpu_custom_call" | custom-call | tf_op jit(solution)/shard_map/finish/pallas_call | solution.py:922
